TPU v7x, 256 devices: a whole 4x4x8 slice. The times are simulated.
256 devices in a mesh: tm: 16 (over x, z_lo, core), space: 16 (over z_hi, y).
Axes of the slice: x: 4, y: 4, z: 8 (z_hi: 4, z_lo: 2; z = z_hi * 2 + z_lo), core: 2. Of those that a mesh axis runs over, the one named last changes fastest.
Arguments:
- state_rhs: float32 [32, 32, 128, 128], P('tm', 'space'), may hold values from -5 to 9
- adjoint_rhs: float32 [32, 32, 128, 128], P('tm', 'space'), may hold values from -5 to 9
- reaction: float32 [32, 128, 128], P('space'), may hold values from 0.01 to 1
Outputs:
- state_out: float32 [32, 32, 128, 128], P('tm', 'space')
- adjoint_out: float32 [32, 32, 128, 128], P('tm', 'space')
All inputs are finite; a program needn't handle non-finite values.
Results may differ from a plain program's by a relative error of at most 0.00021.
Values sent between devices are 32-bit elements; how exact they have to be, the bound alone decides.
No kernel may reach another device: no remote copies, remote signals or barrier semaphores. Data moves between devices by JAX's collectives and lax.ppermute only.
A program may use at most 64 MiB of HBM per device.

v0:
```python
import math

import jax
import jax.numpy as jnp
from jax import lax
from jax.sharding import Mesh
from jax.sharding import PartitionSpec as P

STEPS = 32
SWEEPS = 12
TM = ("tm_0", "tm_1", "tm_2")


ALPHA = 0.1
MU = 1.0
BETA = 1.0


def in_one_piece(arrays, axis, split_dim, concat_dim, along):
    ends, at = ([], 0)
    for a in arrays[:-1]:
        at += a.shape[along]
        ends.append(at)
    both = jnp.concatenate(arrays, axis=along)
    return tuple(
        jnp.split(
            lax.all_to_all(both, axis, split_axis=split_dim, concat_axis=concat_dim, tiled=True),
            ends,
            axis=along,
        )
    )


def split_up(x, dim, count):
    lengths = x.shape
    pieces = x.reshape(*lengths[:dim], count, lengths[dim] // count, *lengths[dim + 1 :])
    return jnp.moveaxis(pieces, dim, 0)


def joined_along(pieces, dim):
    lengths = list(pieces.shape[1:])
    lengths[dim] *= pieces.shape[0]
    return jnp.moveaxis(pieces, 0, dim).reshape(lengths)


def moved_by_axis(pieces, axes, turns):
    lengths = [lax.axis_size(a) for a in axes]
    pieces = pieces.reshape(*lengths, *pieces.shape[1:])
    for k in turns:
        pieces = lax.all_to_all(pieces, axes[k], split_axis=k, concat_axis=k, tiled=True)
    return pieces.reshape(-1, *pieces.shape[len(axes) :])


def two_step_exchange(x, groups, turns, split_dim, concat_dim):
    count = lax.axis_size(groups[0]) * lax.axis_size(groups[1])
    pieces = split_up(x, split_dim, count)
    return joined_along(moved_by_axis(pieces, groups, turns), concat_dim)


def padded_2(cells, sides, width):
    for axis, dim in sides:
        count = lax.axis_size(axis)
        ends = count - 1
        head = lax.slice_in_dim(cells, 0, width, axis=dim)
        tail = lax.slice_in_dim(cells, cells.shape[dim] - width, cells.shape[dim], axis=dim)
        cells = jnp.concatenate(
            [
                lax.ppermute(tail, axis, [(i, (i + 1) % count) for i in range(ends)]),
                cells,
                lax.ppermute(head, axis, [((i + 1) % count, i) for i in range(ends)]),
            ],
            axis=dim,
        )
    return cells


def coefficients(reaction, freqs):
    turn = 2.0 * math.pi * freqs.astype(jnp.float32) / STEPS
    rate = math.exp(math.log(ALPHA) / STEPS)
    lam_re = 1.0 - rate * jnp.cos(turn)
    lam_im = rate * jnp.sin(turn)
    shaped = (-1,) + (1,) * reaction.ndim
    d_re = lam_re.reshape(shaped) + MU * (6.0 + reaction)
    d_im = jnp.broadcast_to(lam_im.reshape(shaped), d_re.shape)
    den_re = d_re * d_re - d_im * d_im + BETA * BETA
    den_im = 2.0 * d_re * d_im
    magnitude = den_re * den_re + den_im * den_im
    inv_re = den_re / magnitude
    inv_im = -den_im / magnitude
    return (
        d_re * inv_re - d_im * inv_im,
        d_re * inv_im + d_im * inv_re,
        BETA * inv_re,
        BETA * inv_im,
    )


def block_solve(coefficient, source):
    q_re, q_im, r_re, r_im = coefficient
    y_real = source[..., 0, :, :, :]
    y_imag = source[..., 1, :, :, :]
    p_real = source[..., 2, :, :, :]
    p_imag = source[..., 3, :, :, :]
    new_yre = q_re * y_real - q_im * y_imag + (r_re * p_real - r_im * p_imag)
    new_yim = q_re * y_imag + q_im * y_real + (r_re * p_imag + r_im * p_real)
    new_pre = q_re * p_real - q_im * p_imag - (r_re * y_real - r_im * y_imag)
    new_pim = q_re * p_imag + q_im * p_real - (r_re * y_imag + r_im * y_real)
    return jnp.stack((new_yre, new_yim, new_pre, new_pim), axis=-4)


def neighbour_sum(zpadded):
    inner = zpadded[:, :, 1:-1]
    padded = jnp.pad(inner, ((0, 0), (0, 0), (0, 0), (1, 1), (1, 1)))
    total = zpadded[:, :, 2:] + zpadded[:, :, :-2]
    total = total + padded[:, :, :, 2:, 1:-1] + padded[:, :, :, :-2, 1:-1]
    return total + padded[:, :, :, 1:-1, 2:] + padded[:, :, :, 1:-1, :-2]


def effective(times, reverse):
    if reverse:
        return STEPS - 1 - times
    return times


def forward_table(freqs, times, reverse):
    moment = effective(times, reverse)
    phase = freqs[:, None] * moment[None, :] % STEPS
    angle = 2.0 * math.pi / STEPS * phase.astype(jnp.float32)
    growth = jnp.exp(math.log(ALPHA) * moment.astype(jnp.float32) / STEPS)[None, :]
    table = jnp.stack((jnp.cos(angle) * growth, -jnp.sin(angle) * growth), axis=1)
    return table.reshape(-1, times.shape[0])


def inverse_table(freqs, times, reverse):
    moment = effective(times, reverse)
    phase = moment[:, None] * freqs[None, :] % STEPS
    angle = 2.0 * math.pi / STEPS * phase.astype(jnp.float32)
    shrink = jnp.exp(-math.log(ALPHA) * moment.astype(jnp.float32) / STEPS)[:, None] / STEPS
    table = jnp.stack((jnp.cos(angle) * shrink, -jnp.sin(angle) * shrink), axis=2)
    return table.reshape(times.shape[0], -1)


def forward_pair(state_part, adjoint_part, freqs, times):
    rows = state_part.shape[0]
    state_hat = jnp.dot(
        forward_table(freqs, times, False),
        state_part.reshape(rows, -1),
        precision=lax.Precision.HIGHEST,
    )
    adjoint_hat = jnp.dot(
        forward_table(freqs, times, True),
        adjoint_part.reshape(rows, -1),
        precision=lax.Precision.HIGHEST,
    )
    return (state_hat, adjoint_hat)


def backward_pair(solved, freqs, times):
    count = solved.shape[0]
    slab = solved.shape[2:]
    flat_state = solved[:, 0:2].reshape(2 * count, -1)
    flat_adjoint = solved[:, 2:4].reshape(2 * count, -1)
    state_time = jnp.dot(
        inverse_table(freqs, times, False), flat_state, precision=lax.Precision.HIGHEST
    )
    adjoint_time = jnp.dot(
        inverse_table(freqs, times, True), flat_adjoint, precision=lax.Precision.HIGHEST
    )
    shaped = (times.shape[0],) + slab
    return (state_time.reshape(shaped), adjoint_time.reshape(shaped))


def body(state_rhs, adjoint_rhs, reaction):
    groups = lax.axis_size(TM)
    freq_count = STEPS // groups
    freqs = lax.axis_index(TM) * freq_count + jnp.arange(freq_count, dtype=jnp.int32)
    state_all, adjoint_all = in_one_piece((state_rhs, adjoint_rhs), TM, 2, 0, 1)
    every = jnp.arange(STEPS, dtype=jnp.int32)
    state_hat, adjoint_hat = forward_pair(state_all, adjoint_all, every, every)
    narrow = state_all.shape[1:]
    spread = jnp.concatenate(
        (state_hat.reshape((STEPS, 2) + narrow), adjoint_hat.reshape((STEPS, 2) + narrow)), axis=1
    )
    sources = two_step_exchange(spread, (("tm_0", "tm_1"), "tm_2"), (1, 0), 0, 3)
    coefficient = coefficients(reaction, freqs)
    field = block_solve(coefficient, sources)

    def sweep(sweep_index, current):
        zpadded = padded_2(current, (("space", 2),), 1)
        return block_solve(coefficient, sources + MU * neighbour_sum(zpadded))

    solved = lax.fori_loop(0, SWEEPS - 1, sweep, field)
    by_time = two_step_exchange(solved, (("tm_0", "tm_1"), "tm_2"), (1, 0), 3, 0)
    every = jnp.arange(STEPS, dtype=jnp.int32)
    state_time, adjoint_time = backward_pair(by_time, every, every)
    state_out, adjoint_out = in_one_piece((state_time, adjoint_time), TM, 0, 2, 1)
    return (state_out, adjoint_out)


def solution(mesh):
    split = Mesh(
        mesh.devices.reshape(4, 2, 2, mesh.shape["space"]), ("tm_0", "tm_1", "tm_2", "space")
    )
    placed = (P(TM, "space", None, None), P(TM, "space", None, None), P("space", None, None))
    return jax.shard_map(
        body,
        mesh=split,
        in_specs=placed,
        out_specs=(P(TM, "space", None, None), P(TM, "space", None, None)),
        check_vma=False,
    )
```

profile of v0, /device:TPU:88, one launch (start us, length us, event | category | flops | bytes accessed | tf_op | source)
XLA Modules:
  0.0 451.5 jit_solution(1778864663796750010)
XLA Ops:
  4.0 5.8 %all-to-all-start = ((f32[2,4,128,128]{3,1,0,2:T(4,128)}), f32[2,4,128,128]{3,1,0,2:T(4,128)S(1)}, u32[]{:S(2)}, u32[]{:S(2)}) async-start(f32[2,4,128,128]{3,1,0,2:T(4,128)} %pad_maximum_fusion.5), calls=%async_computation | async-start | bytes 1048576 | tf_op jit(solution)/shard_map/all_to_all | solution.py:27
  10.0 10.6 %all-to-all-done = f32[2,4,128,128]{3,1,0,2:T(4,128)S(1)} async-done(((f32[2,4,128,128]{3,1,0,2:T(4,128)}), f32[2,4,128,128]{3,1,0,2:T(4,128)S(1)}, u32[]{:S(2)}, u32[]{:S(2)}) %all-to-all-start) | async-done | bytes 524320 | tf_op jit(solution)/shard_map/all_to_all | solution.py:27
  23.0 4.6 %all_to_all.56 = f32[8,2,2,4,2,8,128]{6,2,0,5,4,3,1:T(2,128)S(1)} all-to-all(f32[8,2,2,4,2,8,128]{6,2,0,5,4,3,1:T(2,128)S(1)} %copy.84), channel_id=1, replica_groups=mesh['tm_0'=4,'tm_1'=2,'tm_2'=2,'space'=16] {'tm_2'}, dimensions={1} | all-to-all | bytes 2097152 | tf_op jit(solution)/shard_map/all_to_all | solution.py:50
  33.0 16.1 %all-to-all-done.2 = f32[8,2,2,4,2,8,128]{6,2,1,5,4,3,0:T(2,128)S(1)} async-done(((f32[8,2,2,4,2,8,128]{6,2,1,5,4,3,0:T(2,128)}), f32[8,2,2,4,2,8,128]{6,2,1,5,4,3,0:T(2,128)S(1)}, u32[]{:S(2)}, u32[]{:S(2)}) %all-to-all-start.2) | async-done | bytes 1048608 | tf_op jit(solution)/shard_map/all_to_all | solution.py:50
  50.0 339.6 %while.14 = (s32[]{:T(128)}, f32[2,4,2,128,128]{4,3,2,1,0:T(8,128)S(1)}, f32[2,4,2,128,128]{4,3,2,1,0:T(8,128)S(1)}, f32[2]{0:T(128)S(1)}, f32[2,128,128]{2,1,0:...) while((s32[]{:T(128)}, ...), condition=%wide.region_1.2_spmd.clone.clone, body=%wide.region_0.1_spmd.clone.clone.sunk | while | flops 6946818 | bytes 15991021 | solution.py:192
  50.1 5.2 %collective-permute-start = (f32[2,4,1,128,128]{4,3,2,1,0:T(8,128)S(1)}, f32[2,4,1,128,128]{4,3,2,1,0:T(8,128)}, u32[]{:S(2)}, u32[]{:S(2)}) collective-permute-start(f32[2,4,1,128,128]{4,3,2,1,0:T(8,128)S(1)} %get-tuple-element.276), channel_id=1, source_target_pairs={{0,1},{1,2},{2,3},{3,4},{4,5},{5,6},{6,7},{7,8},{8,9},{9,10},{10,1... | collective-permute-start | bytes 1572872 | tf_op jit(solution)/shard_map/while/body/eval_jaxpr/ppermute | solution.py:68
  57.2 19.2 %collective-permute-done = f32[2,4,1,128,128]{4,3,2,1,0:T(8,128)} collective-permute-done((f32[2,4,1,128,128]{4,3,2,1,0:T(8,128)S(1)}, f32[2,4,1,128,128]{4,3,2,1,0:T(8,128)}, u32[]{:S(2)}, u32[]{:S(2)}) %collective-permute-start) | collective-permute-done | bytes 524320 | tf_op jit(solution)/shard_map/while/body/eval_jaxpr/ppermute | solution.py:68
  76.4 9.0 %collective-permute-done.1 = f32[2,4,1,128,128]{4,3,2,1,0:T(8,128)} collective-permute-done((f32[2,4,1,128,128]{4,3,2,1,0:T(8,128)S(1)}, f32[2,4,1,128,128]{4,3,2,1,0:T(8,128)}, u32[]{:S(2)}, u32[]{:S(2)}) %collective-permute-start.1) | collective-permute-done | bytes 524320 | tf_op jit(solution)/shard_map/while/body/eval_jaxpr/ppermute | solution.py:70
  94.0 15.7 %collective-permute-done = f32[2,4,1,128,128]{4,3,2,1,0:T(8,128)} collective-permute-done((f32[2,4,1,128,128]{4,3,2,1,0:T(8,128)S(1)}, f32[2,4,1,128,128]{4,3,2,1,0:T(8,128)}, u32[]{:S(2)}, u32[]{:S(2)}) %collective-permute-start) | collective-permute-done | bytes 524320 | tf_op jit(solution)/shard_map/while/body/eval_jaxpr/ppermute | solution.py:68
  109.6 8.2 %collective-permute-done.1 = f32[2,4,1,128,128]{4,3,2,1,0:T(8,128)} collective-permute-done((f32[2,4,1,128,128]{4,3,2,1,0:T(8,128)S(1)}, f32[2,4,1,128,128]{4,3,2,1,0:T(8,128)}, u32[]{:S(2)}, u32[]{:S(2)}) %collective-permute-start.1) | collective-permute-done | bytes 524320 | tf_op jit(solution)/shard_map/while/body/eval_jaxpr/ppermute | solution.py:70
  126.4 14.5 %collective-permute-done = f32[2,4,1,128,128]{4,3,2,1,0:T(8,128)} collective-permute-done((f32[2,4,1,128,128]{4,3,2,1,0:T(8,128)S(1)}, f32[2,4,1,128,128]{4,3,2,1,0:T(8,128)}, u32[]{:S(2)}, u32[]{:S(2)}) %collective-permute-start) | collective-permute-done | bytes 524320 | tf_op jit(solution)/shard_map/while/body/eval_jaxpr/ppermute | solution.py:68
  140.9 4.8 %collective-permute-done.1 = f32[2,4,1,128,128]{4,3,2,1,0:T(8,128)} collective-permute-done((f32[2,4,1,128,128]{4,3,2,1,0:T(8,128)S(1)}, f32[2,4,1,128,128]{4,3,2,1,0:T(8,128)}, u32[]{:S(2)}, u32[]{:S(2)}) %collective-permute-start.1) | collective-permute-done | bytes 524320 | tf_op jit(solution)/shard_map/while/body/eval_jaxpr/ppermute | solution.py:70
  154.3 9.0 %collective-permute-done = f32[2,4,1,128,128]{4,3,2,1,0:T(8,128)} collective-permute-done((f32[2,4,1,128,128]{4,3,2,1,0:T(8,128)S(1)}, f32[2,4,1,128,128]{4,3,2,1,0:T(8,128)}, u32[]{:S(2)}, u32[]{:S(2)}) %collective-permute-start) | collective-permute-done | bytes 524320 | tf_op jit(solution)/shard_map/while/body/eval_jaxpr/ppermute | solution.py:68
  163.4 8.3 %collective-permute-done.1 = f32[2,4,1,128,128]{4,3,2,1,0:T(8,128)} collective-permute-done((f32[2,4,1,128,128]{4,3,2,1,0:T(8,128)S(1)}, f32[2,4,1,128,128]{4,3,2,1,0:T(8,128)}, u32[]{:S(2)}, u32[]{:S(2)}) %collective-permute-start.1) | collective-permute-done | bytes 524320 | tf_op jit(solution)/shard_map/while/body/eval_jaxpr/ppermute | solution.py:70
  180.3 8.5 %collective-permute-done = f32[2,4,1,128,128]{4,3,2,1,0:T(8,128)} collective-permute-done((f32[2,4,1,128,128]{4,3,2,1,0:T(8,128)S(1)}, f32[2,4,1,128,128]{4,3,2,1,0:T(8,128)}, u32[]{:S(2)}, u32[]{:S(2)}) %collective-permute-start) | collective-permute-done | bytes 524320 | tf_op jit(solution)/shard_map/while/body/eval_jaxpr/ppermute | solution.py:68
  188.7 11.2 %collective-permute-done.1 = f32[2,4,1,128,128]{4,3,2,1,0:T(8,128)} collective-permute-done((f32[2,4,1,128,128]{4,3,2,1,0:T(8,128)S(1)}, f32[2,4,1,128,128]{4,3,2,1,0:T(8,128)}, u32[]{:S(2)}, u32[]{:S(2)}) %collective-permute-start.1) | collective-permute-done | bytes 524320 | tf_op jit(solution)/shard_map/while/body/eval_jaxpr/ppermute | solution.py:70
  208.5 9.9 %collective-permute-done = f32[2,4,1,128,128]{4,3,2,1,0:T(8,128)} collective-permute-done((f32[2,4,1,128,128]{4,3,2,1,0:T(8,128)S(1)}, f32[2,4,1,128,128]{4,3,2,1,0:T(8,128)}, u32[]{:S(2)}, u32[]{:S(2)}) %collective-permute-start) | collective-permute-done | bytes 524320 | tf_op jit(solution)/shard_map/while/body/eval_jaxpr/ppermute | solution.py:68
  218.4 11.1 %collective-permute-done.1 = f32[2,4,1,128,128]{4,3,2,1,0:T(8,128)} collective-permute-done((f32[2,4,1,128,128]{4,3,2,1,0:T(8,128)S(1)}, f32[2,4,1,128,128]{4,3,2,1,0:T(8,128)}, u32[]{:S(2)}, u32[]{:S(2)}) %collective-permute-start.1) | collective-permute-done | bytes 524320 | tf_op jit(solution)/shard_map/while/body/eval_jaxpr/ppermute | solution.py:70
  238.0 9.9 %collective-permute-done = f32[2,4,1,128,128]{4,3,2,1,0:T(8,128)} collective-permute-done((f32[2,4,1,128,128]{4,3,2,1,0:T(8,128)S(1)}, f32[2,4,1,128,128]{4,3,2,1,0:T(8,128)}, u32[]{:S(2)}, u32[]{:S(2)}) %collective-permute-start) | collective-permute-done | bytes 524320 | tf_op jit(solution)/shard_map/while/body/eval_jaxpr/ppermute | solution.py:68
  248.0 10.4 %collective-permute-done.1 = f32[2,4,1,128,128]{4,3,2,1,0:T(8,128)} collective-permute-done((f32[2,4,1,128,128]{4,3,2,1,0:T(8,128)S(1)}, f32[2,4,1,128,128]{4,3,2,1,0:T(8,128)}, u32[]{:S(2)}, u32[]{:S(2)}) %collective-permute-start.1) | collective-permute-done | bytes 524320 | tf_op jit(solution)/shard_map/while/body/eval_jaxpr/ppermute | solution.py:70
  261.0 7.4 %collective-permute-start = (f32[2,4,1,128,128]{4,3,2,1,0:T(8,128)S(1)}, f32[2,4,1,128,128]{4,3,2,1,0:T(8,128)}, u32[]{:S(2)}, u32[]{:S(2)}) collective-permute-start(f32[2,4,1,128,128]{4,3,2,1,0:T(8,128)S(1)} %get-tuple-element.276), channel_id=1, source_target_pairs={{0,1},{1,2},{2,3},{3,4},{4,5},{5,6},{6,7},{7,8},{8,9},{9,10},{10,1... | collective-permute-start | bytes 1572872 | tf_op jit(solution)/shard_map/while/body/eval_jaxpr/ppermute | solution.py:68
  270.4 16.0 %collective-permute-done = f32[2,4,1,128,128]{4,3,2,1,0:T(8,128)} collective-permute-done((f32[2,4,1,128,128]{4,3,2,1,0:T(8,128)S(1)}, f32[2,4,1,128,128]{4,3,2,1,0:T(8,128)}, u32[]{:S(2)}, u32[]{:S(2)}) %collective-permute-start) | collective-permute-done | bytes 524320 | tf_op jit(solution)/shard_map/while/body/eval_jaxpr/ppermute | solution.py:68
  286.4 4.7 %collective-permute-done.1 = f32[2,4,1,128,128]{4,3,2,1,0:T(8,128)} collective-permute-done((f32[2,4,1,128,128]{4,3,2,1,0:T(8,128)S(1)}, f32[2,4,1,128,128]{4,3,2,1,0:T(8,128)}, u32[]{:S(2)}, u32[]{:S(2)}) %collective-permute-start.1) | collective-permute-done | bytes 524320 | tf_op jit(solution)/shard_map/while/body/eval_jaxpr/ppermute | solution.py:70
  299.8 16.6 %collective-permute-done = f32[2,4,1,128,128]{4,3,2,1,0:T(8,128)} collective-permute-done((f32[2,4,1,128,128]{4,3,2,1,0:T(8,128)S(1)}, f32[2,4,1,128,128]{4,3,2,1,0:T(8,128)}, u32[]{:S(2)}, u32[]{:S(2)}) %collective-permute-start) | collective-permute-done | bytes 524320 | tf_op jit(solution)/shard_map/while/body/eval_jaxpr/ppermute | solution.py:68
  316.4 8.1 %collective-permute-done.1 = f32[2,4,1,128,128]{4,3,2,1,0:T(8,128)} collective-permute-done((f32[2,4,1,128,128]{4,3,2,1,0:T(8,128)S(1)}, f32[2,4,1,128,128]{4,3,2,1,0:T(8,128)}, u32[]{:S(2)}, u32[]{:S(2)}) %collective-permute-start.1) | collective-permute-done | bytes 524320 | tf_op jit(solution)/shard_map/while/body/eval_jaxpr/ppermute | solution.py:70
  333.1 18.9 %collective-permute-done = f32[2,4,1,128,128]{4,3,2,1,0:T(8,128)} collective-permute-done((f32[2,4,1,128,128]{4,3,2,1,0:T(8,128)S(1)}, f32[2,4,1,128,128]{4,3,2,1,0:T(8,128)}, u32[]{:S(2)}, u32[]{:S(2)}) %collective-permute-start) | collective-permute-done | bytes 524320 | tf_op jit(solution)/shard_map/while/body/eval_jaxpr/ppermute | solution.py:68
  358.5 4.9 %collective-permute-start = (f32[2,4,1,128,128]{4,3,2,1,0:T(8,128)S(1)}, f32[2,4,1,128,128]{4,3,2,1,0:T(8,128)}, u32[]{:S(2)}, u32[]{:S(2)}) collective-permute-start(f32[2,4,1,128,128]{4,3,2,1,0:T(8,128)S(1)} %get-tuple-element.276), channel_id=1, source_target_pairs={{0,1},{1,2},{2,3},{3,4},{4,5},{5,6},{6,7},{7,8},{8,9},{9,10},{10,1... | collective-permute-start | bytes 1572872 | tf_op jit(solution)/shard_map/while/body/eval_jaxpr/ppermute | solution.py:68
  365.4 20.0 %collective-permute-done = f32[2,4,1,128,128]{4,3,2,1,0:T(8,128)} collective-permute-done((f32[2,4,1,128,128]{4,3,2,1,0:T(8,128)S(1)}, f32[2,4,1,128,128]{4,3,2,1,0:T(8,128)}, u32[]{:S(2)}, u32[]{:S(2)}) %collective-permute-start) | collective-permute-done | bytes 524320 | tf_op jit(solution)/shard_map/while/body/eval_jaxpr/ppermute | solution.py:68
  389.7 4.6 %all_to_all.57 = f32[8,2,2,4,2,8,128]{6,5,4,3,2,0,1:T(8,128)S(1)} all-to-all(f32[8,2,2,4,2,8,128]{6,5,4,3,2,0,1:T(8,128)S(1)} %copy.89), channel_id=1, replica_groups=mesh['tm_0'=4,'tm_1'=2,'tm_2'=2,'space'=16] {'tm_2'}, dimensions={1} | all-to-all | bytes 2097152 | tf_op jit(solution)/shard_map/all_to_all | solution.py:50
  395.4 23.6 %all-to-all-start.4 = ((f32[8,2,2,4,2,8,128]{6,5,4,3,2,1,0:T(8,128)}), f32[8,2,2,4,2,8,128]{6,5,4,3,2,1,0:T(8,128)S(1)}, u32[]{:S(2)}, u32[]{:S(2)}) async-start(f32[8,2,2,4,2,8,128]{6,5,4,3,2,1,0:T(8,128)} %copy.90), calls=%async_computation.4 | async-start | bytes 2097152 | tf_op jit(solution)/shard_map/all_to_all | solution.py:50
  419.4 15.6 %all-to-all-done.4 = f32[8,2,2,4,2,8,128]{6,5,4,3,2,1,0:T(8,128)S(1)} async-done(((f32[8,2,2,4,2,8,128]{6,5,4,3,2,1,0:T(8,128)}), f32[8,2,2,4,2,8,128]{6,5,4,3,2,1,0:T(8,128)S(1)}, u32[]{:S(2)}, u32[]{:S(2)}) %all-to-all-start.4) | async-done | bytes 1048608 | tf_op jit(solution)/shard_map/all_to_all | solution.py:50
  437.0 13.7 %all_to_all.58 = f32[32,4,8,128]{3,2,1,0:T(8,128)S(1)} all-to-all(f32[32,4,8,128]{3,2,1,0:T(8,128)S(1)} %copy.96), channel_id=1, replica_groups=mesh['tm_0'=4,'tm_1'=2,'tm_2'=2,'space'=16] {'tm_0','tm_1','tm_2'}, dimensions={0} | all-to-all | bytes 1048576 | tf_op jit(solution)/shard_map/all_to_all | solution.py:27
  (127 shorter events, 104.0 us)
Async XLA Ops:
  4.0 16.6 %all-to-all-start = ((f32[2,4,128,128]{3,1,0,2:T(4,128)}), f32[2,4,128,128]{3,1,0,2:T(4,128)S(1)}, u32[]{:S(2)}, u32[]{:S(2)}) async-start(f32[2,4,128,128]{3,1,0,2:T(4,128)} %pad_maximum_fusion.5), calls=%async_computation | async-start | bytes 1048576 | tf_op jit(solution)/shard_map/all_to_all | solution.py:27
  29.1 3.8 copy-start
  29.1 20.0 %all-to-all-start.2 = ((f32[8,2,2,4,2,8,128]{6,2,1,5,4,3,0:T(2,128)}), f32[8,2,2,4,2,8,128]{6,2,1,5,4,3,0:T(2,128)S(1)}, u32[]{:S(2)}, u32[]{:S(2)}) async-start(f32[8,2,2,4,2,8,128]{6,2,1,5,4,3,0:T(2,128)} %copy.85), calls=%async_computation.2 | async-start | bytes 2097152 | tf_op jit(solution)/shard_map/all_to_all | solution.py:50
  50.1 26.3 %collective-permute-start = (f32[2,4,1,128,128]{4,3,2,1,0:T(8,128)S(1)}, f32[2,4,1,128,128]{4,3,2,1,0:T(8,128)}, u32[]{:S(2)}, u32[]{:S(2)}) collective-permute-start(f32[2,4,1,128,128]{4,3,2,1,0:T(8,128)S(1)} %get-tuple-element.276), channel_id=1, source_target_pairs={{0,1},{1,2},{2,3},{3,4},{4,5},{5,6},{6,7},{7,8},{8,9},{9,10},{10,1... | collective-permute-start | bytes 1572872 | tf_op jit(solution)/shard_map/while/body/eval_jaxpr/ppermute | solution.py:68
  55.3 30.2 %collective-permute-start.1 = (f32[2,4,1,128,128]{4,3,2,1,0:T(8,128)S(1)}, f32[2,4,1,128,128]{4,3,2,1,0:T(8,128)}, u32[]{:S(2)}, u32[]{:S(2)}) collective-permute-start(f32[2,4,1,128,128]{4,3,2,1,0:T(8,128)S(1)} %get-tuple-element.277), channel_id=1, source_target_pairs={{1,0},{2,1},{3,2},{4,3},{5,4},{6,5},{7,6},{8,7},{9,8},{10,9},{11,1... | collective-permute-start | bytes 1572872 | tf_op jit(solution)/shard_map/while/body/eval_jaxpr/ppermute | solution.py:70
  88.1 21.5 %collective-permute-start = (f32[2,4,1,128,128]{4,3,2,1,0:T(8,128)S(1)}, f32[2,4,1,128,128]{4,3,2,1,0:T(8,128)}, u32[]{:S(2)}, u32[]{:S(2)}) collective-permute-start(f32[2,4,1,128,128]{4,3,2,1,0:T(8,128)S(1)} %get-tuple-element.276), channel_id=1, source_target_pairs={{0,1},{1,2},{2,3},{3,4},{4,5},{5,6},{6,7},{7,8},{8,9},{9,10},{10,1... | collective-permute-start | bytes 1572872 | tf_op jit(solution)/shard_map/while/body/eval_jaxpr/ppermute | solution.py:68
  90.1 27.7 %collective-permute-start.1 = (f32[2,4,1,128,128]{4,3,2,1,0:T(8,128)S(1)}, f32[2,4,1,128,128]{4,3,2,1,0:T(8,128)}, u32[]{:S(2)}, u32[]{:S(2)}) collective-permute-start(f32[2,4,1,128,128]{4,3,2,1,0:T(8,128)S(1)} %get-tuple-element.277), channel_id=1, source_target_pairs={{1,0},{2,1},{3,2},{4,3},{5,4},{6,5},{7,6},{8,7},{9,8},{10,9},{11,1... | collective-permute-start | bytes 1572872 | tf_op jit(solution)/shard_map/while/body/eval_jaxpr/ppermute | solution.py:70
  120.5 20.4 %collective-permute-start = (f32[2,4,1,128,128]{4,3,2,1,0:T(8,128)S(1)}, f32[2,4,1,128,128]{4,3,2,1,0:T(8,128)}, u32[]{:S(2)}, u32[]{:S(2)}) collective-permute-start(f32[2,4,1,128,128]{4,3,2,1,0:T(8,128)S(1)} %get-tuple-element.276), channel_id=1, source_target_pairs={{0,1},{1,2},{2,3},{3,4},{4,5},{5,6},{6,7},{7,8},{8,9},{9,10},{10,1... | collective-permute-start | bytes 1572872 | tf_op jit(solution)/shard_map/while/body/eval_jaxpr/ppermute | solution.py:68
  122.4 23.3 %collective-permute-start.1 = (f32[2,4,1,128,128]{4,3,2,1,0:T(8,128)S(1)}, f32[2,4,1,128,128]{4,3,2,1,0:T(8,128)}, u32[]{:S(2)}, u32[]{:S(2)}) collective-permute-start(f32[2,4,1,128,128]{4,3,2,1,0:T(8,128)S(1)} %get-tuple-element.277), channel_id=1, source_target_pairs={{1,0},{2,1},{3,2},{4,3},{5,4},{6,5},{7,6},{8,7},{9,8},{10,9},{11,1... | collective-permute-start | bytes 1572872 | tf_op jit(solution)/shard_map/while/body/eval_jaxpr/ppermute | solution.py:70
  148.4 15.0 %collective-permute-start = (f32[2,4,1,128,128]{4,3,2,1,0:T(8,128)S(1)}, f32[2,4,1,128,128]{4,3,2,1,0:T(8,128)}, u32[]{:S(2)}, u32[]{:S(2)}) collective-permute-start(f32[2,4,1,128,128]{4,3,2,1,0:T(8,128)S(1)} %get-tuple-element.276), channel_id=1, source_target_pairs={{0,1},{1,2},{2,3},{3,4},{4,5},{5,6},{6,7},{7,8},{8,9},{9,10},{10,1... | collective-permute-start | bytes 1572872 | tf_op jit(solution)/shard_map/while/body/eval_jaxpr/ppermute | solution.py:68
  152.4 19.3 %collective-permute-start.1 = (f32[2,4,1,128,128]{4,3,2,1,0:T(8,128)S(1)}, f32[2,4,1,128,128]{4,3,2,1,0:T(8,128)}, u32[]{:S(2)}, u32[]{:S(2)}) collective-permute-start(f32[2,4,1,128,128]{4,3,2,1,0:T(8,128)S(1)} %get-tuple-element.277), channel_id=1, source_target_pairs={{1,0},{2,1},{3,2},{4,3},{5,4},{6,5},{7,6},{8,7},{9,8},{10,9},{11,1... | collective-permute-start | bytes 1572872 | tf_op jit(solution)/shard_map/while/body/eval_jaxpr/ppermute | solution.py:70
  174.4 14.3 %collective-permute-start = (f32[2,4,1,128,128]{4,3,2,1,0:T(8,128)S(1)}, f32[2,4,1,128,128]{4,3,2,1,0:T(8,128)}, u32[]{:S(2)}, u32[]{:S(2)}) collective-permute-start(f32[2,4,1,128,128]{4,3,2,1,0:T(8,128)S(1)} %get-tuple-element.276), channel_id=1, source_target_pairs={{0,1},{1,2},{2,3},{3,4},{4,5},{5,6},{6,7},{7,8},{8,9},{9,10},{10,1... | collective-permute-start | bytes 1572872 | tf_op jit(solution)/shard_map/while/body/eval_jaxpr/ppermute | solution.py:68
  176.3 23.5 %collective-permute-start.1 = (f32[2,4,1,128,128]{4,3,2,1,0:T(8,128)S(1)}, f32[2,4,1,128,128]{4,3,2,1,0:T(8,128)}, u32[]{:S(2)}, u32[]{:S(2)}) collective-permute-start(f32[2,4,1,128,128]{4,3,2,1,0:T(8,128)S(1)} %get-tuple-element.277), channel_id=1, source_target_pairs={{1,0},{2,1},{3,2},{4,3},{5,4},{6,5},{7,6},{8,7},{9,8},{10,9},{11,1... | collective-permute-start | bytes 1572872 | tf_op jit(solution)/shard_map/while/body/eval_jaxpr/ppermute | solution.py:70
  202.6 15.8 %collective-permute-start = (f32[2,4,1,128,128]{4,3,2,1,0:T(8,128)S(1)}, f32[2,4,1,128,128]{4,3,2,1,0:T(8,128)}, u32[]{:S(2)}, u32[]{:S(2)}) collective-permute-start(f32[2,4,1,128,128]{4,3,2,1,0:T(8,128)S(1)} %get-tuple-element.276), channel_id=1, source_target_pairs={{0,1},{1,2},{2,3},{3,4},{4,5},{5,6},{6,7},{7,8},{8,9},{9,10},{10,1... | collective-permute-start | bytes 1572872 | tf_op jit(solution)/shard_map/while/body/eval_jaxpr/ppermute | solution.py:68
  204.5 24.9 %collective-permute-start.1 = (f32[2,4,1,128,128]{4,3,2,1,0:T(8,128)S(1)}, f32[2,4,1,128,128]{4,3,2,1,0:T(8,128)}, u32[]{:S(2)}, u32[]{:S(2)}) collective-permute-start(f32[2,4,1,128,128]{4,3,2,1,0:T(8,128)S(1)} %get-tuple-element.277), channel_id=1, source_target_pairs={{1,0},{2,1},{3,2},{4,3},{5,4},{6,5},{7,6},{8,7},{9,8},{10,9},{11,1... | collective-permute-start | bytes 1572872 | tf_op jit(solution)/shard_map/while/body/eval_jaxpr/ppermute | solution.py:70
  232.2 15.8 %collective-permute-start = (f32[2,4,1,128,128]{4,3,2,1,0:T(8,128)S(1)}, f32[2,4,1,128,128]{4,3,2,1,0:T(8,128)}, u32[]{:S(2)}, u32[]{:S(2)}) collective-permute-start(f32[2,4,1,128,128]{4,3,2,1,0:T(8,128)S(1)} %get-tuple-element.276), channel_id=1, source_target_pairs={{0,1},{1,2},{2,3},{3,4},{4,5},{5,6},{6,7},{7,8},{8,9},{9,10},{10,1... | collective-permute-start | bytes 1572872 | tf_op jit(solution)/shard_map/while/body/eval_jaxpr/ppermute | solution.py:68
  234.1 24.2 %collective-permute-start.1 = (f32[2,4,1,128,128]{4,3,2,1,0:T(8,128)S(1)}, f32[2,4,1,128,128]{4,3,2,1,0:T(8,128)}, u32[]{:S(2)}, u32[]{:S(2)}) collective-permute-start(f32[2,4,1,128,128]{4,3,2,1,0:T(8,128)S(1)} %get-tuple-element.277), channel_id=1, source_target_pairs={{1,0},{2,1},{3,2},{4,3},{5,4},{6,5},{7,6},{8,7},{9,8},{10,9},{11,1... | collective-permute-start | bytes 1572872 | tf_op jit(solution)/shard_map/while/body/eval_jaxpr/ppermute | solution.py:70
  261.0 25.4 %collective-permute-start = (f32[2,4,1,128,128]{4,3,2,1,0:T(8,128)S(1)}, f32[2,4,1,128,128]{4,3,2,1,0:T(8,128)}, u32[]{:S(2)}, u32[]{:S(2)}) collective-permute-start(f32[2,4,1,128,128]{4,3,2,1,0:T(8,128)S(1)} %get-tuple-element.276), channel_id=1, source_target_pairs={{0,1},{1,2},{2,3},{3,4},{4,5},{5,6},{6,7},{7,8},{8,9},{9,10},{10,1... | collective-permute-start | bytes 1572872 | tf_op jit(solution)/shard_map/while/body/eval_jaxpr/ppermute | solution.py:68
  268.4 22.7 %collective-permute-start.1 = (f32[2,4,1,128,128]{4,3,2,1,0:T(8,128)S(1)}, f32[2,4,1,128,128]{4,3,2,1,0:T(8,128)}, u32[]{:S(2)}, u32[]{:S(2)}) collective-permute-start(f32[2,4,1,128,128]{4,3,2,1,0:T(8,128)S(1)} %get-tuple-element.277), channel_id=1, source_target_pairs={{1,0},{2,1},{3,2},{4,3},{5,4},{6,5},{7,6},{8,7},{9,8},{10,9},{11,1... | collective-permute-start | bytes 1572872 | tf_op jit(solution)/shard_map/while/body/eval_jaxpr/ppermute | solution.py:70
  293.8 22.6 %collective-permute-start = (f32[2,4,1,128,128]{4,3,2,1,0:T(8,128)S(1)}, f32[2,4,1,128,128]{4,3,2,1,0:T(8,128)}, u32[]{:S(2)}, u32[]{:S(2)}) collective-permute-start(f32[2,4,1,128,128]{4,3,2,1,0:T(8,128)S(1)} %get-tuple-element.276), channel_id=1, source_target_pairs={{0,1},{1,2},{2,3},{3,4},{4,5},{5,6},{6,7},{7,8},{8,9},{9,10},{10,1... | collective-permute-start | bytes 1572872 | tf_op jit(solution)/shard_map/while/body/eval_jaxpr/ppermute | solution.py:68
  297.9 26.6 %collective-permute-start.1 = (f32[2,4,1,128,128]{4,3,2,1,0:T(8,128)S(1)}, f32[2,4,1,128,128]{4,3,2,1,0:T(8,128)}, u32[]{:S(2)}, u32[]{:S(2)}) collective-permute-start(f32[2,4,1,128,128]{4,3,2,1,0:T(8,128)S(1)} %get-tuple-element.277), channel_id=1, source_target_pairs={{1,0},{2,1},{3,2},{4,3},{5,4},{6,5},{7,6},{8,7},{9,8},{10,9},{11,1... | collective-permute-start | bytes 1572872 | tf_op jit(solution)/shard_map/while/body/eval_jaxpr/ppermute | solution.py:70
  327.2 24.8 %collective-permute-start = (f32[2,4,1,128,128]{4,3,2,1,0:T(8,128)S(1)}, f32[2,4,1,128,128]{4,3,2,1,0:T(8,128)}, u32[]{:S(2)}, u32[]{:S(2)}) collective-permute-start(f32[2,4,1,128,128]{4,3,2,1,0:T(8,128)S(1)} %get-tuple-element.276), channel_id=1, source_target_pairs={{0,1},{1,2},{2,3},{3,4},{4,5},{5,6},{6,7},{7,8},{8,9},{9,10},{10,1... | collective-permute-start | bytes 1572872 | tf_op jit(solution)/shard_map/while/body/eval_jaxpr/ppermute | solution.py:68
  329.1 26.7 %collective-permute-start.1 = (f32[2,4,1,128,128]{4,3,2,1,0:T(8,128)S(1)}, f32[2,4,1,128,128]{4,3,2,1,0:T(8,128)}, u32[]{:S(2)}, u32[]{:S(2)}) collective-permute-start(f32[2,4,1,128,128]{4,3,2,1,0:T(8,128)S(1)} %get-tuple-element.277), channel_id=1, source_target_pairs={{1,0},{2,1},{3,2},{4,3},{5,4},{6,5},{7,6},{8,7},{9,8},{10,9},{11,1... | collective-permute-start | bytes 1572872 | tf_op jit(solution)/shard_map/while/body/eval_jaxpr/ppermute | solution.py:70
  358.5 26.8 %collective-permute-start = (f32[2,4,1,128,128]{4,3,2,1,0:T(8,128)S(1)}, f32[2,4,1,128,128]{4,3,2,1,0:T(8,128)}, u32[]{:S(2)}, u32[]{:S(2)}) collective-permute-start(f32[2,4,1,128,128]{4,3,2,1,0:T(8,128)S(1)} %get-tuple-element.276), channel_id=1, source_target_pairs={{0,1},{1,2},{2,3},{3,4},{4,5},{5,6},{6,7},{7,8},{8,9},{9,10},{10,1... | collective-permute-start | bytes 1572872 | tf_op jit(solution)/shard_map/while/body/eval_jaxpr/ppermute | solution.py:68
  363.5 23.5 %collective-permute-start.1 = (f32[2,4,1,128,128]{4,3,2,1,0:T(8,128)S(1)}, f32[2,4,1,128,128]{4,3,2,1,0:T(8,128)}, u32[]{:S(2)}, u32[]{:S(2)}) collective-permute-start(f32[2,4,1,128,128]{4,3,2,1,0:T(8,128)S(1)} %get-tuple-element.277), channel_id=1, source_target_pairs={{1,0},{2,1},{3,2},{4,3},{5,4},{6,5},{7,6},{8,7},{9,8},{10,9},{11,1... | collective-permute-start | bytes 1572872 | tf_op jit(solution)/shard_map/while/body/eval_jaxpr/ppermute | solution.py:70
  395.4 39.6 %all-to-all-start.4 = ((f32[8,2,2,4,2,8,128]{6,5,4,3,2,1,0:T(8,128)}), f32[8,2,2,4,2,8,128]{6,5,4,3,2,1,0:T(8,128)S(1)}, u32[]{:S(2)}, u32[]{:S(2)}) async-start(f32[8,2,2,4,2,8,128]{6,5,4,3,2,1,0:T(8,128)} %copy.90), calls=%async_computation.4 | async-start | bytes 2097152 | tf_op jit(solution)/shard_map/all_to_all | solution.py:50
where the time goes:
time: 453 us; the launch traced here: 452 us
  waiting for transfers between devices  282 us (62%)
  starting transfers between devices  103 us (23%)
  other arithmetic  30.8 us (7%)
  blocking collectives  22.8 us (5%)
  local copies, waits for them, and re-layouts  8.98 us (2%)
    ppermute x11, waiting for transfers between devices, padded_2(): lax.ppermute(tail, axis, [(i, (i + 1) % count) for i in range(ends)])  158 us
    ppermute x11, waiting for transfers between devices, padded_2(): lax.ppermute(head, axis, [((i + 1) % count, i) for i in range(ends)])  81.2 us
    ppermute x11, starting transfers between devices, padded_2(): lax.ppermute(tail, axis, [(i, (i + 1) % count) for i in range(ends)])  37.1 us
    ppermute x11, starting transfers between devices, padded_2(): lax.ppermute(head, axis, [((i + 1) % count, i) for i in range(ends)])  33.1 us
    all_to_all x2, waiting for transfers between devices, moved_by_axis(): lax.all_to_all(pieces, axes[k], split_axis=k, concat_axis=k, tiled=True)  31.7 us
    all_to_all x2, starting transfers between devices, moved_by_axis(): lax.all_to_all(pieces, axes[k], split_axis=k, concat_axis=k, tiled=True)  27.2 us
    add x11, other arithmetic, sweep(): return block_solve(coefficient, sources + MU * neighbour_sum(zpadded))  19.8 us
    all_to_all x1, blocking collectives, in_one_piece(): lax.all_to_all(both, axis, split_axis=split_dim, concat_axis=concat_dim,...  13.7 us
  transfers between devices with their start and end apart: 25, of which 25 were waited for; matrix products, arithmetic and copies ran while one was open for 0% of the time, Pallas kernels for 0%

commit v1 on v0

v1 whole, which is shorter than its diff:
```python
import math

import jax
import jax.numpy as jnp
from jax import lax
from jax.experimental import pallas as pl
from jax.experimental.pallas import tpu as pltpu
from jax.sharding import Mesh
from jax.sharding import PartitionSpec as P

STEPS = 32
SWEEPS = 12
ALPHA = 0.1
MU = 1.0
BETA = 1.0

TM = ("x", "zl", "core")
SPACE = ("zh", "y")

HALO = SWEEPS - 1
ROWS = 8
WINDOW = ROWS + 2 * HALO
FAR = HALO - ROWS


def place_of(index):
    ix, zl, core = index // 4, (index // 2) % 2, index % 2
    turn = (zl + ix) % 2
    return 4 * ix + 2 * turn + (core + turn) % 2


PLACE = [place_of(i) for i in range(16)]
HOLDER = [PLACE.index(p) for p in range(16)]


def my_place():
    ix, zl, core = lax.axis_index("x"), lax.axis_index("zl"), lax.axis_index("core")
    turn = (zl + ix) % 2
    return 4 * ix + 2 * turn + (core + turn) % 2


def my_freq():
    return lax.axis_index("zh") * 4 + lax.axis_index("y")


def add(a, b):
    return a[0] + b[0], a[1] + b[1]


def sub(a, b):
    return a[0] - b[0], a[1] - b[1]


def turned(a, k, n, sign):
    re, im = a
    if k == 0:
        return a
    if 4 * k == n:
        return (-im, re) if sign > 0 else (im, -re)
    if 8 * k == n:
        h = math.sqrt(0.5)
        return (h * (re - im), h * (im + re)) if sign > 0 else (h * (re + im), h * (im - re))
    if 8 * k == 3 * n:
        h = math.sqrt(0.5)
        return (-h * (re + im), h * (re - im)) if sign > 0 else (h * (im - re), -h * (re + im))
    c = math.cos(2.0 * math.pi * k / n)
    s = sign * math.sin(2.0 * math.pi * k / n)
    return c * re - s * im, c * im + s * re


def fourier(values, sign):
    n = len(values)
    if n == 1:
        return values
    even = fourier(values[0::2], sign)
    odd = fourier(values[1::2], sign)
    odd = [turned(odd[k], k, n, sign) for k in range(n // 2)]
    return [add(e, o) for e, o in zip(even, odd)] + [sub(e, o) for e, o in zip(even, odd)]


def growth(n):
    return math.exp(math.log(ALPHA) * n / STEPS)


def forward_kernel(times, reaction, out):
    first = pl.multiple_of(my_place() * ROWS, ROWS)
    for z in range(2):
        values = [
            (
                times[n // 2, 0, n % 2, z] * growth(n),
                times[(31 - n) // 2, 1, (31 - n) % 2, z] * growth(n),
            )
            for n in range(STEPS)
        ]
        hat = fourier(values, -1)
        here = reaction[z, pl.ds(first, ROWS), :]
        for k in range(16):
            out[k, 0, z] = hat[k][0]
            out[k, 1, z] = hat[k][1]
            out[k, 2, z] = hat[k + 16][0]
            out[k, 3, z] = hat[k + 16][1]
            out[k, 4, z] = here


def backward_kernel(solved, out):
    for z in range(2):
        values = [
            (solved[k % 16, 2 * (k // 16), z], solved[k % 16, 2 * (k // 16) + 1, z])
            for k in range(STEPS)
        ]
        back = fourier(values, 1)
        for n in range(STEPS):
            scale = 1.0 / (growth(n) * STEPS)
            out[n // 2, 0, n % 2, z] = back[n][0] * scale
            out[(31 - n) // 2, 1, (31 - n) % 2, z] = back[n][1] * scale


def sweep_kernel(left2, left1, own, right1, right2, out, src, coef, u0, u1):
    rate = math.exp(math.log(ALPHA) / STEPS)
    freq = my_freq()
    cos, sin = jnp.float32(1.0), jnp.float32(0.0)
    for k in range(1, 16):
        cos = jnp.where(freq == k, jnp.float32(math.cos(math.pi * k / 16)), cos)
        sin = jnp.where(freq == k, jnp.float32(math.sin(math.pi * k / 16)), sin)
    shift_re = (1.0 - rate * cos + 6.0 * MU, 1.0 + rate * cos + 6.0 * MU)
    shift_im = (BETA + rate * sin, BETA - rate * sin)
    start = my_place() * ROWS - HALO

    def prepare(ref, ref_row, row):
        inside = jnp.logical_and(start + row >= 0, start + row < 16 * ROWS)
        keep = jnp.where(inside, jnp.float32(1.0), jnp.float32(0.0))
        for j in range(4):
            at = slice(8 * j, 8 * j + 8)
            reaction = MU * ref[ref_row, 4, at, :]
            for f in range(2):
                d_re = reaction + shift_re[f]
                d_im = shift_im[f]
                scale = keep / (d_re * d_re + d_im * d_im)
                g_re = d_re * scale
                g_im = -d_im * scale
                re = ref[ref_row, 2 * f, at, :]
                im = ref[ref_row, 2 * f + 1, at, :]
                coef[row, 2 * f, at, :] = g_re
                coef[row, 2 * f + 1, at, :] = g_im
                src[row, 2 * f, at, :] = re
                src[row, 2 * f + 1, at, :] = im
                u0[row, 2 * f, at, :] = g_re * re - g_im * im
                u0[row, 2 * f + 1, at, :] = g_re * im + g_im * re

    def spread(ref, first, count):
        def step(i, carry):
            prepare(ref, i, first + i)
            return carry

        lax.fori_loop(0, count, step, 0)

    spread(left2, 0, FAR)
    spread(left1, FAR, ROWS)
    spread(own, HALO, ROWS)
    spread(right1, HALO + ROWS, ROWS)
    spread(right2, HALO + 2 * ROWS, FAR)

    lane = lax.broadcasted_iota(jnp.int32, (8, 128), 1)
    sublane = lax.broadcasted_iota(jnp.int32, (8, 128), 0)
    first_lane, last_lane = lane == 0, lane == 127
    first_sub, last_sub = sublane == 0, sublane == 7
    zero = jnp.zeros((8, 128), jnp.float32)

    def total(old, row, c):
        tiles = [old[row, c, 8 * j : 8 * j + 8, :] for j in range(4)]
        down = [pltpu.roll(t, 1, 0) for t in tiles]
        up = [pltpu.roll(t, 7, 0) for t in tiles]
        sums = []
        for j in range(4):
            at = slice(8 * j, 8 * j + 8)
            below = jnp.where(first_sub, down[j - 1] if j > 0 else zero, down[j])
            above = jnp.where(last_sub, up[j + 1] if j < 3 else zero, up[j])
            sides = jnp.where(first_lane, zero, pltpu.roll(tiles[j], 1, 1))
            sides = sides + jnp.where(last_lane, zero, pltpu.roll(tiles[j], 127, 1))
            outer = old[row - 1, c, at, :] + old[row + 1, c, at, :]
            sums.append((below + above) + outer + sides)
        return sums

    def sweep(old, m, store):
        def step(row, carry):
            for f in range(2):
                nb_re = total(old, row, 2 * f)
                nb_im = total(old, row, 2 * f + 1)
                for j in range(4):
                    at = slice(8 * j, 8 * j + 8)
                    s_re = src[row, 2 * f, at, :] + MU * nb_re[j]
                    s_im = src[row, 2 * f + 1, at, :] + MU * nb_im[j]
                    g_re = coef[row, 2 * f, at, :]
                    g_im = coef[row, 2 * f + 1, at, :]
                    store(row, 2 * f, at, g_re * s_re - g_im * s_im)
                    store(row, 2 * f + 1, at, g_re * s_im + g_im * s_re)
            return carry

        lax.fori_loop(m, WINDOW - m, step, 0)

    def into(ref, offset):
        def store(row, c, at, value):
            ref[row - offset, c, at, :] = value

        return store

    def two(i, carry):
        sweep(u0, 2 * i + 1, into(u1, 0))
        sweep(u1, 2 * i + 2, into(u0, 0))
        return carry

    lax.fori_loop(0, (SWEEPS - 2) // 2, two, 0)
    sweep(u0, SWEEPS - 1, into(out, HALO))


def f32(*shape):
    return jax.ShapeDtypeStruct(shape, jnp.float32)


def body(state_rhs, adjoint_rhs, reaction):
    both = jnp.stack((state_rhs, adjoint_rhs)).reshape(2, 2, 2, 16, ROWS, 128)
    both = jnp.stack([both[:, :, :, p] for p in PLACE])
    times = lax.all_to_all(both, TM, 0, 0, tiled=True)
    spread = pl.pallas_call(forward_kernel, out_shape=f32(16, 5, 2, ROWS, 128), name="forward")(
        times, reaction
    )
    got = lax.all_to_all(spread, SPACE, 0, 0, tiled=True)
    own = jnp.transpose(got, (3, 1, 0, 2, 4)).reshape(ROWS, 5, 32, 128)
    ahead = [(HOLDER[i], HOLDER[i + 1]) for i in range(15)]
    back = [(b, a) for a, b in ahead]
    ahead2 = [(HOLDER[i], HOLDER[i + 2]) for i in range(14)]
    back2 = [(b, a) for a, b in ahead2]
    left1 = lax.ppermute(own, TM, ahead)
    right1 = lax.ppermute(own, TM, back)
    left2 = lax.ppermute(own[ROWS - FAR :], TM, ahead2)
    right2 = lax.ppermute(own[:FAR], TM, back2)
    window = pltpu.VMEM((WINDOW, 4, 32, 128), jnp.float32)
    solved = pl.pallas_call(
        sweep_kernel,
        out_shape=f32(ROWS, 4, 32, 128),
        scratch_shapes=[window, window, window, window],
        name="sweeps",
    )(left2, left1, own, right1, right2)
    solved = jnp.transpose(solved.reshape(ROWS, 4, 16, 2, 128), (2, 1, 3, 0, 4))
    by_freq = lax.all_to_all(solved, SPACE, 0, 0, tiled=True)
    by_time = pl.pallas_call(
        backward_kernel, out_shape=f32(16, 2, 2, 2, ROWS, 128), name="backward"
    )(by_freq)
    final = lax.all_to_all(by_time, TM, 0, 0, tiled=True)
    final = jnp.stack([final[HOLDER[p]] for p in range(16)], axis=3).reshape(2, 2, 2, 128, 128)
    return final[0], final[1]


def solution(mesh):
    split = Mesh(mesh.devices.reshape(4, 2, 2, 4, 4), TM + SPACE)
    field = P(TM, SPACE, None, None)
    return jax.shard_map(
        body,
        mesh=split,
        in_specs=(field, field, P(SPACE, None, None)),
        out_specs=(field, field),
        check_vma=False,
    )
```

time: 453 us -> 138 us (0.30)
  the two profiles are of different devices: /device:TPU:88 before, /device:TPU:1 now
where the time goes in v1:
time: 138 us; the launch traced here: 137 us
  blocking collectives  79.7 us (58%)
  Pallas kernels  28.2 us (20%)
  starting transfers between devices  15.5 us (11%)
  waiting for transfers between devices  6.66 us (5%)
  local copies, waits for them, and re-layouts  5.01 us (4%)
    all_to_all x1, blocking collectives, body(): got = lax.all_to_all(spread, SPACE, 0, 0, tiled=True)  26.7 us
    pallas_call x1, Pallas kernels, body(): pl.pallas_call(sweep_kernel, out_shape=f32(ROWS, 4, 32, 128), scratch_sha...  24.1 us
    all_to_all x1, blocking collectives, body(): by_freq = lax.all_to_all(solved, SPACE, 0, 0, tiled=True)  18.3 us
    all_to_all x1, blocking collectives, body(): final = lax.all_to_all(by_time, TM, 0, 0, tiled=True)  17.9 us
    all_to_all x1, blocking collectives, body(): times = lax.all_to_all(both, TM, 0, 0, tiled=True)  16.7 us
    ppermute x1, waiting for transfers between devices, body(): left2 = lax.ppermute(own[ROWS - FAR:], TM, ahead2)  6.42 us
    ppermute x1, starting transfers between devices, body(): right1 = lax.ppermute(own, TM, back)  5.76 us
    ppermute x1, starting transfers between devices, body(): left2 = lax.ppermute(own[ROWS - FAR:], TM, ahead2)  4.66 us
  transfers between devices with their start and end apart: 4, of which 2 were waited for; matrix products, arithmetic and copies ran while one was open for 0% of the time, Pallas kernels for 0%

profile of v1, /device:TPU:1, one launch (start us, length us, event | category | flops | bytes accessed | tf_op | source)
XLA Modules:
  0.0 136.9 jit_solution(641821802029357025)
XLA Ops:
  0.6 0.0 copy-start
  0.6 0.0 copy-start.1
  0.6 0.8 constant_dynamic-update-slice_fusion.15
  1.4 0.2 copy-done
  1.6 0.1 copy-done.1
  1.9 16.7 %all_to_all.20.times = f32[16,2,2,2,8,128]{5,4,3,2,1,0:T(8,128)} all-to-all(f32[16,2,2,2,8,128]{5,4,3,2,1,0:T(8,128)S(1)} %constant_dynamic-update-slice_fusion), channel_id=1, replica_groups=mesh['x'=4,'zl'=2,'core'=2,'zh'=4,'y'=4] {'x','zl','core'}, dimensions={0} | all-to-all | bytes 1048576 | tf_op jit(solution)/shard_map/all_to_all | solution.py:223
  18.6 2.1 %forward.1 = f32[16,5,2,8,128]{4,3,2,1,0:T(8,128)} custom-call(f32[16,2,2,2,8,128]{5,4,3,2,1,0:T(8,128)} %all_to_all.20.times, f32[2,128,128]{2,1,0:T(8,128)} %reaction.1), custom_call_target="tpu_custom_call" | custom-call | tf_op jit(solution)/shard_map/forward/pallas_call | solution.py:224
  20.7 26.7 %all_to_all.21 = f32[16,5,2,8,128]{4,3,2,1,0:T(8,128)S(1)} all-to-all(f32[16,5,2,8,128]{4,3,2,1,0:T(8,128)} %forward.1), channel_id=1, replica_groups=mesh['x'=4,'zl'=2,'core'=2,'zh'=4,'y'=4] {'zh','y'}, dimensions={0} | all-to-all | bytes 1310720 | tf_op jit(solution)/shard_map/all_to_all | solution.py:227
  47.4 0.3 copy.11
  47.8 0.0 copy-start.2
  47.8 5.8 %collective-permute-start.2 = (f32[8,5,32,128]{3,2,1,0:T(8,128)S(1)}, f32[8,5,32,128]{3,2,1,0:T(8,128)S(1)}, u32[]{:S(2)}, u32[]{:S(2)}) collective-permute-start(f32[8,5,32,128]{3,2,1,0:T(8,128)S(1)} %bitcast.178), channel_id=1, source_target_pairs={{16,0},{48,16},{32,48},{96,32},{112,96},{80,112},{64,80},{128,64},... | collective-permute-start | bytes 1966088 | tf_op jit(solution)/shard_map/ppermute | solution.py:234
  53.5 3.8 %collective-permute-start.1 = (f32[8,5,32,128]{3,2,1,0:T(8,128)S(1)}, f32[8,5,32,128]{3,2,1,0:T(8,128)S(1)}, u32[]{:S(2)}, u32[]{:S(2)}) collective-permute-start(f32[8,5,32,128]{3,2,1,0:T(8,128)S(1)} %bitcast.179), channel_id=1, source_target_pairs={{0,16},{16,48},{48,32},{32,96},{96,112},{112,80},{80,64},{64,128},... | collective-permute-start | bytes 1966088 | tf_op jit(solution)/shard_map/ppermute | solution.py:233
  57.4 0.1 fusion.16
  57.5 0.0 copy-done.2
  57.5 0.1 copy.12
  57.6 0.1 copy.10
  57.8 4.7 %collective-permute-start = (f32[3,5,32,128]{3,2,1,0:T(8,128)S(1)}, f32[3,5,32,128]{3,2,1,0:T(8,128)S(1)}, u32[]{:S(2)}, u32[]{:S(2)}) collective-permute-start(f32[3,5,32,128]{3,2,1,0:T(8,128)S(1)} %bitcast.184), channel_id=1, source_target_pairs={{0,48},{16,32},{48,96},{32,112},{96,80},{112,64},{80,128},{64,144}... | collective-permute-start | bytes 737288 | tf_op jit(solution)/shard_map/ppermute | solution.py:235
  62.4 1.3 collective-permute-start.3
  63.7 6.4 %collective-permute-done.left2 = f32[3,5,32,128]{3,2,1,0:T(8,128)S(1)} collective-permute-done((f32[3,5,32,128]{3,2,1,0:T(8,128)S(1)}, f32[3,5,32,128]{3,2,1,0:T(8,128)S(1)}, u32[]{:S(2)}, u32[]{:S(2)}) %collective-permute-start) | collective-permute-done | bytes 245792 | tf_op jit(solution)/shard_map/ppermute | solution.py:235
  70.2 0.2 collective-permute-done.3.right2
  70.4 0.0 collective-permute-done.2.right1
  70.4 0.0 collective-permute-done.1.left1
  70.4 0.4 copy-done.5
  70.9 0.2 copy-done.6
  71.1 0.2 copy-done.3
  71.3 0.8 copy-done.4
  72.2 24.1 %sweeps.1 = f32[8,4,32,128]{3,2,1,0:T(8,128)} custom-call(f32[3,5,32,128]{3,2,1,0:T(8,128)} %copy-done.5, f32[8,5,32,128]{3,2,1,0:T(8,128)} %copy-done.4, f32[8,5,32,128]{3,2,1,0:T(8,128)} %bitcast.180, f32[8,5,32,128]{3,2,1,0:T(8,128)} %copy-done.3, f32[3,5,32,128]{3,2,1,0:T(8,128)} %copy-done.6), custom_call_target="tpu_custom_call" | custom-call | tf_op jit(solution)/shard_map/sweeps/pallas_call | solution.py:238
  96.3 1.3 copy.39
  97.6 18.3 %all_to_all.22.solved = f32[16,4,2,8,128]{4,3,2,1,0:T(8,128)} all-to-all(f32[16,4,2,8,128]{4,3,2,1,0:T(8,128)S(1)} %bitcast.181), channel_id=1, replica_groups=mesh['x'=4,'zl'=2,'core'=2,'zh'=4,'y'=4] {'zh','y'}, dimensions={0} | all-to-all | bytes 1048576 | tf_op jit(solution)/shard_map/all_to_all | solution.py:245
  115.9 2.0 %backward.1 = f32[16,2,2,2,8,128]{5,4,3,2,1,0:T(8,128)} custom-call(f32[16,4,2,8,128]{4,3,2,1,0:T(8,128)} %all_to_all.22.solved), custom_call_target="tpu_custom_call" | custom-call | tf_op jit(solution)/shard_map/backward/pallas_call | solution.py:246
  117.9 17.9 %all_to_all.23 = f32[16,2,2,2,8,128]{5,4,3,2,1,0:T(8,128)S(1)} all-to-all(f32[16,2,2,2,8,128]{5,4,3,2,1,0:T(8,128)} %backward.1), channel_id=1, replica_groups=mesh['x'=4,'zl'=2,'core'=2,'zh'=4,'y'=4] {'x','zl','core'}, dimensions={0} | all-to-all | bytes 1048576 | tf_op jit(solution)/shard_map/all_to_all | solution.py:249
  136.1 0.8 copy_bitcast_fusion.1
  (36 shorter events, 0.2 us)
Async XLA Ops:
  0.6 1.0 copy-start
  0.6 1.1 copy-start.1
  47.8 9.7 %copy-start.2 = (f32[8,5,16,2,128]{4,3,2,1,0:T(2,128)}, f32[8,5,16,2,128]{4,3,2,1,0:T(2,128)S(1)}, u32[]{:S(2)}) copy-start(f32[8,5,16,2,128]{4,3,2,1,0:T(2,128)S(1)} %copy.11) | copy-start | bytes 1966084
  47.8 22.6 %collective-permute-start.2 = (f32[8,5,32,128]{3,2,1,0:T(8,128)S(1)}, f32[8,5,32,128]{3,2,1,0:T(8,128)S(1)}, u32[]{:S(2)}, u32[]{:S(2)}) collective-permute-start(f32[8,5,32,128]{3,2,1,0:T(8,128)S(1)} %bitcast.178), channel_id=1, source_target_pairs={{16,0},{48,16},{32,48},{96,32},{112,96},{80,112},{64,80},{128,64},... | collective-permute-start | bytes 1966088 | tf_op jit(solution)/shard_map/ppermute | solution.py:234
  53.5 16.9 %collective-permute-start.1 = (f32[8,5,32,128]{3,2,1,0:T(8,128)S(1)}, f32[8,5,32,128]{3,2,1,0:T(8,128)S(1)}, u32[]{:S(2)}, u32[]{:S(2)}) collective-permute-start(f32[8,5,32,128]{3,2,1,0:T(8,128)S(1)} %bitcast.179), channel_id=1, source_target_pairs={{0,16},{16,48},{48,32},{32,96},{96,112},{112,80},{80,64},{64,128},... | collective-permute-start | bytes 1966088 | tf_op jit(solution)/shard_map/ppermute | solution.py:233
  57.8 12.4 %collective-permute-start = (f32[3,5,32,128]{3,2,1,0:T(8,128)S(1)}, f32[3,5,32,128]{3,2,1,0:T(8,128)S(1)}, u32[]{:S(2)}, u32[]{:S(2)}) collective-permute-start(f32[3,5,32,128]{3,2,1,0:T(8,128)S(1)} %bitcast.184), channel_id=1, source_target_pairs={{0,48},{16,32},{48,96},{32,112},{96,80},{112,64},{80,128},{64,144}... | collective-permute-start | bytes 737288 | tf_op jit(solution)/shard_map/ppermute | solution.py:235
  62.4 8.0 %collective-permute-start.3 = (f32[3,5,32,128]{3,2,1,0:T(8,128)S(1)}, f32[3,5,32,128]{3,2,1,0:T(8,128)S(1)}, u32[]{:S(2)}, u32[]{:S(2)}) collective-permute-start(f32[3,5,32,128]{3,2,1,0:T(8,128)S(1)} %bitcast.183), channel_id=1, source_target_pairs={{48,0},{32,16},{96,48},{112,32},{80,96},{64,112},{128,80},{144,64}... | collective-permute-start | bytes 737288 | tf_op jit(solution)/shard_map/ppermute | solution.py:236
  70.2 0.7 copy-start.5
  70.4 0.7 copy-start.6
  70.4 0.9 copy-start.3
  71.3 0.8 copy-start.4

commit v2 on v1

v2 whole, which is shorter than its diff:
```python
import math

import jax
import jax.numpy as jnp
from jax import lax
from jax.experimental import pallas as pl
from jax.experimental.pallas import tpu as pltpu
from jax.sharding import Mesh
from jax.sharding import PartitionSpec as P

STEPS = 32
SWEEPS = 12
ALPHA = 0.1
MU = 1.0
BETA = 1.0

TM = ("x", "zl", "core")
SPACE = ("zh", "y")
FREQ = ("zh", "y", "core")

HALO = SWEEPS - 1
ROWS = 8
BLOCK = 2 * ROWS
WINDOW = BLOCK + 2 * HALO
PADDED = 40
VMEM = 12 << 20


def place_of(ix, zl):
    return 2 * ix + (zl + ix) % 2


PLACE = [2 * place_of(i // 4, (i // 2) % 2) + i % 2 for i in range(16)]
HOLDER = [PLACE.index(p) for p in range(16)]


def my_place():
    return place_of(lax.axis_index("x"), lax.axis_index("zl"))


def my_freq():
    return lax.axis_index("zh") * 8 + lax.axis_index("y") * 2 + lax.axis_index("core")


def add(a, b):
    return a[0] + b[0], a[1] + b[1]


def sub(a, b):
    return a[0] - b[0], a[1] - b[1]


def turned(a, k, n, sign):
    re, im = a
    if k == 0:
        return a
    if 4 * k == n:
        return (-im, re) if sign > 0 else (im, -re)
    if 8 * k == n:
        h = math.sqrt(0.5)
        return (h * (re - im), h * (im + re)) if sign > 0 else (h * (re + im), h * (im - re))
    if 8 * k == 3 * n:
        h = math.sqrt(0.5)
        return (-h * (re + im), h * (re - im)) if sign > 0 else (h * (im - re), -h * (re + im))
    c = math.cos(2.0 * math.pi * k / n)
    s = sign * math.sin(2.0 * math.pi * k / n)
    return c * re - s * im, c * im + s * re


def fourier(values, sign):
    n = len(values)
    if n == 1:
        return values
    even = fourier(values[0::2], sign)
    odd = fourier(values[1::2], sign)
    odd = [turned(odd[k], k, n, sign) for k in range(n // 2)]
    return [add(e, o) for e, o in zip(even, odd)] + [sub(e, o) for e, o in zip(even, odd)]


def growth(n):
    return math.exp(math.log(ALPHA) * n / STEPS)


def forward_kernel(times, out):
    for z in range(2):
        values = [
            (
                times[n // 2, 0, n % 2, z] * growth(n),
                times[(31 - n) // 2, 1, (31 - n) % 2, z] * growth(n),
            )
            for n in range(STEPS)
        ]
        hat = fourier(values, -1)
        for k in range(STEPS):
            out[k, 0, z] = hat[k][0]
            out[k, 1, z] = hat[k][1]


def backward_kernel(solved, out):
    for z in range(2):
        values = [(solved[k, 0, z], solved[k, 1, z]) for k in range(STEPS)]
        back = fourier(values, 1)
        for n in range(STEPS):
            scale = 1.0 / (growth(n) * STEPS)
            out[n // 2, 0, n % 2, z] = back[n][0] * scale
            out[(31 - n) // 2, 1, (31 - n) % 2, z] = back[n][1] * scale


def planes_to_rows_kernel(got, out):
    for half in range(2):
        for c in range(2):
            for j in range(4):
                tiles = got[:, j // 2, half, c, j % 2]
                out[ROWS * half : ROWS * half + ROWS, c, j] = jnp.swapaxes(tiles, 0, 1)


def rows_to_planes_kernel(solved, out):
    for half in range(2):
        for c in range(2):
            for j in range(4):
                tiles = solved[ROWS * half : ROWS * half + ROWS, c, j]
                out[:, j // 2, half, c, j % 2] = jnp.swapaxes(tiles, 0, 1)


def coefficient_kernel(reaction, coef):
    rate = math.exp(math.log(ALPHA) / STEPS)
    freq = my_freq()
    cos, sin = jnp.float32(1.0), jnp.float32(0.0)
    for k in range(1, STEPS):
        cos = jnp.where(freq == k, jnp.float32(math.cos(2.0 * math.pi * k / STEPS)), cos)
        sin = jnp.where(freq == k, jnp.float32(math.sin(2.0 * math.pi * k / STEPS)), sin)
    shift_re = 1.0 - rate * cos + 6.0 * MU
    d_im = BETA + rate * sin
    start = my_place() * BLOCK - HALO
    for j in range(4):
        for first in range(0, PADDED, ROWS):
            tiles = reaction[:, j // 2, j % 2, first : first + ROWS]
            d_re = MU * jnp.swapaxes(tiles, 0, 1) + shift_re
            row = start + first + lax.broadcasted_iota(jnp.int32, (ROWS, 8, 128), 0)
            inside = jnp.logical_and(row >= 0, row < 16 * ROWS)
            scale = jnp.where(inside, 1.0, 0.0) / (d_re * d_re + d_im * d_im)
            coef[first : first + ROWS, 0, j] = d_re * scale
            coef[first : first + ROWS, 1, j] = -d_im * scale


def sweep_kernel(left, own, right, coef, out, src, u0, u1):
    def prepare(ref, ref_row, row):
        for j in range(4):
            g_re, g_im = coef[row, 0, j], coef[row, 1, j]
            re, im = ref[ref_row, 0, j], ref[ref_row, 1, j]
            src[row, 0, j] = re
            src[row, 1, j] = im
            u0[row, 0, j] = g_re * re - g_im * im
            u0[row, 1, j] = g_re * im + g_im * re

    def spread(ref, first, count):
        def step(i, carry):
            prepare(ref, i, first + i)
            return carry

        lax.fori_loop(0, count, step, 0)

    spread(left, 0, HALO)
    spread(own, HALO, BLOCK)
    spread(right, HALO + BLOCK, HALO)

    lane = lax.broadcasted_iota(jnp.int32, (8, 128), 1)
    sublane = lax.broadcasted_iota(jnp.int32, (8, 128), 0)
    first_lane, last_lane = lane == 0, lane == 127
    first_sub, last_sub = sublane == 0, sublane == 7
    zero = jnp.zeros((8, 128), jnp.float32)

    def total(old, row, c):
        tiles = [old[row, c, j] for j in range(4)]
        below = [jnp.where(first_sub, zero, pltpu.roll(tiles[3], 1, 0))] + tiles[:3]
        above = tiles[1:] + [jnp.where(last_sub, zero, pltpu.roll(tiles[0], 7, 0))]
        sums = []
        for j in range(4):
            sides = jnp.where(first_lane, zero, pltpu.roll(tiles[j], 1, 1))
            sides = sides + jnp.where(last_lane, zero, pltpu.roll(tiles[j], 127, 1))
            outer = old[row - 1, c, j] + old[row + 1, c, j]
            sums.append(src[row, c, j] + MU * (((below[j] + above[j]) + outer) + sides))
        return sums

    for m in range(1, SWEEPS):
        old, new = (u0, u1) if m % 2 else (u1, u0)
        for row in range(m, WINDOW - m):
            s_re, s_im = total(old, row, 0), total(old, row, 1)
            for j in range(4):
                g_re, g_im = coef[row, 0, j], coef[row, 1, j]
                re = g_re * s_re[j] - g_im * s_im[j]
                im = g_re * s_im[j] + g_im * s_re[j]
                if m < SWEEPS - 1:
                    new[row, 0, j] = re
                    new[row, 1, j] = im
                else:
                    out[row - HALO, 0, j] = re
                    out[row - HALO, 1, j] = im


def call(kernel, shape, *args, scratch=()):
    return pl.pallas_call(
        kernel,
        out_shape=pltpu.VMEM(shape, jnp.float32),
        scratch_shapes=scratch,
        name=kernel.__name__,
        compiler_params=pltpu.CompilerParams(vmem_limit_bytes=VMEM),
    )(*[pltpu.with_memory_space_constraint(a, pltpu.VMEM) for a in args])


def body(state_rhs, adjoint_rhs, reaction):
    near = jnp.pad(reaction, ((0, 0), (HALO, PADDED - BLOCK - HALO), (0, 0)))
    near = lax.dynamic_slice_in_dim(near, my_place() * BLOCK, PADDED, axis=1)
    near = lax.all_to_all(jnp.broadcast_to(near, (16,) + near.shape), SPACE, 0, 0, tiled=True)
    coef = call(
        coefficient_kernel, (PADDED, 2, 4, 8, 128), near.reshape(8, 2, 2, PADDED, 128)
    )

    both = jnp.stack((state_rhs, adjoint_rhs)).reshape(2, 2, 2, 16, ROWS, 128)
    both = jnp.stack([both[:, :, :, p] for p in PLACE])
    times = lax.all_to_all(both, TM, 0, 0, tiled=True)
    hat = call(forward_kernel, (STEPS, 2, 2, ROWS, 128), times)
    got = lax.all_to_all(hat, FREQ, 0, 0, tiled=True)
    own = call(
        planes_to_rows_kernel, (BLOCK, 2, 4, 8, 128), got.reshape(8, 2, 2, 2, 2, ROWS, 128)
    )
    chain = [[HOLDER[2 * i + core] for i in range(8)] for core in range(2)]
    ahead = [(c[i], c[i + 1]) for c in chain for i in range(7)]
    left = lax.ppermute(own[BLOCK - HALO :], TM, ahead)
    right = lax.ppermute(own[:HALO], TM, [(b, a) for a, b in ahead])
    window = pltpu.VMEM((WINDOW, 2, 4, 8, 128), jnp.float32)
    solved = call(
        sweep_kernel, (BLOCK, 2, 4, 8, 128), left, own, right, coef, scratch=[window] * 3
    )
    solved = call(rows_to_planes_kernel, (8, 2, 2, 2, 2, ROWS, 128), solved)
    by_freq = lax.all_to_all(
        solved.reshape(STEPS, 2, 2, ROWS, 128), FREQ, 0, 0, tiled=True
    )
    by_time = call(backward_kernel, (16, 2, 2, 2, ROWS, 128), by_freq)
    final = lax.all_to_all(by_time, TM, 0, 0, tiled=True)
    final = jnp.stack([final[HOLDER[p]] for p in range(16)], axis=3).reshape(2, 2, 2, 128, 128)
    return final[0], final[1]


def solution(mesh):
    split = Mesh(mesh.devices.reshape(4, 2, 2, 4, 4), TM + SPACE)
    field = P(TM, SPACE, None, None)
    return jax.shard_map(
        body,
        mesh=split,
        in_specs=(field, field, P(SPACE, None, None)),
        out_specs=(field, field),
        check_vma=False,
    )
```

time: 138 us -> 125 us (0.906)
  waiting for transfers between devices: 6.66 us -> 34.1 us
  blocking collectives: 79.7 us -> 57.4 us
  Pallas kernels: 28.2 us -> 7.01 us
  starting transfers between devices: 15.5 us -> 20.6 us
  local copies, waits for them, and re-layouts: 5.01 us -> 1.95 us
  other arithmetic: 0.89 us -> 2.36 us
    all_to_all x0 -> x2, waiting for transfers between devices: none -> 33 us  [the longest x1 18.4 us: body(): got = lax.all_to_all(hat, FREQ, 0, 0, tiled=True)]
    pallas_call x3 -> x6, Pallas kernels: 28.2 us -> 7.01 us  [call(): pl.pallas_call(kernel, out_shape=pltpu.VMEM(shape, jnp.float32), scratch_...]
    all_to_all x2 -> x1, blocking collectives: 45 us -> 29.4 us  [body(): lax.all_to_all(solved.reshape(STEPS, 2, 2, ROWS, 128), FREQ, 0, 0, tiled=...]
    all_to_all x0 -> x2, starting transfers between devices: none -> 15.3 us  [the longest x1 11.6 us: body(): got = lax.all_to_all(hat, FREQ, 0, 0, tiled=True)]
    ppermute x4 -> x2, starting transfers between devices: 15.5 us -> 5.3 us  [the longest x1 4.01 us: body(): left = lax.ppermute(own[BLOCK - HALO:], TM, ahead)]
    all_to_all x1, blocking collectives: 17.9 us -> 11.4 us  [body(): final = lax.all_to_all(by_time, TM, 0, 0, tiled=True)]
    ppermute x4 -> x2, waiting for transfers between devices: 6.66 us -> 1.09 us  [the longest x1 1.09 us: body(): right = lax.ppermute(own[:HALO], TM, [(b, a) for a, b in ahead])]
    unnamed x29 -> x21, local copies, waits for them, and re-layouts: 2.09 us -> 0.09 us
  transfers between devices with their start and end apart: 4 -> 4, of which waited for: 2 -> 3; matrix products, arithmetic and copies ran while one was open for 0% -> 0% of each run, Pallas kernels for 0% -> 0%
where the time goes in v2:
time: 125 us; the launch traced here: 124 us
  blocking collectives  57.4 us (46%)
  waiting for transfers between devices  34.1 us (27%)
  starting transfers between devices  20.6 us (16%)
  Pallas kernels  7.01 us (6%)
  other arithmetic  2.36 us (2%)
  local copies, waits for them, and re-layouts  1.95 us (2%)
    all_to_all x1, blocking collectives, body(): lax.all_to_all(solved.reshape(STEPS, 2, 2, ROWS, 128), FREQ, 0, 0, tiled=...  29.4 us
    all_to_all x1, waiting for transfers between devices, body(): got = lax.all_to_all(hat, FREQ, 0, 0, tiled=True)  18.4 us
    all_to_all x1, blocking collectives, body(): times = lax.all_to_all(both, TM, 0, 0, tiled=True)  16.6 us
    all_to_all x1, waiting for transfers between devices, body(): lax.all_to_all(jnp.broadcast_to(near, (16,) + near.shape), SPACE, 0, 0, t...  14.5 us
    all_to_all x1, starting transfers between devices, body(): got = lax.all_to_all(hat, FREQ, 0, 0, tiled=True)  11.6 us
    all_to_all x1, blocking collectives, body(): final = lax.all_to_all(by_time, TM, 0, 0, tiled=True)  11.4 us
    pallas_call x6, Pallas kernels, call(): pl.pallas_call(kernel, out_shape=pltpu.VMEM(shape, jnp.float32), scratch_...  7.01 us
    ppermute x1, starting transfers between devices, body(): left = lax.ppermute(own[BLOCK - HALO:], TM, ahead)  4.01 us
  transfers between devices with their start and end apart: 4, of which 3 were waited for; matrix products, arithmetic and copies ran while one was open for 0% of the time, Pallas kernels for 0%

profile of v2, /device:TPU:1, one launch (start us, length us, event | category | flops | bytes accessed | tf_op | source)
XLA Modules:
  0.0 124.3 jit_solution(6718618735673176733)
XLA Ops:
  0.6 0.0 copy-start
  0.6 0.0 copy-start.1
  0.7 0.8 constant_dynamic-update-slice_fusion.15
  1.4 0.7 constant_dynamic-update-slice_fusion.14
  2.2 0.7 constant_dynamic-update-slice_fusion.13
  2.9 0.0 copy-done
  2.9 0.0 copy-done.1
  3.1 16.6 %all_to_all.25.times = f32[16,2,2,2,8,128]{5,4,3,2,1,0:T(8,128)S(1)} all-to-all(f32[16,2,2,2,8,128]{5,4,3,2,1,0:T(8,128)S(1)} %constant_dynamic-update-slice_fusion), channel_id=1, replica_groups=mesh['x'=4,'zl'=2,'core'=2,'zh'=4,'y'=4] {'x','zl','core'}, dimensions={0} | all-to-all | bytes 1048576 | tf_op jit(solution)/shard_map/all_to_all | solution.py:221
  19.7 0.0 copy-start.2
  19.7 1.0 forward_kernel.1
  20.7 11.6 %all-to-all-start.1 = ((f32[32,2,2,8,128]{4,3,2,1,0:T(8,128)}), f32[32,2,2,8,128]{4,3,2,1,0:T(8,128)S(1)}, u32[]{:S(2)}, u32[]{:S(2)}) async-start(f32[32,2,2,8,128]{4,3,2,1,0:T(8,128)} %forward_kernel.1), calls=%async_computation.1 | async-start | bytes 1048576 | tf_op jit(solution)/shard_map/all_to_all | solution.py:223
  32.4 0.0 copy-done.2
  32.4 18.4 %all-to-all-done.1 = f32[32,2,2,8,128]{4,3,2,1,0:T(8,128)S(1)} async-done(((f32[32,2,2,8,128]{4,3,2,1,0:T(8,128)}), f32[32,2,2,8,128]{4,3,2,1,0:T(8,128)S(1)}, u32[]{:S(2)}, u32[]{:S(2)}) %all-to-all-start.1) | async-done | bytes 524320 | tf_op jit(solution)/shard_map/all_to_all | solution.py:223
  50.8 0.9 broadcast_in_dim.3
  51.7 3.6 %all-to-all-start.2 = ((f32[16,2,40,128]{3,2,1,0:T(8,128)}), f32[16,2,40,128]{3,2,1,0:T(8,128)S(1)}, u32[]{:S(2)}, u32[]{:S(2)}) async-start(f32[16,2,40,128]{3,2,1,0:T(8,128)} %broadcast_in_dim.3), calls=%async_computation.2 | async-start | bytes 1310720 | tf_op jit(solution)/shard_map/all_to_all | solution.py:214
  55.4 0.1 planes_to_rows_kernel.1.own
  55.5 0.1 fusion.17
  55.6 1.3 %collective-permute-start.1 = (f32[11,2,4,8,128]{4,3,2,1,0:T(8,128)S(1)}, f32[11,2,4,8,128]{4,3,2,1,0:T(8,128)S(1)}, u32[]{:S(2)}, u32[]{:S(2)}) collective-permute-start(f32[11,2,4,8,128]{4,3,2,1,0:T(8,128)S(1)} %get-tuple-element.4), channel_id=1, source_target_pairs={{32,0},{96,32},{64,96},{128,64},{160,128},{224,160},{192,224},{48,... | collective-permute-start | bytes 1081352 | tf_op jit(solution)/shard_map/ppermute | solution.py:230
  56.9 4.0 %collective-permute-start = (f32[11,2,4,8,128]{4,3,2,1,0:T(8,128)S(1)}, f32[11,2,4,8,128]{4,3,2,1,0:T(8,128)S(1)}, u32[]{:S(2)}, u32[]{:S(2)}) collective-permute-start(f32[11,2,4,8,128]{4,3,2,1,0:T(8,128)S(1)} %get-tuple-element.5), channel_id=1, source_target_pairs={{0,32},{32,96},{96,64},{64,128},{128,160},{160,224},{224,192},{16,... | collective-permute-start | bytes 1081352 | tf_op jit(solution)/shard_map/ppermute | solution.py:229
  60.9 14.5 %all-to-all-done.2 = f32[16,2,40,128]{3,2,1,0:T(8,128)S(1)} async-done(((f32[16,2,40,128]{3,2,1,0:T(8,128)}), f32[16,2,40,128]{3,2,1,0:T(8,128)S(1)}, u32[]{:S(2)}, u32[]{:S(2)}) %all-to-all-start.2) | async-done | bytes 655392 | tf_op jit(solution)/shard_map/all_to_all | solution.py:214
  75.4 0.3 coefficient_kernel.1.coef
  75.8 1.1 collective-permute-done.1.right
  76.8 0.0 collective-permute-done.left
  76.8 5.3 %sweep_kernel.1.solved = f32[16,2,4,8,128]{4,3,2,1,0:T(8,128)S(1)} custom-call(f32[11,2,4,8,128]{4,3,2,1,0:T(8,128)S(1)} %collective-permute-done.left, f32[16,2,4,8,128]{4,3,2,1,0:T(8,128)S(1)} %planes_to_rows_kernel.1.own, f32[11,2,4,8,128]{4,3,2,1,0:T(8,128)S(1)} %collective-permute-done.1.right, f32[40,2,4,8,128]{4,3,2,1,0:T(8,128)S(1)} %coefficient_kernel.1.coef), custom_call_target="tpu_custom_call" | custom-call | tf_op jit(solution)/shard_map/sweep_kernel/pallas_call | solution.py:202
  82.2 0.1 rows_to_planes_kernel.1
  82.3 29.4 %all_to_all.26.solved = f32[32,2,2,8,128]{4,3,2,1,0:T(8,128)S(1)} all-to-all(f32[32,2,2,8,128]{4,3,2,1,0:T(8,128)S(1)} %bitcast.141), channel_id=1, replica_groups=mesh['x'=4,'zl'=2,'core'=2,'zh'=4,'y'=4] {'zh','y','core'}, dimensions={0} | all-to-all | bytes 1048576 | tf_op jit(solution)/shard_map/all_to_all | solution.py:236
  111.7 0.2 backward_kernel.1
  111.9 11.4 %all_to_all.27 = f32[16,2,2,2,8,128]{5,4,3,2,1,0:T(8,128)S(1)} all-to-all(f32[16,2,2,2,8,128]{5,4,3,2,1,0:T(8,128)S(1)} %backward_kernel.1), channel_id=1, replica_groups=mesh['x'=4,'zl'=2,'core'=2,'zh'=4,'y'=4] {'x','zl','core'}, dimensions={0} | all-to-all | bytes 1048576 | tf_op jit(solution)/shard_map/all_to_all | solution.py:240
  123.5 0.8 copy_bitcast_fusion
  (31 shorter events, 0.2 us)
Async XLA Ops:
  0.6 2.3 %copy-start = (f32[2,2,128,128]{3,2,1,0:T(8,128)S(1)}, f32[2,2,128,128]{3,2,1,0:T(8,128)}, u32[]{:S(2)}) copy-start(f32[2,2,128,128]{3,2,1,0:T(8,128)} %param.4) | copy-start | bytes 786436
  0.6 2.3 %copy-start.1 = (f32[2,2,128,128]{3,2,1,0:T(8,128)S(1)}, f32[2,2,128,128]{3,2,1,0:T(8,128)}, u32[]{:S(2)}) copy-start(f32[2,2,128,128]{3,2,1,0:T(8,128)} %param.3) | copy-start | bytes 786436
  19.7 12.6 %copy-start.2 = (f32[2,128,128]{2,1,0:T(8,128)S(1)}, f32[2,128,128]{2,1,0:T(8,128)}, u32[]{:S(2)}) copy-start(f32[2,128,128]{2,1,0:T(8,128)} %param.5) | copy-start | bytes 393220
  20.7 30.1 %all-to-all-start.1 = ((f32[32,2,2,8,128]{4,3,2,1,0:T(8,128)}), f32[32,2,2,8,128]{4,3,2,1,0:T(8,128)S(1)}, u32[]{:S(2)}, u32[]{:S(2)}) async-start(f32[32,2,2,8,128]{4,3,2,1,0:T(8,128)} %forward_kernel.1), calls=%async_computation.1 | async-start | bytes 1048576 | tf_op jit(solution)/shard_map/all_to_all | solution.py:223
  51.7 23.7 %all-to-all-start.2 = ((f32[16,2,40,128]{3,2,1,0:T(8,128)}), f32[16,2,40,128]{3,2,1,0:T(8,128)S(1)}, u32[]{:S(2)}, u32[]{:S(2)}) async-start(f32[16,2,40,128]{3,2,1,0:T(8,128)} %broadcast_in_dim.3), calls=%async_computation.2 | async-start | bytes 1310720 | tf_op jit(solution)/shard_map/all_to_all | solution.py:214
  55.6 21.3 %collective-permute-start.1 = (f32[11,2,4,8,128]{4,3,2,1,0:T(8,128)S(1)}, f32[11,2,4,8,128]{4,3,2,1,0:T(8,128)S(1)}, u32[]{:S(2)}, u32[]{:S(2)}) collective-permute-start(f32[11,2,4,8,128]{4,3,2,1,0:T(8,128)S(1)} %get-tuple-element.4), channel_id=1, source_target_pairs={{32,0},{96,32},{64,96},{128,64},{160,128},{224,160},{192,224},{48,... | collective-permute-start | bytes 1081352 | tf_op jit(solution)/shard_map/ppermute | solution.py:230
  56.9 20.0 %collective-permute-start = (f32[11,2,4,8,128]{4,3,2,1,0:T(8,128)S(1)}, f32[11,2,4,8,128]{4,3,2,1,0:T(8,128)S(1)}, u32[]{:S(2)}, u32[]{:S(2)}) collective-permute-start(f32[11,2,4,8,128]{4,3,2,1,0:T(8,128)S(1)} %get-tuple-element.5), channel_id=1, source_target_pairs={{0,32},{32,96},{96,64},{64,128},{128,160},{160,224},{224,192},{16,... | collective-permute-start | bytes 1081352 | tf_op jit(solution)/shard_map/ppermute | solution.py:229

commit v3 on v2

--- a/solution.py
+++ b/solution.py
@@ -7,6 +7,7 @@
 from jax.experimental.pallas import tpu as pltpu
 from jax.sharding import Mesh
 from jax.sharding import PartitionSpec as P
+
 
 STEPS = 32
 SWEEPS = 12
@@ -81,6 +82,28 @@
     return math.exp(math.log(ALPHA) * n / STEPS)
 
 
+def copy_all(pairs, sems):
+    copies = [pltpu.make_async_copy(a, b, sems.at[n]) for n, (a, b) in enumerate(pairs)]
+    for copy in copies:
+        copy.start()
+    for copy in copies:
+        copy.wait()
+
+
+def block_of(field, i):
+    return field.at[:, :, ROWS * PLACE[i] : ROWS * PLACE[i] + ROWS, :]
+
+
+def pack_kernel(state, adjoint, out, sems):
+    fields = (state, adjoint)
+    copy_all([(block_of(fields[f], i), out.at[i, f]) for i in range(16) for f in range(2)], sems)
+
+
+def unpack_kernel(blocks, state, adjoint, sems):
+    fields = (state, adjoint)
+    copy_all([(blocks.at[i, f], block_of(fields[f], i)) for i in range(16) for f in range(2)], sems)
+
+
 def forward_kernel(times, out):
     for z in range(2):
         values = [
@@ -122,20 +145,40 @@
                 out[:, j // 2, half, c, j % 2] = jnp.swapaxes(tiles, 0, 1)
 
 
-def coefficient_kernel(reaction, coef):
-    rate = math.exp(math.log(ALPHA) / STEPS)
-    freq = my_freq()
-    cos, sin = jnp.float32(1.0), jnp.float32(0.0)
+def table_of(freq, function):
+    value = jnp.float32(function(0.0))
     for k in range(1, STEPS):
-        cos = jnp.where(freq == k, jnp.float32(math.cos(2.0 * math.pi * k / STEPS)), cos)
-        sin = jnp.where(freq == k, jnp.float32(math.sin(2.0 * math.pi * k / STEPS)), sin)
-    shift_re = 1.0 - rate * cos + 6.0 * MU
-    d_im = BETA + rate * sin
+        value = jnp.where(freq == k, jnp.float32(function(2.0 * math.pi * k / STEPS)), value)
+    return value
+
+
+RATE = math.exp(math.log(ALPHA) / STEPS)
+
+
+def real_kernel(out):
+    value = 1.0 - RATE * table_of(my_freq(), math.cos) + 6.0 * MU
+    out[...] = jnp.zeros((8, 128), jnp.float32) + value
+
+
+def imaginary_kernel(out):
+    value = BETA + RATE * table_of(my_freq(), math.sin)
+    out[...] = jnp.zeros((8, 128), jnp.float32) + value
+
+
+def coefficient_kernel(mine, other, real, imaginary, coef):
+    core, zh, y = lax.axis_index("core"), lax.axis_index("zh"), lax.axis_index("y")
+    shift_re, d_im = real[...], imaginary[...]
     start = my_place() * BLOCK - HALO
     for j in range(4):
         for first in range(0, PADDED, ROWS):
-            tiles = reaction[:, j // 2, j % 2, first : first + ROWS]
-            d_re = MU * jnp.swapaxes(tiles, 0, 1) + shift_re
+            at = slice(first, first + ROWS)
+            tiles = []
+            for slab in range(8):
+                pair = 2 * slab + j // 2
+                back_zh, back_y = (zh + 4 - pair // 4) % 4, (y + 4 - pair % 4) % 4
+                a, b = mine[back_y, back_zh, at], other[back_y, back_zh, at]
+                tiles.append(jnp.where(core == j % 2, a, b))
+            d_re = MU * jnp.swapaxes(jnp.stack(tiles), 0, 1) + shift_re
             row = start + first + lax.broadcasted_iota(jnp.int32, (ROWS, 8, 128), 0)
             inside = jnp.logical_and(row >= 0, row < 16 * ROWS)
             scale = jnp.where(inside, 1.0, 0.0) / (d_re * d_re + d_im * d_im)
@@ -203,24 +246,42 @@
         kernel,
         out_shape=pltpu.VMEM(shape, jnp.float32),
         scratch_shapes=scratch,
-        name=kernel.__name__,
         compiler_params=pltpu.CompilerParams(vmem_limit_bytes=VMEM),
     )(*[pltpu.with_memory_space_constraint(a, pltpu.VMEM) for a in args])
 
 
-def body(state_rhs, adjoint_rhs, reaction):
+def near_reaction(reaction):
     near = jnp.pad(reaction, ((0, 0), (HALO, PADDED - BLOCK - HALO), (0, 0)))
-    near = lax.dynamic_slice_in_dim(near, my_place() * BLOCK, PADDED, axis=1)
-    near = lax.all_to_all(jnp.broadcast_to(near, (16,) + near.shape), SPACE, 0, 0, tiled=True)
-    coef = call(
-        coefficient_kernel, (PADDED, 2, 4, 8, 128), near.reshape(8, 2, 2, PADDED, 128)
-    )
-
-    both = jnp.stack((state_rhs, adjoint_rhs)).reshape(2, 2, 2, 16, ROWS, 128)
-    both = jnp.stack([both[:, :, :, p] for p in PLACE])
-    times = lax.all_to_all(both, TM, 0, 0, tiled=True)
+    first = (lax.axis_index("core"), my_place() * BLOCK, 0)
+    return lax.dynamic_slice(near, first, (1, PADDED, 128))[0]
+
+
+def gathered(x, axis):
+    others = [lax.ppermute(x, axis, [(i, (i + d) % 4) for i in range(4)]) for d in (1, 2, 3)]
+    return jnp.stack([x] + others)
+
+
+def exchange(x, axes):
+    return lax.all_to_all(x, axes, 0, 0, tiled=True)
+
+
+def stages(state_rhs, adjoint_rhs, reaction):
+    sems = pltpu.SemaphoreType.DMA((32,))
+    both = pl.pallas_call(
+        pack_kernel,
+        in_specs=[pl.BlockSpec(memory_space=pltpu.HBM)] * 2,
+        out_shape=pltpu.VMEM((16, 2, 2, 2, ROWS, 128), jnp.float32),
+        scratch_shapes=[sems],
+        compiler_params=pltpu.CompilerParams(vmem_limit_bytes=VMEM),
+        name="pack_kernel",
+    )(*[pltpu.with_memory_space_constraint(a, pltpu.HBM) for a in (state_rhs, adjoint_rhs)])
+    times = exchange(both, TM)
+    mine = gathered(gathered(near_reaction(reaction), "zh"), "y")
+    other = lax.ppermute(mine, "core", [(0, 1), (1, 0)])
+    real, imaginary = call(real_kernel, (8, 128)), call(imaginary_kernel, (8, 128))
+    coef = call(coefficient_kernel, (PADDED, 2, 4, 8, 128), mine, other, real, imaginary)
     hat = call(forward_kernel, (STEPS, 2, 2, ROWS, 128), times)
-    got = lax.all_to_all(hat, FREQ, 0, 0, tiled=True)
+    got = exchange(hat, FREQ)
     own = call(
         planes_to_rows_kernel, (BLOCK, 2, 4, 8, 128), got.reshape(8, 2, 2, 2, 2, ROWS, 128)
     )
@@ -233,20 +294,24 @@
         sweep_kernel, (BLOCK, 2, 4, 8, 128), left, own, right, coef, scratch=[window] * 3
     )
     solved = call(rows_to_planes_kernel, (8, 2, 2, 2, 2, ROWS, 128), solved)
-    by_freq = lax.all_to_all(
-        solved.reshape(STEPS, 2, 2, ROWS, 128), FREQ, 0, 0, tiled=True
-    )
+    by_freq = exchange(solved.reshape(STEPS, 2, 2, ROWS, 128), FREQ)
     by_time = call(backward_kernel, (16, 2, 2, 2, ROWS, 128), by_freq)
-    final = lax.all_to_all(by_time, TM, 0, 0, tiled=True)
-    final = jnp.stack([final[HOLDER[p]] for p in range(16)], axis=3).reshape(2, 2, 2, 128, 128)
-    return final[0], final[1]
+    final = exchange(by_time, TM)
+    return pl.pallas_call(
+        unpack_kernel,
+        out_specs=[pl.BlockSpec(memory_space=pltpu.HBM)] * 2,
+        out_shape=[jax.ShapeDtypeStruct(state_rhs.shape, jnp.float32)] * 2,
+        scratch_shapes=[sems],
+        compiler_params=pltpu.CompilerParams(vmem_limit_bytes=VMEM),
+        name="unpack_kernel",
+    )(pltpu.with_memory_space_constraint(final, pltpu.VMEM))
 
 
 def solution(mesh):
     split = Mesh(mesh.devices.reshape(4, 2, 2, 4, 4), TM + SPACE)
     field = P(TM, SPACE, None, None)
     return jax.shard_map(
-        body,
+        stages,
         mesh=split,
         in_specs=(field, field, P(SPACE, None, None)),
         out_specs=(field, field),

time: 125 us -> 111 us (0.89)
  waiting for transfers between devices: 34.1 us -> 11.8 us
  starting transfers between devices: 20.6 us -> 33.5 us
  Pallas kernels: 7.01 us -> 9.38 us
  other arithmetic: 2.36 us -> 0.04 us
  blocking collectives: 57.4 us -> 55.1 us
  local copies, waits for them, and re-layouts: 1.95 us -> 0.11 us
    all_to_all x2 -> x1, waiting for transfers between devices: 33 us -> 0.01 us  [exchange(): return lax.all_to_all(x, axes, 0, 0, tiled=True)]
    ppermute x2 -> x9, starting transfers between devices: 5.3 us -> 21.8 us  [the longest x6 13.9 us: gathered(): lax.ppermute(x, axis, [(i, (i + d) % 4) for i in range(4)])]
    ppermute x2 -> x9, waiting for transfers between devices: 1.09 us -> 11.8 us  [the longest x6 9.45 us: gathered(): lax.ppermute(x, axis, [(i, (i + d) % 4) for i in range(4)])]
    all_to_all x2 -> x1, starting transfers between devices: 15.3 us -> 11.6 us  [exchange(): return lax.all_to_all(x, axes, 0, 0, tiled=True)]
    unnamed x15 -> x0, other arithmetic: 2.35 us -> none
    pallas_call x0 -> x2, Pallas kernels: none -> 2.34 us  [the longest x1 1.28 us: stages(): pl.pallas_call(pack_kernel, in_specs=[pl.BlockSpec(memory_space=pltpu.HBM...]
    all_to_all x3, blocking collectives: 57.4 us -> 55.1 us  [exchange(): return lax.all_to_all(x, axes, 0, 0, tiled=True)]
    pallas_call x6 -> x8, Pallas kernels: 7.01 us -> 7.05 us  [call(): pl.pallas_call(kernel, out_shape=pltpu.VMEM(shape, jnp.float32), scratch_...]
  transfers between devices with their start and end apart: 4 -> 10, of which waited for: 3 -> 5; matrix products, arithmetic and copies ran while one was open for 0% -> 0% of each run, Pallas kernels for 0% -> 0%
where the time goes in v3:
time: 111 us
  blocking collectives  55.1 us (50%)
  starting transfers between devices  33.5 us (30%)
  waiting for transfers between devices  11.8 us (11%)
  Pallas kernels  9.38 us (8%)
    all_to_all x3, blocking collectives, exchange(): return lax.all_to_all(x, axes, 0, 0, tiled=True)  55.1 us
    ppermute x6, starting transfers between devices, gathered(): lax.ppermute(x, axis, [(i, (i + d) % 4) for i in range(4)])  13.9 us
    all_to_all x1, starting transfers between devices, exchange(): return lax.all_to_all(x, axes, 0, 0, tiled=True)  11.6 us
    ppermute x6, waiting for transfers between devices, gathered(): lax.ppermute(x, axis, [(i, (i + d) % 4) for i in range(4)])  9.45 us
    pallas_call x8, Pallas kernels, call(): pl.pallas_call(kernel, out_shape=pltpu.VMEM(shape, jnp.float32), scratch_...  7.05 us
    ppermute x1, starting transfers between devices, stages(): left = lax.ppermute(own[BLOCK - HALO:], TM, ahead)  4.01 us
    ppermute x1, starting transfers between devices, stages(): other = lax.ppermute(mine, 'core', [(0, 1), (1, 0)])  2.65 us
  transfers between devices with their start and end apart: 10, of which 5 were waited for; matrix products, arithmetic and copies ran while one was open for 0% of the time, Pallas kernels for 0%

profile of v3, /device:TPU:1, one launch (start us, length us, event | category | flops | bytes accessed | tf_op | source)
XLA Modules:
  0.0 110.7 jit_solution(1789547446250833257)
XLA Ops:
  0.6 1.3 %pack_kernel.1 = f32[16,2,2,2,8,128]{5,4,3,2,1,0:T(8,128)S(1)} custom-call(f32[2,2,128,128]{3,2,1,0:T(8,128)} %state.1, f32[2,2,128,128]{3,2,1,0:T(8,128)} %adjoint.1), custom_call_target="tpu_custom_call" | custom-call | tf_op jit(solution)/shard_map/pack_kernel/pallas_call | solution.py:270
  1.9 16.6 %all_to_all.20.times = f32[16,2,2,2,8,128]{5,4,3,2,1,0:T(8,128)S(1)} all-to-all(f32[16,2,2,2,8,128]{5,4,3,2,1,0:T(8,128)S(1)} %pack_kernel.1), channel_id=1, replica_groups=mesh['x'=4,'zl'=2,'core'=2,'zh'=4,'y'=4] {'x','zl','core'}, dimensions={0} | all-to-all | bytes 1048576 | tf_op jit(solution)/shard_map/all_to_all | solution.py:265
  18.5 1.0 shard_map.50
  19.5 11.6 %all-to-all-start.1 = ((f32[32,2,2,8,128]{4,3,2,1,0:T(8,128)}), f32[32,2,2,8,128]{4,3,2,1,0:T(8,128)S(1)}, u32[]{:S(2)}, u32[]{:S(2)}) async-start(f32[32,2,2,8,128]{4,3,2,1,0:T(8,128)} %shard_map.50), calls=%async_computation.1 | async-start | bytes 1048576 | tf_op jit(solution)/shard_map/all_to_all | solution.py:265
  31.2 3.6 %collective-permute-start.4 = (f32[40,128]{1,0:T(8,128)S(1)}, f32[40,128]{1,0:T(8,128)S(1)}, u32[]{:S(2)}, u32[]{:S(2)}) collective-permute-start(f32[40,128]{1,0:T(8,128)S(1)} %fusion.2), channel_id=1, source_target_pairs={{0,12},{4,0},{8,4},{12,8},{1,13},{5,1},{9,5},{13,9},{2,14},{6,2},{... | collective-permute-start | bytes 61448 | tf_op jit(solution)/shard_map/ppermute | solution.py:260
  34.8 2.0 %collective-permute-start.3 = (f32[40,128]{1,0:T(8,128)S(1)}, f32[40,128]{1,0:T(8,128)S(1)}, u32[]{:S(2)}, u32[]{:S(2)}) collective-permute-start(f32[40,128]{1,0:T(8,128)S(1)} %fusion.2), channel_id=1, source_target_pairs={{0,8},{4,12},{8,0},{12,4},{1,9},{5,13},{9,1},{13,5},{2,10},{6,14},... | collective-permute-start | bytes 61448 | tf_op jit(solution)/shard_map/ppermute | solution.py:260
  36.8 2.1 %collective-permute-start.2 = (f32[40,128]{1,0:T(8,128)S(1)}, f32[40,128]{1,0:T(8,128)S(1)}, u32[]{:S(2)}, u32[]{:S(2)}) collective-permute-start(f32[40,128]{1,0:T(8,128)S(1)} %fusion.2), channel_id=1, source_target_pairs={{0,4},{4,8},{8,12},{12,0},{1,5},{5,9},{9,13},{13,1},{2,6},{6,10},{... | collective-permute-start | bytes 61448 | tf_op jit(solution)/shard_map/ppermute | solution.py:260
  38.9 7.7 %collective-permute-done.4 = f32[40,128]{1,0:T(8,128)S(1)} collective-permute-done((f32[40,128]{1,0:T(8,128)S(1)}, f32[40,128]{1,0:T(8,128)S(1)}, u32[]{:S(2)}, u32[]{:S(2)}) %collective-permute-start.4) | collective-permute-done | bytes 20512 | tf_op jit(solution)/shard_map/ppermute | solution.py:260
  46.6 1.8 %collective-permute-done.3 = f32[40,128]{1,0:T(8,128)S(1)} collective-permute-done((f32[40,128]{1,0:T(8,128)S(1)}, f32[40,128]{1,0:T(8,128)S(1)}, u32[]{:S(2)}, u32[]{:S(2)}) %collective-permute-start.3) | collective-permute-done | bytes 20512 | tf_op jit(solution)/shard_map/ppermute | solution.py:260
  48.4 0.0 collective-permute-done.2
  48.4 3.5 %collective-permute-start.6 = (f32[4,40,128]{2,1,0:T(8,128)S(1)}, f32[4,40,128]{2,1,0:T(8,128)S(1)}, u32[]{:S(2)}, u32[]{:S(2)}) collective-permute-start(f32[4,40,128]{2,1,0:T(8,128)S(1)} %get-tuple-element.5), channel_id=1, source_target_pairs={{0,2},{1,3},{2,0},{3,1},{4,6},{5,7},{6,4},{7,5},{8,10},{9,11},{10,... | collective-permute-start | bytes 245768 | tf_op jit(solution)/shard_map/ppermute | solution.py:260
  51.9 0.3 collective-permute-start.5
  52.2 2.4 %collective-permute-start.7 = (f32[4,40,128]{2,1,0:T(8,128)S(1)}, f32[4,40,128]{2,1,0:T(8,128)S(1)}, u32[]{:S(2)}, u32[]{:S(2)}) collective-permute-start(f32[4,40,128]{2,1,0:T(8,128)S(1)} %get-tuple-element.5), channel_id=1, source_target_pairs={{0,3},{1,0},{2,1},{3,2},{4,7},{5,4},{6,5},{7,6},{8,11},{9,8},{10,9... | collective-permute-start | bytes 245768 | tf_op jit(solution)/shard_map/ppermute | solution.py:260
  54.6 0.0 all-to-all-done.1
  54.6 0.1 shard_map.51.own
  54.7 0.1 fusion.1
  54.8 1.3 %collective-permute-start.1 = (f32[11,2,4,8,128]{4,3,2,1,0:T(8,128)S(1)}, f32[11,2,4,8,128]{4,3,2,1,0:T(8,128)S(1)}, u32[]{:S(2)}, u32[]{:S(2)}) collective-permute-start(f32[11,2,4,8,128]{4,3,2,1,0:T(8,128)S(1)} %get-tuple-element.2), channel_id=1, source_target_pairs={{32,0},{96,32},{64,96},{128,64},{160,128},{224,160},{192,224},{48,... | collective-permute-start | bytes 1081352 | tf_op jit(solution)/shard_map/ppermute | solution.py:291
  56.1 4.0 %collective-permute-start = (f32[11,2,4,8,128]{4,3,2,1,0:T(8,128)S(1)}, f32[11,2,4,8,128]{4,3,2,1,0:T(8,128)S(1)}, u32[]{:S(2)}, u32[]{:S(2)}) collective-permute-start(f32[11,2,4,8,128]{4,3,2,1,0:T(8,128)S(1)} %get-tuple-element.3), channel_id=1, source_target_pairs={{0,32},{32,96},{96,64},{64,128},{128,160},{160,224},{224,192},{16,... | collective-permute-start | bytes 1081352 | tf_op jit(solution)/shard_map/ppermute | solution.py:290
  60.1 0.0 collective-permute-done.6
  60.1 0.0 collective-permute-done.5
  60.1 0.0 collective-permute-done.7
  60.1 2.7 %collective-permute-start.8 = (f32[4,4,40,128]{3,2,1,0:T(8,128)S(1)}, f32[4,4,40,128]{3,2,1,0:T(8,128)S(1)}, u32[]{:S(2)}, u32[]{:S(2)}) collective-permute-start(f32[4,4,40,128]{3,2,1,0:T(8,128)S(1)} %pad_maximum_fusion.mine), channel_id=1, source_target_pairs={{0,16},{16,0},{1,17},{17,1},{2,18},{18,2},{3,19},{19,3},{4,20},{20... | collective-permute-start | bytes 983048 | tf_op jit(solution)/shard_map/ppermute | solution.py:280
  62.8 1.3 %collective-permute-done.8.other = f32[4,4,40,128]{3,2,1,0:T(8,128)S(1)} collective-permute-done((f32[4,4,40,128]{3,2,1,0:T(8,128)S(1)}, f32[4,4,40,128]{3,2,1,0:T(8,128)S(1)}, u32[]{:S(2)}, u32[]{:S(2)}) %collective-permute-start.8) | collective-permute-done | bytes 327712 | tf_op jit(solution)/shard_map/ppermute | solution.py:280
  64.0 0.3 shard_map.54.coef
  64.4 0.2 collective-permute-done.1.right
  64.6 0.9 collective-permute-done.left
  65.5 5.3 %shard_map.55.solved = f32[16,2,4,8,128]{4,3,2,1,0:T(8,128)S(1)} custom-call(f32[11,2,4,8,128]{4,3,2,1,0:T(8,128)S(1)} %collective-permute-done.left, f32[16,2,4,8,128]{4,3,2,1,0:T(8,128)S(1)} %shard_map.51.own, f32[11,2,4,8,128]{4,3,2,1,0:T(8,128)S(1)} %collective-permute-done.1.right, f32[40,2,4,8,128]{4,3,2,1,0:T(8,128)S(1)} %shard_map.54.coef), custom_call_target="tpu_custom_call" | custom-call | tf_op jit(solution)/shard_map/pallas_call | solution.py:245
  70.8 0.1 shard_map.56
  71.0 23.2 %all_to_all.21.solved = f32[32,2,2,8,128]{4,3,2,1,0:T(8,128)S(1)} all-to-all(f32[32,2,2,8,128]{4,3,2,1,0:T(8,128)S(1)} %bitcast.13), channel_id=1, replica_groups=mesh['x'=4,'zl'=2,'core'=2,'zh'=4,'y'=4] {'zh','y','core'}, dimensions={0} | all-to-all | bytes 1048576 | tf_op jit(solution)/shard_map/all_to_all | solution.py:265
  94.2 0.2 shard_map.57
  94.4 15.2 %all_to_all.22.blocks = f32[16,2,2,2,8,128]{5,4,3,2,1,0:T(8,128)S(1)} all-to-all(f32[16,2,2,2,8,128]{5,4,3,2,1,0:T(8,128)S(1)} %shard_map.57), channel_id=1, replica_groups=mesh['x'=4,'zl'=2,'core'=2,'zh'=4,'y'=4] {'x','zl','core'}, dimensions={0} | all-to-all | bytes 1048576 | tf_op jit(solution)/shard_map/all_to_all | solution.py:265
  109.6 1.1 unpack_kernel.1
  (8 shorter events, 0.1 us)
Async XLA Ops:
  18.5 12.6 %copy-start = (f32[2,128,128]{2,1,0:T(8,128)S(1)}, f32[2,128,128]{2,1,0:T(8,128)}, u32[]{:S(2)}) copy-start(f32[2,128,128]{2,1,0:T(8,128)} %param.5) | copy-start | bytes 393220
  19.5 35.1 %all-to-all-start.1 = ((f32[32,2,2,8,128]{4,3,2,1,0:T(8,128)}), f32[32,2,2,8,128]{4,3,2,1,0:T(8,128)S(1)}, u32[]{:S(2)}, u32[]{:S(2)}) async-start(f32[32,2,2,8,128]{4,3,2,1,0:T(8,128)} %shard_map.50), calls=%async_computation.1 | async-start | bytes 1048576 | tf_op jit(solution)/shard_map/all_to_all | solution.py:265
  31.2 15.4 %collective-permute-start.4 = (f32[40,128]{1,0:T(8,128)S(1)}, f32[40,128]{1,0:T(8,128)S(1)}, u32[]{:S(2)}, u32[]{:S(2)}) collective-permute-start(f32[40,128]{1,0:T(8,128)S(1)} %fusion.2), channel_id=1, source_target_pairs={{0,12},{4,0},{8,4},{12,8},{1,13},{5,1},{9,5},{13,9},{2,14},{6,2},{... | collective-permute-start | bytes 61448 | tf_op jit(solution)/shard_map/ppermute | solution.py:260
  34.8 13.6 %collective-permute-start.3 = (f32[40,128]{1,0:T(8,128)S(1)}, f32[40,128]{1,0:T(8,128)S(1)}, u32[]{:S(2)}, u32[]{:S(2)}) collective-permute-start(f32[40,128]{1,0:T(8,128)S(1)} %fusion.2), channel_id=1, source_target_pairs={{0,8},{4,12},{8,0},{12,4},{1,9},{5,13},{9,1},{13,5},{2,10},{6,14},... | collective-permute-start | bytes 61448 | tf_op jit(solution)/shard_map/ppermute | solution.py:260
  36.8 11.5 %collective-permute-start.2 = (f32[40,128]{1,0:T(8,128)S(1)}, f32[40,128]{1,0:T(8,128)S(1)}, u32[]{:S(2)}, u32[]{:S(2)}) collective-permute-start(f32[40,128]{1,0:T(8,128)S(1)} %fusion.2), channel_id=1, source_target_pairs={{0,4},{4,8},{8,12},{12,0},{1,5},{5,9},{9,13},{13,1},{2,6},{6,10},{... | collective-permute-start | bytes 61448 | tf_op jit(solution)/shard_map/ppermute | solution.py:260
  48.4 11.7 %collective-permute-start.6 = (f32[4,40,128]{2,1,0:T(8,128)S(1)}, f32[4,40,128]{2,1,0:T(8,128)S(1)}, u32[]{:S(2)}, u32[]{:S(2)}) collective-permute-start(f32[4,40,128]{2,1,0:T(8,128)S(1)} %get-tuple-element.5), channel_id=1, source_target_pairs={{0,2},{1,3},{2,0},{3,1},{4,6},{5,7},{6,4},{7,5},{8,10},{9,11},{10,... | collective-permute-start | bytes 245768 | tf_op jit(solution)/shard_map/ppermute | solution.py:260
  51.9 8.2 %collective-permute-start.5 = (f32[4,40,128]{2,1,0:T(8,128)S(1)}, f32[4,40,128]{2,1,0:T(8,128)S(1)}, u32[]{:S(2)}, u32[]{:S(2)}) collective-permute-start(f32[4,40,128]{2,1,0:T(8,128)S(1)} %get-tuple-element.5), channel_id=1, source_target_pairs={{0,1},{1,2},{2,3},{3,0},{4,5},{5,6},{6,7},{7,4},{8,9},{9,10},{10,1... | collective-permute-start | bytes 245768 | tf_op jit(solution)/shard_map/ppermute | solution.py:260
  52.2 7.9 %collective-permute-start.7 = (f32[4,40,128]{2,1,0:T(8,128)S(1)}, f32[4,40,128]{2,1,0:T(8,128)S(1)}, u32[]{:S(2)}, u32[]{:S(2)}) collective-permute-start(f32[4,40,128]{2,1,0:T(8,128)S(1)} %get-tuple-element.5), channel_id=1, source_target_pairs={{0,3},{1,0},{2,1},{3,2},{4,7},{5,4},{6,5},{7,6},{8,11},{9,8},{10,9... | collective-permute-start | bytes 245768 | tf_op jit(solution)/shard_map/ppermute | solution.py:260
  54.8 9.9 %collective-permute-start.1 = (f32[11,2,4,8,128]{4,3,2,1,0:T(8,128)S(1)}, f32[11,2,4,8,128]{4,3,2,1,0:T(8,128)S(1)}, u32[]{:S(2)}, u32[]{:S(2)}) collective-permute-start(f32[11,2,4,8,128]{4,3,2,1,0:T(8,128)S(1)} %get-tuple-element.2), channel_id=1, source_target_pairs={{32,0},{96,32},{64,96},{128,64},{160,128},{224,160},{192,224},{48,... | collective-permute-start | bytes 1081352 | tf_op jit(solution)/shard_map/ppermute | solution.py:291
  56.1 9.5 %collective-permute-start = (f32[11,2,4,8,128]{4,3,2,1,0:T(8,128)S(1)}, f32[11,2,4,8,128]{4,3,2,1,0:T(8,128)S(1)}, u32[]{:S(2)}, u32[]{:S(2)}) collective-permute-start(f32[11,2,4,8,128]{4,3,2,1,0:T(8,128)S(1)} %get-tuple-element.3), channel_id=1, source_target_pairs={{0,32},{32,96},{96,64},{64,128},{128,160},{160,224},{224,192},{16,... | collective-permute-start | bytes 1081352 | tf_op jit(solution)/shard_map/ppermute | solution.py:290
  60.1 3.9 %collective-permute-start.8 = (f32[4,4,40,128]{3,2,1,0:T(8,128)S(1)}, f32[4,4,40,128]{3,2,1,0:T(8,128)S(1)}, u32[]{:S(2)}, u32[]{:S(2)}) collective-permute-start(f32[4,4,40,128]{3,2,1,0:T(8,128)S(1)} %pad_maximum_fusion.mine), channel_id=1, source_target_pairs={{0,16},{16,0},{1,17},{17,1},{2,18},{18,2},{3,19},{19,3},{4,20},{20... | collective-permute-start | bytes 983048 | tf_op jit(solution)/shard_map/ppermute | solution.py:280

commit v4 on v3

--- a/solution.py
+++ b/solution.py
@@ -17,30 +17,38 @@
 
 TM = ("x", "zl", "core")
 SPACE = ("zh", "y")
-FREQ = ("zh", "y", "core")
+TIME = ("core", "x", "zl")
+FREQ = ("zl", "y", "zh")
 
 HALO = SWEEPS - 1
 ROWS = 8
 BLOCK = 2 * ROWS
 WINDOW = BLOCK + 2 * HALO
 PADDED = 40
+NEAR = PADDED + BLOCK
 VMEM = 12 << 20
 
 
-def place_of(ix, zl):
-    return 2 * ix + (zl + ix) % 2
-
-
-PLACE = [2 * place_of(i // 4, (i // 2) % 2) + i % 2 for i in range(16)]
-HOLDER = [PLACE.index(p) for p in range(16)]
+def place_of(ix, core):
+    return 2 * ix + (core + ix) % 2
+
+
+def device_of(place, zl):
+    ix = place // 2
+    return 4 * ix + 2 * zl + (place + ix) % 2
+
+
+TIME_TO_TM = [4 * ((e // 2) % 4) + 2 * (e % 2) + e // 8 for e in range(16)]
+TM_TO_TIME = [TIME_TO_TM.index(i) for i in range(16)]
+PLACE = [2 * place_of((e // 2) % 4, e // 8) + e % 2 for e in range(16)]
 
 
 def my_place():
-    return place_of(lax.axis_index("x"), lax.axis_index("zl"))
+    return place_of(lax.axis_index("x"), lax.axis_index("core"))
 
 
 def my_freq():
-    return lax.axis_index("zh") * 8 + lax.axis_index("y") * 2 + lax.axis_index("core")
+    return lax.axis_index("zl") * 16 + lax.axis_index("y") * 4 + lax.axis_index("zh")
 
 
 def add(a, b):
@@ -105,13 +113,12 @@
 
 
 def forward_kernel(times, out):
+    def time(field, n, z):
+        return times[TM_TO_TIME[n // 2], field, n % 2, z]
+
     for z in range(2):
         values = [
-            (
-                times[n // 2, 0, n % 2, z] * growth(n),
-                times[(31 - n) // 2, 1, (31 - n) % 2, z] * growth(n),
-            )
-            for n in range(STEPS)
+            (time(0, n, z) * growth(n), time(1, 31 - n, z) * growth(n)) for n in range(STEPS)
         ]
         hat = fourier(values, -1)
         for k in range(STEPS):
@@ -125,24 +132,27 @@
         back = fourier(values, 1)
         for n in range(STEPS):
             scale = 1.0 / (growth(n) * STEPS)
-            out[n // 2, 0, n % 2, z] = back[n][0] * scale
-            out[(31 - n) // 2, 1, (31 - n) % 2, z] = back[n][1] * scale
+            out[TM_TO_TIME[n // 2], 0, n % 2, z] = back[n][0] * scale
+            out[TM_TO_TIME[(31 - n) // 2], 1, (31 - n) % 2, z] = back[n][1] * scale
 
 
 def planes_to_rows_kernel(got, out):
     for half in range(2):
         for c in range(2):
             for j in range(4):
-                tiles = got[:, j // 2, half, c, j % 2]
-                out[ROWS * half : ROWS * half + ROWS, c, j] = jnp.swapaxes(tiles, 0, 1)
+                tiles = [got[half, q % 2, j // 2, q // 2, c, j % 2] for q in range(8)]
+                at = slice(ROWS * half, ROWS * half + ROWS)
+                out[at, c, j] = jnp.swapaxes(jnp.stack(tiles), 0, 1)
 
 
 def rows_to_planes_kernel(solved, out):
     for half in range(2):
         for c in range(2):
             for j in range(4):
-                tiles = solved[ROWS * half : ROWS * half + ROWS, c, j]
-                out[:, j // 2, half, c, j % 2] = jnp.swapaxes(tiles, 0, 1)
+                at = slice(ROWS * half, ROWS * half + ROWS)
+                tiles = jnp.swapaxes(solved[at, c, j], 0, 1)
+                for q in range(8):
+                    out[half, q % 2, j // 2, q // 2, c, j % 2] = tiles[q]
 
 
 def table_of(freq, function):
@@ -169,9 +179,10 @@
     core, zh, y = lax.axis_index("core"), lax.axis_index("zh"), lax.axis_index("y")
     shift_re, d_im = real[...], imaginary[...]
     start = my_place() * BLOCK - HALO
+    offset = pl.multiple_of(my_place() % 2 * BLOCK, BLOCK)
     for j in range(4):
         for first in range(0, PADDED, ROWS):
-            at = slice(first, first + ROWS)
+            at = pl.ds(offset + first, ROWS)
             tiles = []
             for slab in range(8):
                 pair = 2 * slab + j // 2
@@ -251,9 +262,9 @@
 
 
 def near_reaction(reaction):
-    near = jnp.pad(reaction, ((0, 0), (HALO, PADDED - BLOCK - HALO), (0, 0)))
-    first = (lax.axis_index("core"), my_place() * BLOCK, 0)
-    return lax.dynamic_slice(near, first, (1, PADDED, 128))[0]
+    near = jnp.pad(reaction, ((0, 0), (HALO, NEAR - 2 * BLOCK - HALO), (0, 0)))
+    first = (lax.axis_index("core"), lax.axis_index("x") * 2 * BLOCK, 0)
+    return lax.dynamic_slice(near, first, (1, NEAR, 128))[0]
 
 
 def gathered(x, axis):
@@ -275,28 +286,26 @@
         compiler_params=pltpu.CompilerParams(vmem_limit_bytes=VMEM),
         name="pack_kernel",
     )(*[pltpu.with_memory_space_constraint(a, pltpu.HBM) for a in (state_rhs, adjoint_rhs)])
-    times = exchange(both, TM)
+    times = exchange(both, TIME)
     mine = gathered(gathered(near_reaction(reaction), "zh"), "y")
     other = lax.ppermute(mine, "core", [(0, 1), (1, 0)])
     real, imaginary = call(real_kernel, (8, 128)), call(imaginary_kernel, (8, 128))
     coef = call(coefficient_kernel, (PADDED, 2, 4, 8, 128), mine, other, real, imaginary)
     hat = call(forward_kernel, (STEPS, 2, 2, ROWS, 128), times)
     got = exchange(hat, FREQ)
-    own = call(
-        planes_to_rows_kernel, (BLOCK, 2, 4, 8, 128), got.reshape(8, 2, 2, 2, 2, ROWS, 128)
-    )
-    chain = [[HOLDER[2 * i + core] for i in range(8)] for core in range(2)]
-    ahead = [(c[i], c[i + 1]) for c in chain for i in range(7)]
+    got = got.reshape(2, 2, 2, 4, 2, 2, ROWS, 128)
+    own = call(planes_to_rows_kernel, (BLOCK, 2, 4, 8, 128), got)
+    ahead = [(device_of(i, zl), device_of(i + 1, zl)) for zl in range(2) for i in range(7)]
     left = lax.ppermute(own[BLOCK - HALO :], TM, ahead)
     right = lax.ppermute(own[:HALO], TM, [(b, a) for a, b in ahead])
     window = pltpu.VMEM((WINDOW, 2, 4, 8, 128), jnp.float32)
     solved = call(
         sweep_kernel, (BLOCK, 2, 4, 8, 128), left, own, right, coef, scratch=[window] * 3
     )
-    solved = call(rows_to_planes_kernel, (8, 2, 2, 2, 2, ROWS, 128), solved)
+    solved = call(rows_to_planes_kernel, (2, 2, 2, 4, 2, 2, ROWS, 128), solved)
     by_freq = exchange(solved.reshape(STEPS, 2, 2, ROWS, 128), FREQ)
     by_time = call(backward_kernel, (16, 2, 2, 2, ROWS, 128), by_freq)
-    final = exchange(by_time, TM)
+    final = exchange(by_time, TIME)
     return pl.pallas_call(
         unpack_kernel,
         out_specs=[pl.BlockSpec(memory_space=pltpu.HBM)] * 2,

time: 111 us -> 111 us (level)
  waiting for transfers between devices: 11.8 us -> 15.7 us
  blocking collectives: 55.1 us -> 51.3 us
    all_to_all x3, blocking collectives: 55.1 us -> 51.3 us  [exchange(): return lax.all_to_all(x, axes, 0, 0, tiled=True)]
    ppermute x6, waiting for transfers between devices: 9.45 us -> 11.8 us  [gathered(): lax.ppermute(x, axis, [(i, (i + d) % 4) for i in range(4)])]
    ppermute x1, starting transfers between devices: 2.65 us -> 4.91 us  [stages(): other = lax.ppermute(mine, 'core', [(0, 1), (1, 0)])]
    ppermute x1, waiting for transfers between devices: 0.22 us -> 2.39 us  [stages(): right = lax.ppermute(own[:HALO], TM, [(b, a) for a, b in ahead])]
    ppermute x6, starting transfers between devices: 13.9 us -> 12.1 us  [gathered(): lax.ppermute(x, axis, [(i, (i + d) % 4) for i in range(4)])]
    ppermute x1, waiting for transfers between devices: 1.25 us -> 0.01 us  [stages(): other = lax.ppermute(mine, 'core', [(0, 1), (1, 0)])]
  transfers between devices with their start and end apart: 10 -> 10, of which waited for: 5 -> 6; matrix products, arithmetic and copies ran while one was open for 0% -> 0% of each run, Pallas kernels for 0% -> 0%
where the time goes in v4:
time: 111 us; the launch traced here: 110 us
  blocking collectives  51.3 us (46%)
  starting transfers between devices  32.9 us (30%)
  waiting for transfers between devices  15.7 us (14%)
  Pallas kernels  9.48 us (9%)
    all_to_all x3, blocking collectives, exchange(): return lax.all_to_all(x, axes, 0, 0, tiled=True)  51.3 us
    ppermute x6, starting transfers between devices, gathered(): lax.ppermute(x, axis, [(i, (i + d) % 4) for i in range(4)])  12.1 us
    ppermute x6, waiting for transfers between devices, gathered(): lax.ppermute(x, axis, [(i, (i + d) % 4) for i in range(4)])  11.8 us
    all_to_all x1, starting transfers between devices, exchange(): return lax.all_to_all(x, axes, 0, 0, tiled=True)  10.6 us
    pallas_call x8, Pallas kernels, call(): pl.pallas_call(kernel, out_shape=pltpu.VMEM(shape, jnp.float32), scratch_...  7.14 us
    ppermute x1, starting transfers between devices, stages(): other = lax.ppermute(mine, 'core', [(0, 1), (1, 0)])  4.91 us
    ppermute x1, starting transfers between devices, stages(): left = lax.ppermute(own[BLOCK - HALO:], TM, ahead)  3.35 us
    ppermute x1, waiting for transfers between devices, stages(): right = lax.ppermute(own[:HALO], TM, [(b, a) for a, b in ahead])  2.39 us
  transfers between devices with their start and end apart: 10, of which 6 were waited for; matrix products, arithmetic and copies ran while one was open for 0% of the time, Pallas kernels for 0%

profile of v4, /device:TPU:1, one launch (start us, length us, event | category | flops | bytes accessed | tf_op | source)
XLA Modules:
  0.0 110.3 jit_solution(10329354394891463139)
XLA Ops:
  0.6 1.3 %pack_kernel.1 = f32[16,2,2,2,8,128]{5,4,3,2,1,0:T(8,128)S(1)} custom-call(f32[2,2,128,128]{3,2,1,0:T(8,128)} %state.1, f32[2,2,128,128]{3,2,1,0:T(8,128)} %adjoint.1), custom_call_target="tpu_custom_call" | custom-call | tf_op jit(solution)/shard_map/pack_kernel/pallas_call | solution.py:281
  1.9 16.2 %all_to_all.20.times = f32[16,2,2,2,8,128]{5,4,3,2,1,0:T(8,128)S(1)} all-to-all(f32[16,2,2,2,8,128]{5,4,3,2,1,0:T(8,128)S(1)} %pack_kernel.1), channel_id=1, replica_groups=mesh['x'=4,'zl'=2,'core'=2,'zh'=4,'y'=4] {'core','x','zl'}, dimensions={0} | all-to-all | bytes 1048576 | tf_op jit(solution)/shard_map/all_to_all | solution.py:276
  18.2 1.0 shard_map.50
  19.1 10.6 %all-to-all-start.1 = ((f32[32,2,2,8,128]{4,3,2,1,0:T(8,128)}), f32[32,2,2,8,128]{4,3,2,1,0:T(8,128)S(1)}, u32[]{:S(2)}, u32[]{:S(2)}) async-start(f32[32,2,2,8,128]{4,3,2,1,0:T(8,128)} %shard_map.50), calls=%async_computation.1 | async-start | bytes 1048576 | tf_op jit(solution)/shard_map/all_to_all | solution.py:276
  29.8 3.4 %collective-permute-start.4 = (f32[56,128]{1,0:T(8,128)S(1)}, f32[56,128]{1,0:T(8,128)S(1)}, u32[]{:S(2)}, u32[]{:S(2)}) collective-permute-start(f32[56,128]{1,0:T(8,128)S(1)} %fusion.2), channel_id=1, source_target_pairs={{0,12},{4,0},{8,4},{12,8},{1,13},{5,1},{9,5},{13,9},{2,14},{6,2},{... | collective-permute-start | bytes 86024 | tf_op jit(solution)/shard_map/ppermute | solution.py:271
  33.2 2.1 %collective-permute-start.3 = (f32[56,128]{1,0:T(8,128)S(1)}, f32[56,128]{1,0:T(8,128)S(1)}, u32[]{:S(2)}, u32[]{:S(2)}) collective-permute-start(f32[56,128]{1,0:T(8,128)S(1)} %fusion.2), channel_id=1, source_target_pairs={{0,8},{4,12},{8,0},{12,4},{1,9},{5,13},{9,1},{13,5},{2,10},{6,14},... | collective-permute-start | bytes 86024 | tf_op jit(solution)/shard_map/ppermute | solution.py:271
  35.3 2.1 %collective-permute-start.2 = (f32[56,128]{1,0:T(8,128)S(1)}, f32[56,128]{1,0:T(8,128)S(1)}, u32[]{:S(2)}, u32[]{:S(2)}) collective-permute-start(f32[56,128]{1,0:T(8,128)S(1)} %fusion.2), channel_id=1, source_target_pairs={{0,4},{4,8},{8,12},{12,0},{1,5},{5,9},{9,13},{13,1},{2,6},{6,10},{... | collective-permute-start | bytes 86024 | tf_op jit(solution)/shard_map/ppermute | solution.py:271
  37.4 5.4 %collective-permute-done.4 = f32[56,128]{1,0:T(8,128)S(1)} collective-permute-done((f32[56,128]{1,0:T(8,128)S(1)}, f32[56,128]{1,0:T(8,128)S(1)}, u32[]{:S(2)}, u32[]{:S(2)}) %collective-permute-start.4) | collective-permute-done | bytes 28704 | tf_op jit(solution)/shard_map/ppermute | solution.py:271
  42.8 4.2 %collective-permute-done.3 = f32[56,128]{1,0:T(8,128)S(1)} collective-permute-done((f32[56,128]{1,0:T(8,128)S(1)}, f32[56,128]{1,0:T(8,128)S(1)}, u32[]{:S(2)}, u32[]{:S(2)}) %collective-permute-start.3) | collective-permute-done | bytes 28704 | tf_op jit(solution)/shard_map/ppermute | solution.py:271
  47.0 0.0 collective-permute-done.2
  47.1 1.8 %collective-permute-start.6 = (f32[4,56,128]{2,1,0:T(8,128)S(1)}, f32[4,56,128]{2,1,0:T(8,128)S(1)}, u32[]{:S(2)}, u32[]{:S(2)}) collective-permute-start(f32[4,56,128]{2,1,0:T(8,128)S(1)} %get-tuple-element.5), channel_id=1, source_target_pairs={{0,2},{1,3},{2,0},{3,1},{4,6},{5,7},{6,4},{7,5},{8,10},{9,11},{10,... | collective-permute-start | bytes 344072 | tf_op jit(solution)/shard_map/ppermute | solution.py:271
  48.9 0.7 collective-permute-start.5
  49.6 1.9 %collective-permute-start.7 = (f32[4,56,128]{2,1,0:T(8,128)S(1)}, f32[4,56,128]{2,1,0:T(8,128)S(1)}, u32[]{:S(2)}, u32[]{:S(2)}) collective-permute-start(f32[4,56,128]{2,1,0:T(8,128)S(1)} %get-tuple-element.5), channel_id=1, source_target_pairs={{0,3},{1,0},{2,1},{3,2},{4,7},{5,4},{6,5},{7,6},{8,11},{9,8},{10,9... | collective-permute-start | bytes 344072 | tf_op jit(solution)/shard_map/ppermute | solution.py:271
  51.6 0.7 collective-permute-done.6
  52.3 1.5 %collective-permute-done.5 = f32[4,56,128]{2,1,0:T(8,128)S(1)} collective-permute-done((f32[4,56,128]{2,1,0:T(8,128)S(1)}, f32[4,56,128]{2,1,0:T(8,128)S(1)}, u32[]{:S(2)}, u32[]{:S(2)}) %collective-permute-start.5) | collective-permute-done | bytes 114720 | tf_op jit(solution)/shard_map/ppermute | solution.py:271
  53.7 0.0 collective-permute-done.7
  53.8 4.9 %collective-permute-start.8 = (f32[4,4,56,128]{3,2,1,0:T(8,128)S(1)}, f32[4,4,56,128]{3,2,1,0:T(8,128)S(1)}, u32[]{:S(2)}, u32[]{:S(2)}) collective-permute-start(f32[4,4,56,128]{3,2,1,0:T(8,128)S(1)} %pad_maximum_fusion.mine), channel_id=1, source_target_pairs={{0,16},{16,0},{1,17},{17,1},{2,18},{18,2},{3,19},{19,3},{4,20},{20... | collective-permute-start | bytes 1376264 | tf_op jit(solution)/shard_map/ppermute | solution.py:291
  58.7 0.0 all-to-all-done.1
  58.7 0.1 shard_map.51.own
  58.8 0.1 fusion.1
  58.9 1.9 %collective-permute-start.1 = (f32[11,2,4,8,128]{4,3,2,1,0:T(8,128)S(1)}, f32[11,2,4,8,128]{4,3,2,1,0:T(8,128)S(1)}, u32[]{:S(2)}, u32[]{:S(2)}) collective-permute-start(f32[11,2,4,8,128]{4,3,2,1,0:T(8,128)S(1)} %get-tuple-element.2), channel_id=1, source_target_pairs={{16,0},{80,16},{64,80},{128,64},{144,128},{208,144},{192,208},{48,... | collective-permute-start | bytes 1081352 | tf_op jit(solution)/shard_map/ppermute | solution.py:300
  60.8 3.3 %collective-permute-start = (f32[11,2,4,8,128]{4,3,2,1,0:T(8,128)S(1)}, f32[11,2,4,8,128]{4,3,2,1,0:T(8,128)S(1)}, u32[]{:S(2)}, u32[]{:S(2)}) collective-permute-start(f32[11,2,4,8,128]{4,3,2,1,0:T(8,128)S(1)} %get-tuple-element.3), channel_id=1, source_target_pairs={{0,16},{16,80},{80,64},{64,128},{128,144},{144,208},{208,192},{32,... | collective-permute-start | bytes 1081352 | tf_op jit(solution)/shard_map/ppermute | solution.py:299
  64.3 0.0 collective-permute-done.8.other
  64.3 0.4 shard_map.54.coef
  64.7 2.4 %collective-permute-done.1.right = f32[11,2,4,8,128]{4,3,2,1,0:T(8,128)S(1)} collective-permute-done((f32[11,2,4,8,128]{4,3,2,1,0:T(8,128)S(1)}, f32[11,2,4,8,128]{4,3,2,1,0:T(8,128)S(1)}, u32[]{:S(2)}, u32[]{:S(2)}) %collective-permute-start.1) | collective-permute-done | bytes 360480 | tf_op jit(solution)/shard_map/ppermute | solution.py:300
  67.1 1.5 %collective-permute-done.left = f32[11,2,4,8,128]{4,3,2,1,0:T(8,128)S(1)} collective-permute-done((f32[11,2,4,8,128]{4,3,2,1,0:T(8,128)S(1)}, f32[11,2,4,8,128]{4,3,2,1,0:T(8,128)S(1)}, u32[]{:S(2)}, u32[]{:S(2)}) %collective-permute-start) | collective-permute-done | bytes 360480 | tf_op jit(solution)/shard_map/ppermute | solution.py:299
  68.5 5.3 %shard_map.55.solved = f32[16,2,4,8,128]{4,3,2,1,0:T(8,128)S(1)} custom-call(f32[11,2,4,8,128]{4,3,2,1,0:T(8,128)S(1)} %collective-permute-done.left, f32[16,2,4,8,128]{4,3,2,1,0:T(8,128)S(1)} %shard_map.51.own, f32[11,2,4,8,128]{4,3,2,1,0:T(8,128)S(1)} %collective-permute-done.1.right, f32[40,2,4,8,128]{4,3,2,1,0:T(8,128)S(1)} %shard_map.54.coef), custom_call_target="tpu_custom_call" | custom-call | tf_op jit(solution)/shard_map/pallas_call | solution.py:256
  73.9 0.1 shard_map.56
  74.0 19.5 %all_to_all.21.solved = f32[32,2,2,8,128]{4,3,2,1,0:T(8,128)S(1)} all-to-all(f32[32,2,2,8,128]{4,3,2,1,0:T(8,128)S(1)} %bitcast.13), channel_id=1, replica_groups=mesh['x'=4,'zl'=2,'core'=2,'zh'=4,'y'=4] {'zl','y','zh'}, dimensions={0} | all-to-all | bytes 1048576 | tf_op jit(solution)/shard_map/all_to_all | solution.py:276
  93.5 0.2 shard_map.57
  93.7 15.5 %all_to_all.22.blocks = f32[16,2,2,2,8,128]{5,4,3,2,1,0:T(8,128)S(1)} all-to-all(f32[16,2,2,2,8,128]{5,4,3,2,1,0:T(8,128)S(1)} %shard_map.57), channel_id=1, replica_groups=mesh['x'=4,'zl'=2,'core'=2,'zh'=4,'y'=4] {'core','x','zl'}, dimensions={0} | all-to-all | bytes 1048576 | tf_op jit(solution)/shard_map/all_to_all | solution.py:276
  109.2 1.1 unpack_kernel.1
  (8 shorter events, 0.2 us)
Async XLA Ops:
  18.2 11.6 %copy-start = (f32[2,128,128]{2,1,0:T(8,128)S(1)}, f32[2,128,128]{2,1,0:T(8,128)}, u32[]{:S(2)}) copy-start(f32[2,128,128]{2,1,0:T(8,128)} %param.5) | copy-start | bytes 393220
  19.1 39.6 %all-to-all-start.1 = ((f32[32,2,2,8,128]{4,3,2,1,0:T(8,128)}), f32[32,2,2,8,128]{4,3,2,1,0:T(8,128)S(1)}, u32[]{:S(2)}, u32[]{:S(2)}) async-start(f32[32,2,2,8,128]{4,3,2,1,0:T(8,128)} %shard_map.50), calls=%async_computation.1 | async-start | bytes 1048576 | tf_op jit(solution)/shard_map/all_to_all | solution.py:276
  29.8 13.0 %collective-permute-start.4 = (f32[56,128]{1,0:T(8,128)S(1)}, f32[56,128]{1,0:T(8,128)S(1)}, u32[]{:S(2)}, u32[]{:S(2)}) collective-permute-start(f32[56,128]{1,0:T(8,128)S(1)} %fusion.2), channel_id=1, source_target_pairs={{0,12},{4,0},{8,4},{12,8},{1,13},{5,1},{9,5},{13,9},{2,14},{6,2},{... | collective-permute-start | bytes 86024 | tf_op jit(solution)/shard_map/ppermute | solution.py:271
  33.2 13.8 %collective-permute-start.3 = (f32[56,128]{1,0:T(8,128)S(1)}, f32[56,128]{1,0:T(8,128)S(1)}, u32[]{:S(2)}, u32[]{:S(2)}) collective-permute-start(f32[56,128]{1,0:T(8,128)S(1)} %fusion.2), channel_id=1, source_target_pairs={{0,8},{4,12},{8,0},{12,4},{1,9},{5,13},{9,1},{13,5},{2,10},{6,14},... | collective-permute-start | bytes 86024 | tf_op jit(solution)/shard_map/ppermute | solution.py:271
  35.3 11.7 %collective-permute-start.2 = (f32[56,128]{1,0:T(8,128)S(1)}, f32[56,128]{1,0:T(8,128)S(1)}, u32[]{:S(2)}, u32[]{:S(2)}) collective-permute-start(f32[56,128]{1,0:T(8,128)S(1)} %fusion.2), channel_id=1, source_target_pairs={{0,4},{4,8},{8,12},{12,0},{1,5},{5,9},{9,13},{13,1},{2,6},{6,10},{... | collective-permute-start | bytes 86024 | tf_op jit(solution)/shard_map/ppermute | solution.py:271
  47.1 5.2 %collective-permute-start.6 = (f32[4,56,128]{2,1,0:T(8,128)S(1)}, f32[4,56,128]{2,1,0:T(8,128)S(1)}, u32[]{:S(2)}, u32[]{:S(2)}) collective-permute-start(f32[4,56,128]{2,1,0:T(8,128)S(1)} %get-tuple-element.5), channel_id=1, source_target_pairs={{0,2},{1,3},{2,0},{3,1},{4,6},{5,7},{6,4},{7,5},{8,10},{9,11},{10,... | collective-permute-start | bytes 344072 | tf_op jit(solution)/shard_map/ppermute | solution.py:271
  48.9 4.9 %collective-permute-start.5 = (f32[4,56,128]{2,1,0:T(8,128)S(1)}, f32[4,56,128]{2,1,0:T(8,128)S(1)}, u32[]{:S(2)}, u32[]{:S(2)}) collective-permute-start(f32[4,56,128]{2,1,0:T(8,128)S(1)} %get-tuple-element.5), channel_id=1, source_target_pairs={{0,1},{1,2},{2,3},{3,0},{4,5},{5,6},{6,7},{7,4},{8,9},{9,10},{10,1... | collective-permute-start | bytes 344072 | tf_op jit(solution)/shard_map/ppermute | solution.py:271
  49.6 4.1 %collective-permute-start.7 = (f32[4,56,128]{2,1,0:T(8,128)S(1)}, f32[4,56,128]{2,1,0:T(8,128)S(1)}, u32[]{:S(2)}, u32[]{:S(2)}) collective-permute-start(f32[4,56,128]{2,1,0:T(8,128)S(1)} %get-tuple-element.5), channel_id=1, source_target_pairs={{0,3},{1,0},{2,1},{3,2},{4,7},{5,4},{6,5},{7,6},{8,11},{9,8},{10,9... | collective-permute-start | bytes 344072 | tf_op jit(solution)/shard_map/ppermute | solution.py:271
  53.8 10.5 %collective-permute-start.8 = (f32[4,4,56,128]{3,2,1,0:T(8,128)S(1)}, f32[4,4,56,128]{3,2,1,0:T(8,128)S(1)}, u32[]{:S(2)}, u32[]{:S(2)}) collective-permute-start(f32[4,4,56,128]{3,2,1,0:T(8,128)S(1)} %pad_maximum_fusion.mine), channel_id=1, source_target_pairs={{0,16},{16,0},{1,17},{17,1},{2,18},{18,2},{3,19},{19,3},{4,20},{20... | collective-permute-start | bytes 1376264 | tf_op jit(solution)/shard_map/ppermute | solution.py:291
  58.9 8.2 %collective-permute-start.1 = (f32[11,2,4,8,128]{4,3,2,1,0:T(8,128)S(1)}, f32[11,2,4,8,128]{4,3,2,1,0:T(8,128)S(1)}, u32[]{:S(2)}, u32[]{:S(2)}) collective-permute-start(f32[11,2,4,8,128]{4,3,2,1,0:T(8,128)S(1)} %get-tuple-element.2), channel_id=1, source_target_pairs={{16,0},{80,16},{64,80},{128,64},{144,128},{208,144},{192,208},{48,... | collective-permute-start | bytes 1081352 | tf_op jit(solution)/shard_map/ppermute | solution.py:300
  60.8 7.7 %collective-permute-start = (f32[11,2,4,8,128]{4,3,2,1,0:T(8,128)S(1)}, f32[11,2,4,8,128]{4,3,2,1,0:T(8,128)S(1)}, u32[]{:S(2)}, u32[]{:S(2)}) collective-permute-start(f32[11,2,4,8,128]{4,3,2,1,0:T(8,128)S(1)} %get-tuple-element.3), channel_id=1, source_target_pairs={{0,16},{16,80},{80,64},{64,128},{128,144},{144,208},{208,192},{32,... | collective-permute-start | bytes 1081352 | tf_op jit(solution)/shard_map/ppermute | solution.py:299

commit v5 on v4

--- a/solution.py
+++ b/solution.py
@@ -165,20 +165,25 @@
 RATE = math.exp(math.log(ALPHA) / STEPS)
 
 
+def spread(out, value):
+    out[...] = jnp.zeros((8, 128), jnp.float32) + value
+
+
 def real_kernel(out):
-    value = 1.0 - RATE * table_of(my_freq(), math.cos) + 6.0 * MU
-    out[...] = jnp.zeros((8, 128), jnp.float32) + value
+    spread(out, 1.0 - RATE * table_of(my_freq(), math.cos) + 6.0 * MU)
 
 
 def imaginary_kernel(out):
-    value = BETA + RATE * table_of(my_freq(), math.sin)
-    out[...] = jnp.zeros((8, 128), jnp.float32) + value
-
-
-def coefficient_kernel(mine, other, real, imaginary, coef):
+    spread(out, BETA + RATE * table_of(my_freq(), math.sin))
+
+
+def start_kernel(out):
+    spread(out, (my_place() * BLOCK - HALO).astype(jnp.float32))
+
+
+def coefficient_kernel(mine, other, real, imaginary, start, coef):
     core, zh, y = lax.axis_index("core"), lax.axis_index("zh"), lax.axis_index("y")
     shift_re, d_im = real[...], imaginary[...]
-    start = my_place() * BLOCK - HALO
     offset = pl.multiple_of(my_place() % 2 * BLOCK, BLOCK)
     for j in range(4):
         for first in range(0, PADDED, ROWS):
@@ -190,66 +195,103 @@
                 a, b = mine[back_y, back_zh, at], other[back_y, back_zh, at]
                 tiles.append(jnp.where(core == j % 2, a, b))
             d_re = MU * jnp.swapaxes(jnp.stack(tiles), 0, 1) + shift_re
-            row = start + first + lax.broadcasted_iota(jnp.int32, (ROWS, 8, 128), 0)
-            inside = jnp.logical_and(row >= 0, row < 16 * ROWS)
+            step = lax.broadcasted_iota(jnp.int32, (ROWS, 8, 128), 0).astype(jnp.float32)
+            row = start[...] + (step + first)
+            inside = jnp.logical_and(row >= 0.0, row < 16.0 * ROWS)
             scale = jnp.where(inside, 1.0, 0.0) / (d_re * d_re + d_im * d_im)
             coef[first : first + ROWS, 0, j] = d_re * scale
             coef[first : first + ROWS, 1, j] = -d_im * scale
 
 
-def sweep_kernel(left, own, right, coef, out, src, u0, u1):
-    def prepare(ref, ref_row, row):
-        for j in range(4):
-            g_re, g_im = coef[row, 0, j], coef[row, 1, j]
-            re, im = ref[ref_row, 0, j], ref[ref_row, 1, j]
-            src[row, 0, j] = re
-            src[row, 1, j] = im
-            u0[row, 0, j] = g_re * re - g_im * im
-            u0[row, 1, j] = g_re * im + g_im * re
-
-    def spread(ref, first, count):
-        def step(i, carry):
-            prepare(ref, i, first + i)
-            return carry
-
-        lax.fori_loop(0, count, step, 0)
-
-    spread(left, 0, HALO)
-    spread(own, HALO, BLOCK)
-    spread(right, HALO + BLOCK, HALO)
-
+def swept(get, source, coef, row, c_row):
     lane = lax.broadcasted_iota(jnp.int32, (8, 128), 1)
     sublane = lax.broadcasted_iota(jnp.int32, (8, 128), 0)
-    first_lane, last_lane = lane == 0, lane == 127
-    first_sub, last_sub = sublane == 0, sublane == 7
     zero = jnp.zeros((8, 128), jnp.float32)
 
-    def total(old, row, c):
-        tiles = [old[row, c, j] for j in range(4)]
-        below = [jnp.where(first_sub, zero, pltpu.roll(tiles[3], 1, 0))] + tiles[:3]
-        above = tiles[1:] + [jnp.where(last_sub, zero, pltpu.roll(tiles[0], 7, 0))]
+    def total(c):
+        tiles = [get(row, c, j) for j in range(4)]
+        below = [jnp.where(sublane == 0, zero, pltpu.roll(tiles[3], 1, 0))] + tiles[:3]
+        above = tiles[1:] + [jnp.where(sublane == 7, zero, pltpu.roll(tiles[0], 7, 0))]
         sums = []
         for j in range(4):
-            sides = jnp.where(first_lane, zero, pltpu.roll(tiles[j], 1, 1))
-            sides = sides + jnp.where(last_lane, zero, pltpu.roll(tiles[j], 127, 1))
-            outer = old[row - 1, c, j] + old[row + 1, c, j]
-            sums.append(src[row, c, j] + MU * (((below[j] + above[j]) + outer) + sides))
+            sides = jnp.where(lane == 0, zero, pltpu.roll(tiles[j], 1, 1))
+            sides = sides + jnp.where(lane == 127, zero, pltpu.roll(tiles[j], 127, 1))
+            outer = get(row - 1, c, j) + get(row + 1, c, j)
+            sums.append(source(row, c, j) + MU * (((below[j] + above[j]) + outer) + sides))
         return sums
 
+    return times_coefficient(coef, c_row, total(0), total(1))
+
+
+def times_coefficient(coef, row, s_re, s_im):
+    result = []
+    for j in range(4):
+        g_re, g_im = coef[row, 0, j], coef[row, 1, j]
+        result.append((g_re * s_re[j] - g_im * s_im[j], g_re * s_im[j] + g_im * s_re[j]))
+    return result
+
+
+def put(ref, at, values):
+    for j in range(4):
+        ref[(*at, 0, j)] = values[j][0]
+        ref[(*at, 1, j)] = values[j][1]
+
+
+def first_fields(ref, rows, coef, c_first, write):
+    def step(i, carry):
+        s_re, s_im = ([ref[i, c, j] for j in range(4)] for c in range(2))
+        write(i, times_coefficient(coef, c_first + i, s_re, s_im))
+        return carry
+
+    lax.fori_loop(0, rows, step, 0)
+
+
+INNER = BLOCK // 2
+
+
+def inner_kernel(own, coef, levels):
+    first_fields(own, BLOCK, coef, HALO, lambda i, values: put(levels, (0, i), values))
+    for m in range(1, INNER):
+        for row in range(m, BLOCK - m):
+            values = swept(
+                lambda r, c, j, m=m: levels[m - 1, r, c, j],
+                lambda r, c, j: own[r, c, j],
+                coef,
+                row,
+                row + HALO,
+            )
+            put(levels, (m, row), values)
+
+
+def sweep_kernel(left, own, right, coef, levels, out, u0, u1):
+    fields = (u0, u1)
+    first_fields(left, HALO, coef, 0, lambda i, values: put(u0, (i,), values))
+    behind = HALO + BLOCK
+    first_fields(right, HALO, coef, behind, lambda i, values: put(u0, (behind + i,), values))
+
+    def inside(m, row):
+        return m < INNER and m <= row - HALO < BLOCK - m
+
+    def source(row, c, j):
+        if row < HALO:
+            return left[row, c, j]
+        return own[row - HALO, c, j] if row < behind else right[row - behind, c, j]
+
+    def getter(m):
+        def get(row, c, j):
+            return levels[m, row - HALO, c, j] if inside(m, row) else fields[m % 2][row, c, j]
+
+        return get
+
     for m in range(1, SWEEPS):
-        old, new = (u0, u1) if m % 2 else (u1, u0)
         for row in range(m, WINDOW - m):
-            s_re, s_im = total(old, row, 0), total(old, row, 1)
-            for j in range(4):
-                g_re, g_im = coef[row, 0, j], coef[row, 1, j]
-                re = g_re * s_re[j] - g_im * s_im[j]
-                im = g_re * s_im[j] + g_im * s_re[j]
-                if m < SWEEPS - 1:
-                    new[row, 0, j] = re
-                    new[row, 1, j] = im
-                else:
-                    out[row - HALO, 0, j] = re
-                    out[row - HALO, 1, j] = im
+            if inside(m, row):
+                continue
+            values = swept(getter(m - 1), source, coef, row, row)
+            if m < SWEEPS - 1:
+                put(fields[m % 2], (row,), values)
+            else:
+                put(out, (row - HALO,), values)
 
 
 def call(kernel, shape, *args, scratch=()):
@@ -289,8 +331,8 @@
     times = exchange(both, TIME)
     mine = gathered(gathered(near_reaction(reaction), "zh"), "y")
     other = lax.ppermute(mine, "core", [(0, 1), (1, 0)])
-    real, imaginary = call(real_kernel, (8, 128)), call(imaginary_kernel, (8, 128))
-    coef = call(coefficient_kernel, (PADDED, 2, 4, 8, 128), mine, other, real, imaginary)
+    shifts = [call(kernel, (8, 128)) for kernel in (real_kernel, imaginary_kernel, start_kernel)]
+    coef = call(coefficient_kernel, (PADDED, 2, 4, 8, 128), mine, other, *shifts)
     hat = call(forward_kernel, (STEPS, 2, 2, ROWS, 128), times)
     got = exchange(hat, FREQ)
     got = got.reshape(2, 2, 2, 4, 2, 2, ROWS, 128)
@@ -298,10 +340,10 @@
     ahead = [(device_of(i, zl), device_of(i + 1, zl)) for zl in range(2) for i in range(7)]
     left = lax.ppermute(own[BLOCK - HALO :], TM, ahead)
     right = lax.ppermute(own[:HALO], TM, [(b, a) for a, b in ahead])
+    levels = call(inner_kernel, (INNER, BLOCK, 2, 4, 8, 128), own, coef)
     window = pltpu.VMEM((WINDOW, 2, 4, 8, 128), jnp.float32)
-    solved = call(
-        sweep_kernel, (BLOCK, 2, 4, 8, 128), left, own, right, coef, scratch=[window] * 3
-    )
+    block = (BLOCK, 2, 4, 8, 128)
+    solved = call(sweep_kernel, block, left, own, right, coef, levels, scratch=[window] * 2)
     solved = call(rows_to_planes_kernel, (2, 2, 2, 4, 2, 2, ROWS, 128), solved)
     by_freq = exchange(solved.reshape(STEPS, 2, 2, ROWS, 128), FREQ)
     by_time = call(backward_kernel, (16, 2, 2, 2, ROWS, 128), by_freq)

time: 111 us -> 110 us (level)
  waiting for transfers between devices: 15.7 us -> 14.4 us
    ppermute x1, waiting for transfers between devices: 2.39 us -> 1.09 us  [stages(): right = lax.ppermute(own[:HALO], TM, [(b, a) for a, b in ahead])]
    pallas_call x8 -> x10, Pallas kernels: 7.14 us -> 7.63 us  [call(): pl.pallas_call(kernel, out_shape=pltpu.VMEM(shape, jnp.float32), scratch_...]
  transfers between devices with their start and end apart: 10 -> 10, of which waited for: 6 -> 6; matrix products, arithmetic and copies ran while one was open for 0% -> 0% of each run, Pallas kernels for 0% -> 2%
where the time goes in v5:
time: 110 us; the launch traced here: 109 us
  blocking collectives  51.3 us (47%)
  starting transfers between devices  32.9 us (30%)
  waiting for transfers between devices  14.4 us (13%)
  Pallas kernels  9.99 us (9%)
    all_to_all x3, blocking collectives, exchange(): return lax.all_to_all(x, axes, 0, 0, tiled=True)  51.3 us
    ppermute x6, starting transfers between devices, gathered(): lax.ppermute(x, axis, [(i, (i + d) % 4) for i in range(4)])  12.1 us
    ppermute x6, waiting for transfers between devices, gathered(): lax.ppermute(x, axis, [(i, (i + d) % 4) for i in range(4)])  11.8 us
    all_to_all x1, starting transfers between devices, exchange(): return lax.all_to_all(x, axes, 0, 0, tiled=True)  10.6 us
    pallas_call x10, Pallas kernels, call(): pl.pallas_call(kernel, out_shape=pltpu.VMEM(shape, jnp.float32), scratch_...  7.63 us
    ppermute x1, starting transfers between devices, stages(): other = lax.ppermute(mine, 'core', [(0, 1), (1, 0)])  4.91 us
    ppermute x1, starting transfers between devices, stages(): left = lax.ppermute(own[BLOCK - HALO:], TM, ahead)  3.35 us
  transfers between devices with their start and end apart: 10, of which 6 were waited for; matrix products, arithmetic and copies ran while one was open for 0% of the time, Pallas kernels for 2%

profile of v5, /device:TPU:1, one launch (start us, length us, event | category | flops | bytes accessed | tf_op | source)
XLA Modules:
  0.0 109.5 jit_solution(17432338019529906998)
XLA Ops:
  0.6 1.3 %pack_kernel.1 = f32[16,2,2,2,8,128]{5,4,3,2,1,0:T(8,128)S(1)} custom-call(f32[2,2,128,128]{3,2,1,0:T(8,128)} %state.1, f32[2,2,128,128]{3,2,1,0:T(8,128)} %adjoint.1), custom_call_target="tpu_custom_call" | custom-call | tf_op jit(solution)/shard_map/pack_kernel/pallas_call | solution.py:323
  2.0 16.2 %all_to_all.20.times = f32[16,2,2,2,8,128]{5,4,3,2,1,0:T(8,128)S(1)} all-to-all(f32[16,2,2,2,8,128]{5,4,3,2,1,0:T(8,128)S(1)} %pack_kernel.1), channel_id=1, replica_groups=mesh['x'=4,'zl'=2,'core'=2,'zh'=4,'y'=4] {'core','x','zl'}, dimensions={0} | all-to-all | bytes 1048576 | tf_op jit(solution)/shard_map/all_to_all | solution.py:318
  18.2 1.0 shard_map.50
  19.2 10.6 %all-to-all-start.1 = ((f32[32,2,2,8,128]{4,3,2,1,0:T(8,128)}), f32[32,2,2,8,128]{4,3,2,1,0:T(8,128)S(1)}, u32[]{:S(2)}, u32[]{:S(2)}) async-start(f32[32,2,2,8,128]{4,3,2,1,0:T(8,128)} %shard_map.50), calls=%async_computation.1 | async-start | bytes 1048576 | tf_op jit(solution)/shard_map/all_to_all | solution.py:318
  29.8 3.4 %collective-permute-start.4 = (f32[56,128]{1,0:T(8,128)S(1)}, f32[56,128]{1,0:T(8,128)S(1)}, u32[]{:S(2)}, u32[]{:S(2)}) collective-permute-start(f32[56,128]{1,0:T(8,128)S(1)} %fusion.2), channel_id=1, source_target_pairs={{0,12},{4,0},{8,4},{12,8},{1,13},{5,1},{9,5},{13,9},{2,14},{6,2},{... | collective-permute-start | bytes 86024 | tf_op jit(solution)/shard_map/ppermute | solution.py:313
  33.2 2.1 %collective-permute-start.3 = (f32[56,128]{1,0:T(8,128)S(1)}, f32[56,128]{1,0:T(8,128)S(1)}, u32[]{:S(2)}, u32[]{:S(2)}) collective-permute-start(f32[56,128]{1,0:T(8,128)S(1)} %fusion.2), channel_id=1, source_target_pairs={{0,8},{4,12},{8,0},{12,4},{1,9},{5,13},{9,1},{13,5},{2,10},{6,14},... | collective-permute-start | bytes 86024 | tf_op jit(solution)/shard_map/ppermute | solution.py:313
  35.3 2.1 %collective-permute-start.2 = (f32[56,128]{1,0:T(8,128)S(1)}, f32[56,128]{1,0:T(8,128)S(1)}, u32[]{:S(2)}, u32[]{:S(2)}) collective-permute-start(f32[56,128]{1,0:T(8,128)S(1)} %fusion.2), channel_id=1, source_target_pairs={{0,4},{4,8},{8,12},{12,0},{1,5},{5,9},{9,13},{13,1},{2,6},{6,10},{... | collective-permute-start | bytes 86024 | tf_op jit(solution)/shard_map/ppermute | solution.py:313
  37.4 5.4 %collective-permute-done.4 = f32[56,128]{1,0:T(8,128)S(1)} collective-permute-done((f32[56,128]{1,0:T(8,128)S(1)}, f32[56,128]{1,0:T(8,128)S(1)}, u32[]{:S(2)}, u32[]{:S(2)}) %collective-permute-start.4) | collective-permute-done | bytes 28704 | tf_op jit(solution)/shard_map/ppermute | solution.py:313
  42.9 4.2 %collective-permute-done.3 = f32[56,128]{1,0:T(8,128)S(1)} collective-permute-done((f32[56,128]{1,0:T(8,128)S(1)}, f32[56,128]{1,0:T(8,128)S(1)}, u32[]{:S(2)}, u32[]{:S(2)}) %collective-permute-start.3) | collective-permute-done | bytes 28704 | tf_op jit(solution)/shard_map/ppermute | solution.py:313
  47.1 0.0 collective-permute-done.2
  47.1 1.8 %collective-permute-start.6 = (f32[4,56,128]{2,1,0:T(8,128)S(1)}, f32[4,56,128]{2,1,0:T(8,128)S(1)}, u32[]{:S(2)}, u32[]{:S(2)}) collective-permute-start(f32[4,56,128]{2,1,0:T(8,128)S(1)} %get-tuple-element.5), channel_id=1, source_target_pairs={{0,2},{1,3},{2,0},{3,1},{4,6},{5,7},{6,4},{7,5},{8,10},{9,11},{10,... | collective-permute-start | bytes 344072 | tf_op jit(solution)/shard_map/ppermute | solution.py:313
  48.9 0.7 collective-permute-start.5
  49.7 1.9 %collective-permute-start.7 = (f32[4,56,128]{2,1,0:T(8,128)S(1)}, f32[4,56,128]{2,1,0:T(8,128)S(1)}, u32[]{:S(2)}, u32[]{:S(2)}) collective-permute-start(f32[4,56,128]{2,1,0:T(8,128)S(1)} %get-tuple-element.5), channel_id=1, source_target_pairs={{0,3},{1,0},{2,1},{3,2},{4,7},{5,4},{6,5},{7,6},{8,11},{9,8},{10,9... | collective-permute-start | bytes 344072 | tf_op jit(solution)/shard_map/ppermute | solution.py:313
  51.6 0.7 collective-permute-done.6
  52.3 1.5 %collective-permute-done.5 = f32[4,56,128]{2,1,0:T(8,128)S(1)} collective-permute-done((f32[4,56,128]{2,1,0:T(8,128)S(1)}, f32[4,56,128]{2,1,0:T(8,128)S(1)}, u32[]{:S(2)}, u32[]{:S(2)}) %collective-permute-start.5) | collective-permute-done | bytes 114720 | tf_op jit(solution)/shard_map/ppermute | solution.py:313
  53.8 4.9 %collective-permute-start.8 = (f32[4,4,56,128]{3,2,1,0:T(8,128)S(1)}, f32[4,4,56,128]{3,2,1,0:T(8,128)S(1)}, u32[]{:S(2)}, u32[]{:S(2)}) collective-permute-start(f32[4,4,56,128]{3,2,1,0:T(8,128)S(1)} %pad_maximum_fusion.mine), channel_id=1, source_target_pairs={{0,16},{16,0},{1,17},{17,1},{2,18},{18,2},{3,19},{19,3},{4,20},{20... | collective-permute-start | bytes 1376264 | tf_op jit(solution)/shard_map/ppermute | solution.py:333
  58.7 0.0 all-to-all-done.1
  58.7 0.1 shard_map.51.own
  58.8 0.1 fusion.1
  58.9 1.9 %collective-permute-start.1 = (f32[11,2,4,8,128]{4,3,2,1,0:T(8,128)S(1)}, f32[11,2,4,8,128]{4,3,2,1,0:T(8,128)S(1)}, u32[]{:S(2)}, u32[]{:S(2)}) collective-permute-start(f32[11,2,4,8,128]{4,3,2,1,0:T(8,128)S(1)} %get-tuple-element.2), channel_id=1, source_target_pairs={{16,0},{80,16},{64,80},{128,64},{144,128},{208,144},{192,208},{48,... | collective-permute-start | bytes 1081352 | tf_op jit(solution)/shard_map/ppermute | solution.py:342
  60.9 3.3 %collective-permute-start = (f32[11,2,4,8,128]{4,3,2,1,0:T(8,128)S(1)}, f32[11,2,4,8,128]{4,3,2,1,0:T(8,128)S(1)}, u32[]{:S(2)}, u32[]{:S(2)}) collective-permute-start(f32[11,2,4,8,128]{4,3,2,1,0:T(8,128)S(1)} %get-tuple-element.3), channel_id=1, source_target_pairs={{0,16},{16,80},{80,64},{64,128},{128,144},{144,208},{208,192},{32,... | collective-permute-start | bytes 1081352 | tf_op jit(solution)/shard_map/ppermute | solution.py:341
  64.3 0.0 collective-permute-done.8.other
  64.3 0.4 shard_map.55.coef
  64.8 1.2 %shard_map.56.levels = f32[8,16,2,4,8,128]{5,4,3,2,1,0:T(8,128)S(1)} custom-call(f32[16,2,4,8,128]{4,3,2,1,0:T(8,128)S(1)} %shard_map.51.own, f32[40,2,4,8,128]{4,3,2,1,0:T(8,128)S(1)} %shard_map.55.coef), custom_call_target="tpu_custom_call" | custom-call | tf_op jit(solution)/shard_map/pallas_call | solution.py:298
  66.0 1.1 collective-permute-done.1.right
  67.1 1.5 %collective-permute-done.left = f32[11,2,4,8,128]{4,3,2,1,0:T(8,128)S(1)} collective-permute-done((f32[11,2,4,8,128]{4,3,2,1,0:T(8,128)S(1)}, f32[11,2,4,8,128]{4,3,2,1,0:T(8,128)S(1)}, u32[]{:S(2)}, u32[]{:S(2)}) %collective-permute-start) | collective-permute-done | bytes 360480 | tf_op jit(solution)/shard_map/ppermute | solution.py:341
  68.6 4.5 %shard_map.57.solved = f32[16,2,4,8,128]{4,3,2,1,0:T(8,128)S(1)} custom-call(f32[11,2,4,8,128]{4,3,2,1,0:T(8,128)S(1)} %collective-permute-done.left, f32[16,2,4,8,128]{4,3,2,1,0:T(8,128)S(1)} %shard_map.51.own, f32[11,2,4,8,128]{4,3,2,1,0:T(8,128)S(1)} %collective-permute-done.1.right, f32[40,2,4,8,128]{4,3,2,1,0:T(8,128)S(1)} %shard_map.55.coef, ...), custom_call_target="tpu_custom_call" | custom-call | tf_op jit(solution)/shard_map/pallas_call | solution.py:298
  73.1 0.1 shard_map.58
  73.2 20.3 %all_to_all.21.solved = f32[32,2,2,8,128]{4,3,2,1,0:T(8,128)S(1)} all-to-all(f32[32,2,2,8,128]{4,3,2,1,0:T(8,128)S(1)} %bitcast.13), channel_id=1, replica_groups=mesh['x'=4,'zl'=2,'core'=2,'zh'=4,'y'=4] {'zl','y','zh'}, dimensions={0} | all-to-all | bytes 1048576 | tf_op jit(solution)/shard_map/all_to_all | solution.py:318
  93.4 0.2 shard_map.59
  93.6 14.8 %all_to_all.22.blocks = f32[16,2,2,2,8,128]{5,4,3,2,1,0:T(8,128)S(1)} all-to-all(f32[16,2,2,2,8,128]{5,4,3,2,1,0:T(8,128)S(1)} %shard_map.59), channel_id=1, replica_groups=mesh['x'=4,'zl'=2,'core'=2,'zh'=4,'y'=4] {'core','x','zl'}, dimensions={0} | all-to-all | bytes 1048576 | tf_op jit(solution)/shard_map/all_to_all | solution.py:318
  108.4 1.1 unpack_kernel.1
  (10 shorter events, 0.2 us)
Async XLA Ops:
  0.6 29.2 %copy-start = (f32[2,128,128]{2,1,0:T(8,128)S(1)}, f32[2,128,128]{2,1,0:T(8,128)}, u32[]{:S(2)}) copy-start(f32[2,128,128]{2,1,0:T(8,128)} %param.5) | copy-start | bytes 393220
  19.2 39.6 %all-to-all-start.1 = ((f32[32,2,2,8,128]{4,3,2,1,0:T(8,128)}), f32[32,2,2,8,128]{4,3,2,1,0:T(8,128)S(1)}, u32[]{:S(2)}, u32[]{:S(2)}) async-start(f32[32,2,2,8,128]{4,3,2,1,0:T(8,128)} %shard_map.50), calls=%async_computation.1 | async-start | bytes 1048576 | tf_op jit(solution)/shard_map/all_to_all | solution.py:318
  29.8 13.0 %collective-permute-start.4 = (f32[56,128]{1,0:T(8,128)S(1)}, f32[56,128]{1,0:T(8,128)S(1)}, u32[]{:S(2)}, u32[]{:S(2)}) collective-permute-start(f32[56,128]{1,0:T(8,128)S(1)} %fusion.2), channel_id=1, source_target_pairs={{0,12},{4,0},{8,4},{12,8},{1,13},{5,1},{9,5},{13,9},{2,14},{6,2},{... | collective-permute-start | bytes 86024 | tf_op jit(solution)/shard_map/ppermute | solution.py:313
  33.2 13.8 %collective-permute-start.3 = (f32[56,128]{1,0:T(8,128)S(1)}, f32[56,128]{1,0:T(8,128)S(1)}, u32[]{:S(2)}, u32[]{:S(2)}) collective-permute-start(f32[56,128]{1,0:T(8,128)S(1)} %fusion.2), channel_id=1, source_target_pairs={{0,8},{4,12},{8,0},{12,4},{1,9},{5,13},{9,1},{13,5},{2,10},{6,14},... | collective-permute-start | bytes 86024 | tf_op jit(solution)/shard_map/ppermute | solution.py:313
  35.3 11.7 %collective-permute-start.2 = (f32[56,128]{1,0:T(8,128)S(1)}, f32[56,128]{1,0:T(8,128)S(1)}, u32[]{:S(2)}, u32[]{:S(2)}) collective-permute-start(f32[56,128]{1,0:T(8,128)S(1)} %fusion.2), channel_id=1, source_target_pairs={{0,4},{4,8},{8,12},{12,0},{1,5},{5,9},{9,13},{13,1},{2,6},{6,10},{... | collective-permute-start | bytes 86024 | tf_op jit(solution)/shard_map/ppermute | solution.py:313
  47.1 5.2 %collective-permute-start.6 = (f32[4,56,128]{2,1,0:T(8,128)S(1)}, f32[4,56,128]{2,1,0:T(8,128)S(1)}, u32[]{:S(2)}, u32[]{:S(2)}) collective-permute-start(f32[4,56,128]{2,1,0:T(8,128)S(1)} %get-tuple-element.5), channel_id=1, source_target_pairs={{0,2},{1,3},{2,0},{3,1},{4,6},{5,7},{6,4},{7,5},{8,10},{9,11},{10,... | collective-permute-start | bytes 344072 | tf_op jit(solution)/shard_map/ppermute | solution.py:313
  48.9 4.9 %collective-permute-start.5 = (f32[4,56,128]{2,1,0:T(8,128)S(1)}, f32[4,56,128]{2,1,0:T(8,128)S(1)}, u32[]{:S(2)}, u32[]{:S(2)}) collective-permute-start(f32[4,56,128]{2,1,0:T(8,128)S(1)} %get-tuple-element.5), channel_id=1, source_target_pairs={{0,1},{1,2},{2,3},{3,0},{4,5},{5,6},{6,7},{7,4},{8,9},{9,10},{10,1... | collective-permute-start | bytes 344072 | tf_op jit(solution)/shard_map/ppermute | solution.py:313
  49.7 4.1 %collective-permute-start.7 = (f32[4,56,128]{2,1,0:T(8,128)S(1)}, f32[4,56,128]{2,1,0:T(8,128)S(1)}, u32[]{:S(2)}, u32[]{:S(2)}) collective-permute-start(f32[4,56,128]{2,1,0:T(8,128)S(1)} %get-tuple-element.5), channel_id=1, source_target_pairs={{0,3},{1,0},{2,1},{3,2},{4,7},{5,4},{6,5},{7,6},{8,11},{9,8},{10,9... | collective-permute-start | bytes 344072 | tf_op jit(solution)/shard_map/ppermute | solution.py:313
  53.8 10.5 %collective-permute-start.8 = (f32[4,4,56,128]{3,2,1,0:T(8,128)S(1)}, f32[4,4,56,128]{3,2,1,0:T(8,128)S(1)}, u32[]{:S(2)}, u32[]{:S(2)}) collective-permute-start(f32[4,4,56,128]{3,2,1,0:T(8,128)S(1)} %pad_maximum_fusion.mine), channel_id=1, source_target_pairs={{0,16},{16,0},{1,17},{17,1},{2,18},{18,2},{3,19},{19,3},{4,20},{20... | collective-permute-start | bytes 1376264 | tf_op jit(solution)/shard_map/ppermute | solution.py:333
  58.9 8.2 %collective-permute-start.1 = (f32[11,2,4,8,128]{4,3,2,1,0:T(8,128)S(1)}, f32[11,2,4,8,128]{4,3,2,1,0:T(8,128)S(1)}, u32[]{:S(2)}, u32[]{:S(2)}) collective-permute-start(f32[11,2,4,8,128]{4,3,2,1,0:T(8,128)S(1)} %get-tuple-element.2), channel_id=1, source_target_pairs={{16,0},{80,16},{64,80},{128,64},{144,128},{208,144},{192,208},{48,... | collective-permute-start | bytes 1081352 | tf_op jit(solution)/shard_map/ppermute | solution.py:342
  60.9 7.7 %collective-permute-start = (f32[11,2,4,8,128]{4,3,2,1,0:T(8,128)S(1)}, f32[11,2,4,8,128]{4,3,2,1,0:T(8,128)S(1)}, u32[]{:S(2)}, u32[]{:S(2)}) collective-permute-start(f32[11,2,4,8,128]{4,3,2,1,0:T(8,128)S(1)} %get-tuple-element.3), channel_id=1, source_target_pairs={{0,16},{16,80},{80,64},{64,128},{128,144},{144,208},{208,192},{32,... | collective-permute-start | bytes 1081352 | tf_op jit(solution)/shard_map/ppermute | solution.py:341

commit v6 on v5

--- a/solution.py
+++ b/solution.py
@@ -191,8 +191,8 @@
             tiles = []
             for slab in range(8):
                 pair = 2 * slab + j // 2
-                back_zh, back_y = (zh + 4 - pair // 4) % 4, (y + 4 - pair % 4) % 4
-                a, b = mine[back_y, back_zh, at], other[back_y, back_zh, at]
+                from_zh, from_y = lax.bitwise_xor(zh, pair // 4), lax.bitwise_xor(y, pair % 4)
+                a, b = mine[from_y, from_zh, at], other[from_y, from_zh, at]
                 tiles.append(jnp.where(core == j % 2, a, b))
             d_re = MU * jnp.swapaxes(jnp.stack(tiles), 0, 1) + shift_re
             step = lax.broadcasted_iota(jnp.int32, (ROWS, 8, 128), 0).astype(jnp.float32)
@@ -263,11 +263,25 @@
             put(levels, (m, row), values)
 
 
-def sweep_kernel(left, own, right, coef, levels, out, u0, u1):
+def sweep_kernel(link, die, own, coef, levels, out, u0, u1, left, right):
     fields = (u0, u1)
-    first_fields(left, HALO, coef, 0, lambda i, values: put(u0, (i,), values))
     behind = HALO + BLOCK
-    first_fields(right, HALO, coef, behind, lambda i, values: put(u0, (behind + i,), values))
+    odd = my_place() % 2
+
+    def side(rows, first, from_die):
+        def step(i, carry):
+            s = [
+                [jnp.where(odd == from_die, die[i, c, j], link[i, c, j]) for j in range(4)]
+                for c in range(2)
+            ]
+            put(rows, (i,), list(zip(*s)))
+            put(u0, (first + i,), times_coefficient(coef, first + i, *s))
+            return carry
+
+        lax.fori_loop(0, HALO, step, 0)
+
+    side(left, 0, 1)
+    side(right, behind, 0)
 
     def inside(m, row):
         return m < INNER and m <= row - HALO < BLOCK - m
@@ -310,12 +324,19 @@
 
 
 def gathered(x, axis):
-    others = [lax.ppermute(x, axis, [(i, (i + d) % 4) for i in range(4)]) for d in (1, 2, 3)]
+    others = [lax.ppermute(x, axis, [(i, i ^ d) for i in range(4)]) for d in (1, 2, 3)]
     return jnp.stack([x] + others)
 
 
 def exchange(x, axes):
     return lax.all_to_all(x, axes, 0, 0, tiled=True)
+
+
+def swaps(first):
+    pairs = [
+        (device_of(i, zl), device_of(i + 1, zl)) for zl in range(2) for i in range(first, 7, 2)
+    ]
+    return pairs + [(b, a) for a, b in pairs]
 
 
 def stages(state_rhs, adjoint_rhs, reaction):
@@ -337,13 +358,17 @@
     got = exchange(hat, FREQ)
     got = got.reshape(2, 2, 2, 4, 2, 2, ROWS, 128)
     own = call(planes_to_rows_kernel, (BLOCK, 2, 4, 8, 128), got)
-    ahead = [(device_of(i, zl), device_of(i + 1, zl)) for zl in range(2) for i in range(7)]
-    left = lax.ppermute(own[BLOCK - HALO :], TM, ahead)
-    right = lax.ppermute(own[:HALO], TM, [(b, a) for a, b in ahead])
+    odd = my_place() % 2
+    last = odd * (BLOCK - HALO)
+    link = lax.ppermute(lax.dynamic_slice_in_dim(own, last, HALO), TM, swaps(1))
+    other_side = lax.dynamic_slice_in_dim(own, BLOCK - HALO - last, HALO)
+    die = lax.ppermute(other_side, TM, swaps(0))
     levels = call(inner_kernel, (INNER, BLOCK, 2, 4, 8, 128), own, coef)
     window = pltpu.VMEM((WINDOW, 2, 4, 8, 128), jnp.float32)
     block = (BLOCK, 2, 4, 8, 128)
-    solved = call(sweep_kernel, block, left, own, right, coef, levels, scratch=[window] * 2)
+    edge = pltpu.VMEM((HALO, 2, 4, 8, 128), jnp.float32)
+    scratch = [window] * 2 + [edge] * 2
+    solved = call(sweep_kernel, block, link, die, own, coef, levels, scratch=scratch)
     solved = call(rows_to_planes_kernel, (2, 2, 2, 4, 2, 2, ROWS, 128), solved)
     by_freq = exchange(solved.reshape(STEPS, 2, 2, ROWS, 128), FREQ)
     by_time = call(backward_kernel, (16, 2, 2, 2, ROWS, 128), by_freq)

time: 110 us -> 108 us (0.982)
  starting transfers between devices: 32.9 us -> 25.8 us
  waiting for transfers between devices: 14.4 us -> 20.3 us
    ppermute x8, waiting for transfers between devices: 14.4 us -> 20.2 us  [the longest x6 15.8 us: gathered(): lax.ppermute(x, axis, [(i, i ^ d) for i in range(4)])]
    ppermute x8, starting transfers between devices: 17.4 us -> 11.8 us  [the longest x6 9.78 us: gathered(): lax.ppermute(x, axis, [(i, i ^ d) for i in range(4)])]
    ppermute x1, starting transfers between devices: 4.91 us -> 3.41 us  [stages(): other = lax.ppermute(mine, 'core', [(0, 1), (1, 0)])]
where the time goes in v6:
time: 108 us; the launch traced here: 107 us
  blocking collectives  50.5 us (47%)
  starting transfers between devices  25.8 us (24%)
  waiting for transfers between devices  20.3 us (19%)
  Pallas kernels  9.93 us (9%)
    all_to_all x3, blocking collectives, exchange(): return lax.all_to_all(x, axes, 0, 0, tiled=True)  50.5 us
    ppermute x6, waiting for transfers between devices, gathered(): lax.ppermute(x, axis, [(i, i ^ d) for i in range(4)])  15.8 us
    all_to_all x1, starting transfers between devices, exchange(): return lax.all_to_all(x, axes, 0, 0, tiled=True)  10.6 us
    ppermute x6, starting transfers between devices, gathered(): lax.ppermute(x, axis, [(i, i ^ d) for i in range(4)])  9.78 us
    pallas_call x10, Pallas kernels, call(): pl.pallas_call(kernel, out_shape=pltpu.VMEM(shape, jnp.float32), scratch_...  7.57 us
    ppermute x1, waiting for transfers between devices, stages(): link = lax.ppermute(lax.dynamic_slice_in_dim(own, last, HALO), TM, swaps(1))  4.45 us
    ppermute x1, starting transfers between devices, stages(): other = lax.ppermute(mine, 'core', [(0, 1), (1, 0)])  3.41 us
  transfers between devices with their start and end apart: 10, of which 6 were waited for; matrix products, arithmetic and copies ran while one was open for 0% of the time, Pallas kernels for 2%

profile of v6, /device:TPU:1, one launch (start us, length us, event | category | flops | bytes accessed | tf_op | source)
XLA Modules:
  0.0 107.4 jit_solution(3866303274717465601)
XLA Ops:
  0.6 1.3 %pack_kernel.1 = f32[16,2,2,2,8,128]{5,4,3,2,1,0:T(8,128)S(1)} custom-call(f32[2,2,128,128]{3,2,1,0:T(8,128)} %state.1, f32[2,2,128,128]{3,2,1,0:T(8,128)} %adjoint.1), custom_call_target="tpu_custom_call" | custom-call | tf_op jit(solution)/shard_map/pack_kernel/pallas_call | solution.py:344
  2.0 16.2 %all_to_all.20.times = f32[16,2,2,2,8,128]{5,4,3,2,1,0:T(8,128)S(1)} all-to-all(f32[16,2,2,2,8,128]{5,4,3,2,1,0:T(8,128)S(1)} %pack_kernel.1), channel_id=1, replica_groups=mesh['x'=4,'zl'=2,'core'=2,'zh'=4,'y'=4] {'core','x','zl'}, dimensions={0} | all-to-all | bytes 1048576 | tf_op jit(solution)/shard_map/all_to_all | solution.py:332
  18.2 1.0 shard_map.50
  19.2 10.6 %all-to-all-start.1 = ((f32[32,2,2,8,128]{4,3,2,1,0:T(8,128)}), f32[32,2,2,8,128]{4,3,2,1,0:T(8,128)S(1)}, u32[]{:S(2)}, u32[]{:S(2)}) async-start(f32[32,2,2,8,128]{4,3,2,1,0:T(8,128)} %shard_map.50), calls=%async_computation.1 | async-start | bytes 1048576 | tf_op jit(solution)/shard_map/all_to_all | solution.py:332
  29.8 3.4 %collective-permute-start.4 = (f32[56,128]{1,0:T(8,128)S(1)}, f32[56,128]{1,0:T(8,128)S(1)}, u32[]{:S(2)}, u32[]{:S(2)}) collective-permute-start(f32[56,128]{1,0:T(8,128)S(1)} %fusion.1), channel_id=1, source_target_pairs={{0,12},{4,8},{8,4},{12,0},{1,13},{5,9},{9,5},{13,1},{2,14},{6,10},... | collective-permute-start | bytes 86024 | tf_op jit(solution)/shard_map/ppermute | solution.py:327
  33.3 2.1 %collective-permute-start.3 = (f32[56,128]{1,0:T(8,128)S(1)}, f32[56,128]{1,0:T(8,128)S(1)}, u32[]{:S(2)}, u32[]{:S(2)}) collective-permute-start(f32[56,128]{1,0:T(8,128)S(1)} %fusion.1), channel_id=1, source_target_pairs={{0,8},{4,12},{8,0},{12,4},{1,9},{5,13},{9,1},{13,5},{2,10},{6,14},... | collective-permute-start | bytes 86024 | tf_op jit(solution)/shard_map/ppermute | solution.py:327
  35.3 0.2 collective-permute-start.2
  35.6 8.7 %collective-permute-done.4 = f32[56,128]{1,0:T(8,128)S(1)} collective-permute-done((f32[56,128]{1,0:T(8,128)S(1)}, f32[56,128]{1,0:T(8,128)S(1)}, u32[]{:S(2)}, u32[]{:S(2)}) %collective-permute-start.4) | collective-permute-done | bytes 28704 | tf_op jit(solution)/shard_map/ppermute | solution.py:327
  44.3 2.7 %collective-permute-done.3 = f32[56,128]{1,0:T(8,128)S(1)} collective-permute-done((f32[56,128]{1,0:T(8,128)S(1)}, f32[56,128]{1,0:T(8,128)S(1)}, u32[]{:S(2)}, u32[]{:S(2)}) %collective-permute-start.3) | collective-permute-done | bytes 28704 | tf_op jit(solution)/shard_map/ppermute | solution.py:327
  47.1 0.0 collective-permute-done.2
  47.1 1.8 %collective-permute-start.6 = (f32[4,56,128]{2,1,0:T(8,128)S(1)}, f32[4,56,128]{2,1,0:T(8,128)S(1)}, u32[]{:S(2)}, u32[]{:S(2)}) collective-permute-start(f32[4,56,128]{2,1,0:T(8,128)S(1)} %get-tuple-element.5), channel_id=1, source_target_pairs={{0,2},{1,3},{2,0},{3,1},{4,6},{5,7},{6,4},{7,5},{8,10},{9,11},{10,... | collective-permute-start | bytes 344072 | tf_op jit(solution)/shard_map/ppermute | solution.py:327
  48.9 0.7 collective-permute-start.5
  49.7 1.5 %collective-permute-start.7 = (f32[4,56,128]{2,1,0:T(8,128)S(1)}, f32[4,56,128]{2,1,0:T(8,128)S(1)}, u32[]{:S(2)}, u32[]{:S(2)}) collective-permute-start(f32[4,56,128]{2,1,0:T(8,128)S(1)} %get-tuple-element.5), channel_id=1, source_target_pairs={{0,3},{1,2},{2,1},{3,0},{4,7},{5,6},{6,5},{7,4},{8,11},{9,10},{10,... | collective-permute-start | bytes 344072 | tf_op jit(solution)/shard_map/ppermute | solution.py:327
  51.1 1.2 %collective-permute-done.6 = f32[4,56,128]{2,1,0:T(8,128)S(1)} collective-permute-done((f32[4,56,128]{2,1,0:T(8,128)S(1)}, f32[4,56,128]{2,1,0:T(8,128)S(1)}, u32[]{:S(2)}, u32[]{:S(2)}) %collective-permute-start.6) | collective-permute-done | bytes 114720 | tf_op jit(solution)/shard_map/ppermute | solution.py:327
  52.3 0.7 collective-permute-done.5
  53.1 2.4 %collective-permute-done.7 = f32[4,56,128]{2,1,0:T(8,128)S(1)} collective-permute-done((f32[4,56,128]{2,1,0:T(8,128)S(1)}, f32[4,56,128]{2,1,0:T(8,128)S(1)}, u32[]{:S(2)}, u32[]{:S(2)}) %collective-permute-start.7) | collective-permute-done | bytes 114720 | tf_op jit(solution)/shard_map/ppermute | solution.py:327
  55.5 3.4 %collective-permute-start.8 = (f32[4,4,56,128]{3,2,1,0:T(8,128)S(1)}, f32[4,4,56,128]{3,2,1,0:T(8,128)S(1)}, u32[]{:S(2)}, u32[]{:S(2)}) collective-permute-start(f32[4,4,56,128]{3,2,1,0:T(8,128)S(1)} %pad_maximum_fusion.mine), channel_id=1, source_target_pairs={{0,16},{16,0},{1,17},{17,1},{2,18},{18,2},{3,19},{19,3},{4,20},{20... | collective-permute-start | bytes 1376264 | tf_op jit(solution)/shard_map/ppermute | solution.py:354
  58.9 0.0 all-to-all-done.1
  58.9 0.1 shard_map.51.own
  59.0 0.1 constant_dynamic-slice_fusion
  59.1 0.1 collective-permute-start.1
  59.2 1.9 %collective-permute-start = (f32[11,2,4,8,128]{4,3,2,1,0:T(8,128)S(1)}, f32[11,2,4,8,128]{4,3,2,1,0:T(8,128)S(1)}, u32[]{:S(2)}, u32[]{:S(2)}) collective-permute-start(f32[11,2,4,8,128]{4,3,2,1,0:T(8,128)S(1)} %get-tuple-element.3), channel_id=1, source_target_pairs={{16,80},{64,128},{144,208},{48,112},{96,160},{176,240},{80,16},{12... | collective-permute-start | bytes 1081352 | tf_op jit(solution)/shard_map/ppermute | solution.py:363
  61.2 0.0 collective-permute-done.8.other
  61.2 0.4 shard_map.55.coef
  61.6 1.2 %shard_map.56.levels = f32[8,16,2,4,8,128]{5,4,3,2,1,0:T(8,128)S(1)} custom-call(f32[16,2,4,8,128]{4,3,2,1,0:T(8,128)S(1)} %shard_map.51.own, f32[40,2,4,8,128]{4,3,2,1,0:T(8,128)S(1)} %shard_map.55.coef), custom_call_target="tpu_custom_call" | custom-call | tf_op jit(solution)/shard_map/pallas_call | solution.py:312
  62.9 4.5 %collective-permute-done.link = f32[11,2,4,8,128]{4,3,2,1,0:T(8,128)S(1)} collective-permute-done((f32[11,2,4,8,128]{4,3,2,1,0:T(8,128)S(1)}, f32[11,2,4,8,128]{4,3,2,1,0:T(8,128)S(1)}, u32[]{:S(2)}, u32[]{:S(2)}) %collective-permute-start) | collective-permute-done | bytes 360480 | tf_op jit(solution)/shard_map/ppermute | solution.py:363
  67.3 4.5 %shard_map.57.solved = f32[16,2,4,8,128]{4,3,2,1,0:T(8,128)S(1)} custom-call(f32[11,2,4,8,128]{4,3,2,1,0:T(8,128)S(1)} %collective-permute-done.link, f32[11,2,4,8,128]{4,3,2,1,0:T(8,128)S(1)} %collective-permute-done.1.die, f32[16,2,4,8,128]{4,3,2,1,0:T(8,128)S(1)} %shard_map.51.own, f32[40,2,4,8,128]{4,3,2,1,0:T(8,128)S(1)} %shard_map.55.coef, ...), custom_call_target="tpu_custom_call" | custom-call | tf_op jit(solution)/shard_map/pallas_call | solution.py:312
  71.8 0.1 shard_map.58
  71.9 17.6 %all_to_all.21.solved = f32[32,2,2,8,128]{4,3,2,1,0:T(8,128)S(1)} all-to-all(f32[32,2,2,8,128]{4,3,2,1,0:T(8,128)S(1)} %bitcast.13), channel_id=1, replica_groups=mesh['x'=4,'zl'=2,'core'=2,'zh'=4,'y'=4] {'zl','y','zh'}, dimensions={0} | all-to-all | bytes 1048576 | tf_op jit(solution)/shard_map/all_to_all | solution.py:332
  89.5 0.2 shard_map.59
  89.7 16.7 %all_to_all.22.blocks = f32[16,2,2,2,8,128]{5,4,3,2,1,0:T(8,128)S(1)} all-to-all(f32[16,2,2,2,8,128]{5,4,3,2,1,0:T(8,128)S(1)} %shard_map.59), channel_id=1, replica_groups=mesh['x'=4,'zl'=2,'core'=2,'zh'=4,'y'=4] {'core','x','zl'}, dimensions={0} | all-to-all | bytes 1048576 | tf_op jit(solution)/shard_map/all_to_all | solution.py:332
  106.4 1.1 unpack_kernel.1
  (10 shorter events, 0.2 us)
Async XLA Ops:
  0.6 29.2 %copy-start = (f32[2,128,128]{2,1,0:T(8,128)S(1)}, f32[2,128,128]{2,1,0:T(8,128)}, u32[]{:S(2)}) copy-start(f32[2,128,128]{2,1,0:T(8,128)} %param.5) | copy-start | bytes 393220
  19.2 39.7 %all-to-all-start.1 = ((f32[32,2,2,8,128]{4,3,2,1,0:T(8,128)}), f32[32,2,2,8,128]{4,3,2,1,0:T(8,128)S(1)}, u32[]{:S(2)}, u32[]{:S(2)}) async-start(f32[32,2,2,8,128]{4,3,2,1,0:T(8,128)} %shard_map.50), calls=%async_computation.1 | async-start | bytes 1048576 | tf_op jit(solution)/shard_map/all_to_all | solution.py:332
  29.8 14.5 %collective-permute-start.4 = (f32[56,128]{1,0:T(8,128)S(1)}, f32[56,128]{1,0:T(8,128)S(1)}, u32[]{:S(2)}, u32[]{:S(2)}) collective-permute-start(f32[56,128]{1,0:T(8,128)S(1)} %fusion.1), channel_id=1, source_target_pairs={{0,12},{4,8},{8,4},{12,0},{1,13},{5,9},{9,5},{13,1},{2,14},{6,10},... | collective-permute-start | bytes 86024 | tf_op jit(solution)/shard_map/ppermute | solution.py:327
  33.3 13.8 %collective-permute-start.3 = (f32[56,128]{1,0:T(8,128)S(1)}, f32[56,128]{1,0:T(8,128)S(1)}, u32[]{:S(2)}, u32[]{:S(2)}) collective-permute-start(f32[56,128]{1,0:T(8,128)S(1)} %fusion.1), channel_id=1, source_target_pairs={{0,8},{4,12},{8,0},{12,4},{1,9},{5,13},{9,1},{13,5},{2,10},{6,14},... | collective-permute-start | bytes 86024 | tf_op jit(solution)/shard_map/ppermute | solution.py:327
  35.3 11.7 %collective-permute-start.2 = (f32[56,128]{1,0:T(8,128)S(1)}, f32[56,128]{1,0:T(8,128)S(1)}, u32[]{:S(2)}, u32[]{:S(2)}) collective-permute-start(f32[56,128]{1,0:T(8,128)S(1)} %fusion.1), channel_id=1, source_target_pairs={{0,4},{4,0},{8,12},{12,8},{1,5},{5,1},{9,13},{13,9},{2,6},{6,2},{1... | collective-permute-start | bytes 86024 | tf_op jit(solution)/shard_map/ppermute | solution.py:327
  47.1 5.2 %collective-permute-start.6 = (f32[4,56,128]{2,1,0:T(8,128)S(1)}, f32[4,56,128]{2,1,0:T(8,128)S(1)}, u32[]{:S(2)}, u32[]{:S(2)}) collective-permute-start(f32[4,56,128]{2,1,0:T(8,128)S(1)} %get-tuple-element.5), channel_id=1, source_target_pairs={{0,2},{1,3},{2,0},{3,1},{4,6},{5,7},{6,4},{7,5},{8,10},{9,11},{10,... | collective-permute-start | bytes 344072 | tf_op jit(solution)/shard_map/ppermute | solution.py:327
  48.9 4.1 %collective-permute-start.5 = (f32[4,56,128]{2,1,0:T(8,128)S(1)}, f32[4,56,128]{2,1,0:T(8,128)S(1)}, u32[]{:S(2)}, u32[]{:S(2)}) collective-permute-start(f32[4,56,128]{2,1,0:T(8,128)S(1)} %get-tuple-element.5), channel_id=1, source_target_pairs={{0,1},{1,0},{2,3},{3,2},{4,5},{5,4},{6,7},{7,6},{8,9},{9,8},{10,11... | collective-permute-start | bytes 344072 | tf_op jit(solution)/shard_map/ppermute | solution.py:327
  49.7 5.8 %collective-permute-start.7 = (f32[4,56,128]{2,1,0:T(8,128)S(1)}, f32[4,56,128]{2,1,0:T(8,128)S(1)}, u32[]{:S(2)}, u32[]{:S(2)}) collective-permute-start(f32[4,56,128]{2,1,0:T(8,128)S(1)} %get-tuple-element.5), channel_id=1, source_target_pairs={{0,3},{1,2},{2,1},{3,0},{4,7},{5,6},{6,5},{7,4},{8,11},{9,10},{10,... | collective-permute-start | bytes 344072 | tf_op jit(solution)/shard_map/ppermute | solution.py:327
  55.5 5.7 %collective-permute-start.8 = (f32[4,4,56,128]{3,2,1,0:T(8,128)S(1)}, f32[4,4,56,128]{3,2,1,0:T(8,128)S(1)}, u32[]{:S(2)}, u32[]{:S(2)}) collective-permute-start(f32[4,4,56,128]{3,2,1,0:T(8,128)S(1)} %pad_maximum_fusion.mine), channel_id=1, source_target_pairs={{0,16},{16,0},{1,17},{17,1},{2,18},{18,2},{3,19},{19,3},{4,20},{20... | collective-permute-start | bytes 1376264 | tf_op jit(solution)/shard_map/ppermute | solution.py:354
  59.1 3.8 %collective-permute-start.1 = (f32[11,2,4,8,128]{4,3,2,1,0:T(8,128)S(1)}, f32[11,2,4,8,128]{4,3,2,1,0:T(8,128)S(1)}, u32[]{:S(2)}, u32[]{:S(2)}) collective-permute-start(f32[11,2,4,8,128]{4,3,2,1,0:T(8,128)S(1)} %get-tuple-element.2), channel_id=1, source_target_pairs={{0,16},{80,64},{128,144},{208,192},{32,48},{112,96},{160,176},{240... | collective-permute-start | bytes 1081352 | tf_op jit(solution)/shard_map/ppermute | solution.py:365
  59.2 8.2 %collective-permute-start = (f32[11,2,4,8,128]{4,3,2,1,0:T(8,128)S(1)}, f32[11,2,4,8,128]{4,3,2,1,0:T(8,128)S(1)}, u32[]{:S(2)}, u32[]{:S(2)}) collective-permute-start(f32[11,2,4,8,128]{4,3,2,1,0:T(8,128)S(1)} %get-tuple-element.3), channel_id=1, source_target_pairs={{16,80},{64,128},{144,208},{48,112},{96,160},{176,240},{80,16},{12... | collective-permute-start | bytes 1081352 | tf_op jit(solution)/shard_map/ppermute | solution.py:363
